TPU v7x, 256 devices: a whole 4x4x8 slice. The times are simulated.
256 devices in a mesh: seq: 32 (over y_lo, z, core), head: 8 (over x, y_hi).
Axes of the slice: x: 4, y: 4 (y_hi: 2, y_lo: 2; y = y_hi * 2 + y_lo), z: 8, core: 2. Of those that a mesh axis runs over, the one named last changes fastest.
Arguments:
- prefix_embed: bfloat16 [256, 1024], replicated, may hold values from -6 to 6
- w_hidden: bfloat16 [1024, 8192], P(None, 'seq'), may hold values from -0.1875 to 0.1875
- b_hidden: float32 [8192], P('seq'), may hold values from -4 to 4
- w_out: bfloat16 [8192, 2, 1024], P('seq', None, 'head'), may hold values from -0.0625 to 0.0625
- queries: bfloat16 [4096, 8192], P('seq', 'head'), may hold values from -6 to 6
- keys: bfloat16 [4096, 1024], P('seq', 'head'), may hold values from -6 to 6
- values: bfloat16 [4096, 1024], P('seq', 'head'), may hold values from -6 to 6
- out_grad: bfloat16 [4096, 8192], P('seq', 'head'), may hold values from -6 to 6
Outputs:
- query_grad: bfloat16 [4096, 8192], P('seq', 'head')
- grad_w_out: float32 [8192, 2, 1024], P('seq', None, 'head')
- grad_w_hidden: float32 [1024, 8192], P(None, 'seq')
- grad_b_hidden: float32 [8192], P('seq')
- grad_prefix: float32 [256, 1024], replicated
All inputs are finite; a program needn't handle non-finite values.
Results may differ from a plain program's by a relative error of at most 0.008.
Values may be sent and summed in bfloat16 or wider, within the bound.
No kernel may reach another device: no remote copies, remote signals or barrier semaphores. Data moves between devices by JAX's collectives and lax.ppermute only.
A program may use at most 64 MiB of HBM per device.

v0:
```python
import functools
import math

import jax
import jax.numpy as jnp
from jax import lax
from jax.experimental import pallas as pl
from jax.experimental.pallas import tpu as pltpu
from jax.sharding import Mesh
from jax.sharding import PartitionSpec as P

HD = 128
SCALE = 1.0 / math.sqrt(HD)
C1 = SCALE * math.log2(math.e)
NEG = -1e30
TILE = 256
PIECES = 2
SEQ = ("y", "z", "c")
CYZ = ("c", "y", "z")
HEAD = ("x", "w")
OWNERS = ("x", "w", "y", "z")
F32 = jnp.float32
BF16 = jnp.bfloat16
SMEM = pl.BlockSpec(memory_space=pltpu.SMEM)
VMEM = pl.BlockSpec(memory_space=pltpu.VMEM)


def dot_nt(a, b):
    return lax.dot_general(a, b, (((1,), (1,)), ((), ())), preferred_element_type=F32)


def dot_nn(a, b):
    return lax.dot_general(a, b, (((1,), (0,)), ((), ())), preferred_element_type=F32)


def dot_tn(a, b):
    return lax.dot_general(a, b, (((0,), (0,)), ((), ())), preferred_element_type=F32)


def span(r):
    return slice(r * TILE, (r + 1) * TILE)


def update(state, s, d):
    m, l, t = state
    s = s.reshape(-1, 8, TILE)
    d = d.reshape(-1, 8, TILE)
    new = jnp.maximum(m, jnp.max(s, axis=0))
    fade = jnp.exp2(m - new)
    w = jnp.exp2(s - new[None])
    return (new, l * fade + jnp.sum(w, axis=0), t * fade + jnp.sum(w * d, axis=0))


def pair_of(kv, j):
    k = jnp.concatenate([kv[2 * j, :HD], kv[2 * j + 1, :HD]], 0)
    v = jnp.concatenate([kv[2 * j, HD : 2 * HD], kv[2 * j + 1, HD : 2 * HD]], 0)
    return k, v


def visible(pos, own, j, shape, key_dim):
    key = lax.broadcasted_iota(jnp.int32, shape, key_dim)
    row = lax.broadcasted_iota(jnp.int32, shape, 1 - key_dim) % HD
    if own:
        return key <= (pos[0] - 2 * j) * HD + row
    return key < (pos[0] + pos[1] - 2 * j) * HD


def sweep_step(pos, q, g, mine, other, j, states, masked=False):
    for own, kv in ((True, mine), (False, other)):
        k, v = pair_of(kv, j)
        seen = visible(pos, own, j, (2 * HD, TILE), 0) if masked else None
        new = []
        for r in range(q.shape[0] // TILE):
            s = dot_nt(k, q[span(r), :]) * C1
            if masked:
                s = jnp.where(seen, s, NEG)
            new.append(update(states[r], s, dot_nt(v, g[span(r), :])))
        states = tuple(new)
    return states


def empty_states(tiles):
    zero = jnp.zeros((8, TILE), F32)
    return tuple((jnp.full((8, TILE), NEG, F32), zero, zero) for _ in range(tiles))


def sweep_kernel(pos, q, g, mine, other, out):
    tiles = q.shape[0] // TILE
    step = functools.partial(sweep_step, pos, q, g, mine, other)
    half = pos[0] // 2
    states = step(half, lax.fori_loop(0, half, step, empty_states(tiles)), True)
    for r in range(tiles):
        for a in range(3):
            out[a, :, span(r)] = states[r][a]


def merged(m, l, t):
    top = jnp.max(m, axis=0, keepdims=True)
    fade = jnp.exp2(m - top)
    return top, jnp.sum(l * fade, axis=0, keepdims=True), jnp.sum(t * fade, axis=0, keepdims=True)


def lent_sweep_kernel(pos, q, g, mine, other, out):
    tiles = q.shape[0] // TILE
    step = functools.partial(sweep_step, pos, q, g, mine, other)
    pairs = jnp.where(pos[2] == 0, mine.shape[0] // 2, 0)
    states = lax.fori_loop(0, pairs, step, empty_states(tiles))
    for r in range(tiles):
        for a, value in enumerate(merged(*states[r])):
            out[a : a + 1, span(r)] = value


def prefix_kernel(pos, q, g, pkv, state, lent, grads, stats):
    npre = pkv.shape[1]
    kg = jnp.zeros((npre, HD), F32)
    vg = jnp.zeros((npre, HD), F32)
    late = pos[2] == 1
    for r in range(q.shape[0] // TILE):
        s = dot_nt(pkv[0], q[span(r), :]) * C1
        d = dot_nt(pkv[1], g[span(r), :])
        near = merged(*update(tuple(state[a, :, span(r)] for a in range(3)), s, d))
        far = tuple(
            jnp.where(late, lent[a : a + 1, span(r)], empty) for a, empty in enumerate((NEG, 0.0, 0.0))
        )
        top = jnp.maximum(near[0], far[0])
        near_fade = jnp.exp2(near[0] - top)
        far_fade = jnp.exp2(far[0] - top)
        total = near[1] * near_fade + far[1] * far_fade
        delta = (near[2] * near_fade + far[2] * far_fade) / total
        log_total = top + jnp.log2(total)
        stats[0:1, span(r)] = log_total
        stats[1:2, span(r)] = delta
        p = jnp.exp2(s - log_total)
        kg = kg + dot_nn((p * (d - delta)).astype(BF16), q[span(r), :])
        vg = vg + dot_nn(p.astype(BF16), g[span(r), :])
    grads[0] = (kg * SCALE).astype(grads.dtype)
    grads[1] = vg.astype(grads.dtype)


def grad_kernel(lent, piece, pos, q, g, stats, mine, other, *refs):
    *extra, out, total, log_total, delta = refs
    rows = q.shape[0]
    pairs = mine.shape[0] // 2
    first = piece * pairs

    def part(k, v, seen=None):
        for r in range(rows // TILE):
            s = dot_nt(q[span(r), :], k) * C1
            if seen is not None:
                s = jnp.where(seen, s, NEG)
            d = dot_nt(g[span(r), :], v)
            pieces = []
            for b in range(k.shape[0] // HD):
                lanes = slice(b * HD, (b + 1) * HD)
                p = jnp.exp2(s[:, lanes] - log_total[span(r), :])
                pieces.append((p * (d[:, lanes] - delta[span(r), :])).astype(BF16))
            total[span(r), :] += dot_nn(jnp.concatenate(pieces, 1), k)

    def step(i, masked=False):
        for own, kv in ((True, mine), (False, other)):
            k, v = pair_of(kv, i)
            seen = visible(pos, own, first + i, (TILE, 2 * HD), 1) if masked else None
            part(k, v, seen)

    def spread():
        columns = stats[...].T
        log_total[...] = jnp.broadcast_to(columns[:, 0:1], (rows, HD))
        delta[...] = jnp.broadcast_to(columns[:, 1:2], (rows, HD))

    if piece == 0:
        total[...] = jnp.zeros((rows, HD), F32)
    else:
        total[...] = extra[0][...]
    if lent:

        @pl.when(pos[2] == 0)
        def _():
            spread()
            lax.fori_loop(0, pairs, lambda i, _: step(i), None)

    else:
        spread()
        if piece == 0:
            part(extra[0][0], extra[0][1])
        half = pos[0] // 2
        lax.fori_loop(0, jnp.clip(half - first, 0, pairs), lambda i, _: step(i), None)

        @pl.when((half >= first) & (half < first + pairs))
        def _():
            step(half - first, True)

    if piece < PIECES - 1:
        out[...] = total[...]
    else:
        out[...] = (total[...] * SCALE).astype(out.dtype)


def sweep(pos, q, g, mine, other):
    return pl.pallas_call(
        sweep_kernel,
        out_shape=jax.ShapeDtypeStruct((3, 8, q.shape[0]), F32),
        in_specs=[SMEM] + [VMEM] * 4,
        out_specs=VMEM,
        cost_estimate=pl.CostEstimate(flops=10**9, bytes_accessed=2 * 10**6, transcendentals=2 * 10**6),
        name="sweep",
    )(pos, q, g, mine, other)


def lent_sweep(pos, q, g, mine, other):
    return pl.pallas_call(
        lent_sweep_kernel,
        out_shape=jax.ShapeDtypeStruct((3, q.shape[0]), F32),
        in_specs=[SMEM] + [VMEM] * 4,
        out_specs=VMEM,
        cost_estimate=pl.CostEstimate(flops=10**9, bytes_accessed=2 * 10**6, transcendentals=2 * 10**6),
        name="lent_sweep",
    )(pos, q, g, mine, other)


def prefix_part(pos, q, g, pkv, state, lent):
    return pl.pallas_call(
        prefix_kernel,
        out_shape=(
            jax.ShapeDtypeStruct(pkv.shape, BF16),
            jax.ShapeDtypeStruct((2, q.shape[0]), F32),
        ),
        in_specs=[SMEM] + [VMEM] * 5,
        out_specs=(VMEM, VMEM),
        cost_estimate=pl.CostEstimate(flops=3 * 10**8, bytes_accessed=10**6, transcendentals=5 * 10**5),
        name="prefix_part",
    )(pos, q, g, pkv, state, lent)


def whole(value):
    return pl.BlockSpec(value.shape, lambda *_: (0,) * value.ndim)


def query_grad_piece(lent, piece, pos, q, g, stats, mine, other, *extra):
    blocks, *shape = mine.shape
    part = pl.BlockSpec((blocks // PIECES, *shape), lambda *_: (piece, 0, 0))
    out = jax.ShapeDtypeStruct(q.shape, BF16 if lent and piece == PIECES - 1 else F32)
    return pl.pallas_call(
        functools.partial(grad_kernel, lent, piece),
        out_shape=out,
        in_specs=[SMEM, whole(q), whole(g), whole(stats), part, part] + [whole(v) for v in extra],
        out_specs=whole(out),
        grid=(1,),
        scratch_shapes=[pltpu.VMEM(q.shape, F32)] * 3,
        cost_estimate=pl.CostEstimate(flops=10**9, bytes_accessed=3 * 10**6, transcendentals=10**6),
        name="query_grad",
    )(pos, q, g, stats, mine, other, *extra)


def w_hidden_kernel(place, embed, *refs):
    *parts, grad_w, grad_b, pre = refs
    lines = len(parts)
    share = parts[0].shape[0] // 2
    for k, part in enumerate(parts):
        line = (place[0] + lines - k) % lines
        for side in range(2):
            source = 2 * line + (place[1] + side) % 2
            pre[pl.ds(pl.multiple_of(source * share, share), share), :] = part[side * share : (side + 1) * share]
    grad_w[...] = dot_tn(embed[...], pre[...])
    grad_b[...] = jnp.sum(pre[...].astype(F32), axis=0)


def w_hidden_grad(place, embed, *parts):
    npre, emb = embed.shape
    units = parts[0].shape[1]
    return pl.pallas_call(
        w_hidden_kernel,
        out_shape=(jax.ShapeDtypeStruct((emb, units), F32), jax.ShapeDtypeStruct((units,), F32)),
        in_specs=[SMEM] + [VMEM] * (1 + len(parts)),
        out_specs=(VMEM, VMEM),
        scratch_shapes=[pltpu.VMEM((npre, units), BF16)],
        cost_estimate=pl.CostEstimate(flops=2 * 10**8, bytes_accessed=2 * 10**6, transcendentals=0),
        name="w_hidden_grad",
    )(place, embed, *parts)


def exchange(value, axes):
    return lax.all_to_all(value, axes, 0, 0, tiled=True)


def to_all(value, axes):
    return exchange(jnp.broadcast_to(value, (lax.axis_size(axes), *value.shape)), axes)


def sum_parts(value, axes, dtype=BF16):
    parts = exchange(value.reshape(lax.axis_size(axes), -1, HD).astype(dtype), axes)
    return jnp.sum(parts.astype(F32), axis=0)


def shift(value, axis, steps):
    count = lax.axis_size(axis)
    return lax.ppermute(value, axis, [(i, (i + steps) % count) for i in range(count)])


def by_head(rows):
    return rows.reshape(rows.shape[0], -1, HD).transpose(1, 0, 2).reshape(-1, HD)


def on_device(prefix_embed, w_hidden, b_hidden, w_out, queries, keys, values, out_grad):
    npre, emb = prefix_embed.shape
    units = w_hidden.shape[1]
    core = lax.axis_index("c")
    late = lax.axis_index("y")
    head = lax.axis_index(HEAD)
    heads = lax.axis_size(HEAD)
    share = npre // heads
    pos = jnp.stack([lax.axis_index("z"), core, late]).astype(jnp.int32)

    hidden_pre = jnp.dot(prefix_embed, w_hidden, preferred_element_type=F32) + b_hidden
    tangent = jnp.tanh(hidden_pre)
    hidden = tangent.astype(BF16)
    partial_kv = jnp.einsum("ph,hck->cpk", hidden, w_out, preferred_element_type=F32)
    groups = lax.axis_size("z")
    kv = jnp.concatenate([keys, values], 0)
    partial_kv = partial_kv.reshape(groups, -1, HD).astype(BF16)
    mine = exchange(
        jnp.concatenate([jnp.broadcast_to(kv, (groups, *kv.shape)), partial_kv], 1), "z"
    )
    q = by_head(queries)
    g = by_head(out_grad)
    lent_q = lax.ppermute(queries, "y", [(1, 0)])
    lent_g = lax.ppermute(out_grad, "y", [(1, 0)])
    lent_q = by_head(lent_q)
    lent_g = by_head(lent_g)
    other = shift(mine, "c", 1)
    own = jnp.sum(mine[:, kv.shape[0] :].astype(F32), axis=0)
    own = own + shift(own, "c", 1)
    own = (own + shift(own, "y", 1)).astype(BF16)
    pkv = to_all(own, "z").reshape(2, npre, HD)
    lent_state = lent_sweep(pos, lent_q, lent_g, mine, other)
    lent_state = lax.ppermute(lent_state, "y", [(0, 1)])
    state = sweep(pos, q, g, mine, other)
    grads, stats = prefix_part(pos, q, g, pkv, state, lent_state)
    lent_stats = lax.ppermute(stats, "y", [(1, 0)])
    own_grads = sum_parts(grads, SEQ).astype(BF16)
    prefix_grads = to_all(own_grads, SEQ).reshape(2, npre, HD)
    lent_grad = ()
    for piece in range(PIECES):
        lent_grad = (
            query_grad_piece(True, piece, pos, lent_q, lent_g, lent_stats, mine, other, *lent_grad),
        )
    lent_grad = lax.ppermute(*lent_grad, "y", [(0, 1)])
    query_grad = pkv
    for piece in range(PIECES):
        query_grad = query_grad_piece(False, piece, pos, q, g, stats, mine, other, query_grad)
    query_grad = (query_grad + lent_grad.astype(F32)).astype(BF16)
    query_grad = query_grad.reshape(-1, queries.shape[0], HD).transpose(1, 0, 2).reshape(queries.shape)
    grad_w_out = jnp.einsum("ph,cpk->hck", hidden, prefix_grads, preferred_element_type=F32)
    hidden_part = jnp.einsum("cpk,hck->ph", prefix_grads, w_out, preferred_element_type=F32)
    parts = exchange(hidden_part.reshape(heads, share, units), HEAD)
    hidden_grad = jnp.sum(parts, axis=0)
    own_tangent = lax.dynamic_slice_in_dim(tangent, head * share, share, 0)
    pre_part = (hidden_grad * (1.0 - own_tangent * own_tangent)).astype(BF16)
    embed_part = dot_nt(pre_part, w_hidden)
    own_embed = sum_parts(embed_part, CYZ).astype(BF16)
    near = to_all(own_embed, OWNERS)
    far = shift(near, "c", 1)
    sides = jnp.stack([jnp.where(core == 0, near, far), jnp.where(core == 0, far, near)], 0)
    sides = sides.reshape(2, heads, -1, emb).transpose(1, 0, 2, 3)
    grad_prefix = sides.reshape(npre, emb).astype(F32)
    both = jnp.concatenate([pre_part, shift(pre_part, "w", 1)], 0)
    turns = [shift(both, "x", k) for k in range(1, lax.axis_size("x"))]
    place = jnp.stack([lax.axis_index("x"), lax.axis_index("w")]).astype(jnp.int32)
    grad_w_hidden, grad_b_hidden = w_hidden_grad(place, prefix_embed, both, *turns)
    return (query_grad, grad_w_out, grad_w_hidden, grad_b_hidden, grad_prefix)


def solution(mesh):
    torus = Mesh(mesh.devices.reshape(2, 8, 2, 4, 2), ("y", "z", "c", "x", "w"))
    placed = (
        P(),
        P(None, SEQ),
        P(SEQ),
        P(SEQ, None, HEAD),
        P(SEQ, HEAD),
        P(SEQ, HEAD),
        P(SEQ, HEAD),
        P(SEQ, HEAD),
    )
    return jax.shard_map(
        on_device,
        mesh=torus,
        in_specs=placed,
        out_specs=(P(SEQ, HEAD), P(SEQ, None, HEAD), P(None, SEQ), P(SEQ), P()),
        check_vma=False,
    )
```

profile of v0, /device:TPU:233, one launch (start us, length us, event | category | flops | bytes accessed | tf_op | source)
XLA Modules:
  0.0 164.8 jit_solution(4521455987584797835)
XLA Ops:
  0.7 1.0 copy-done
  1.7 1.3 fusion
  4.3 5.3 %all-to-all-start = ((bf16[8,320,128]{2,1,0:T(8,128)(2,1)}), bf16[8,320,128]{2,1,0:T(8,128)(2,1)S(1)}, u32[]{:S(2)}, u32[]{:S(2)}) async-start(bf16[8,320,128]{2,1,0:T(8,128)(2,1)} %pad_maximum_fusion), calls=%async_computation | async-start | bytes 1310720 | tf_op jit(solution)/shard_map/all_to_all | solution.py:282
  9.5 2.1 %collective-permute-start.3 = (bf16[128,1024]{1,0:T(8,128)(2,1)S(1)}, bf16[128,1024]{1,0:T(8,128)(2,1)S(1)}, u32[]{:S(2)}, u32[]{:S(2)}) collective-permute-start(bf16[128,1024]{1,0:T(8,128)(2,1)S(1)} %copy-done.3), channel_id=1, source_target_pairs={{128,0},{129,1},{130,2},{131,3},{132,4},{133,5},{134,6},{135,7},{1... | collective-permute-start | bytes 786440 | tf_op jit(solution)/shard_map/ppermute | solution.py:325
  11.6 1.3 collective-permute-start.4
  14.5 7.1 %all-to-all-done.mine = bf16[8,320,128]{2,1,0:T(8,128)(2,1)S(1)} async-done(((bf16[8,320,128]{2,1,0:T(8,128)(2,1)}), bf16[8,320,128]{2,1,0:T(8,128)(2,1)S(1)}, u32[]{:S(2)}, u32[]{:S(2)}) %all-to-all-start) | async-done | bytes 655392 | tf_op jit(solution)/shard_map/all_to_all | solution.py:282
  21.6 5.3 %collective-permute-start = (f32[64,128]{1,0:T(8,128)S(1)}, f32[64,128]{1,0:T(8,128)S(1)}, u32[]{:S(2)}, u32[]{:S(2)}) collective-permute-start(f32[64,128]{1,0:T(8,128)S(1)} %convert_reduce_fusion), channel_id=1, source_target_pairs={{0,8},{8,0},{1,9},{9,1},{2,10},{10,2},{3,11},{11,3},{4,12},{12,4},... | collective-permute-start | bytes 98312 | tf_op jit(solution)/shard_map/ppermute | solution.py:296
  28.7 1.8 %collective-permute-done.1 = f32[64,128]{1,0:T(8,128)S(1)} collective-permute-done((f32[64,128]{1,0:T(8,128)S(1)}, f32[64,128]{1,0:T(8,128)S(1)}, u32[]{:S(2)}, u32[]{:S(2)}) %collective-permute-start.1) | collective-permute-done | bytes 32800 | tf_op jit(solution)/shard_map/ppermute | solution.py:296
  31.2 7.4 %all-to-all-start.1 = ((bf16[8,64,128]{2,1,0:T(8,128)(2,1)}), bf16[8,64,128]{2,1,0:T(8,128)(2,1)S(1)}, u32[]{:S(2)}, u32[]{:S(2)}) async-start(bf16[8,64,128]{2,1,0:T(8,128)(2,1)} %broadcast_in_dim.14), calls=%async_computation.1 | async-start | bytes 262144 | tf_op jit(solution)/shard_map/all_to_all | solution.py:282
  40.2 2.1 %lent_sweep.1 = f32[3,1024]{1,0:T(4,128)} custom-call(s32[3]{0:T(128)} %pad_add_fusion.pos, bf16[1024,128]{1,0:T(8,128)(2,1)} %bitcast.89, bf16[1024,128]{1,0:T(8,128)(2,1)} %bitcast.92, bf16[8,320,128]{2,1,0:T(8,128)(2,1)} %copy-done.1, bf16[8,320,128]{2,1,0:T(8,128)(2,1)} %copy-done.9), custom_call_target="tpu_custom_call" | custom-call | flops 1000000000 | bytes 2000000 | tf_op jit(solution)/shard_map/lent_sweep/pallas_call | solution.py:210
  42.3 1.3 collective-permute-start.5
  43.5 5.5 %sweep.1.state = f32[3,8,1024]{2,1,0:T(8,128)} custom-call(s32[3]{0:T(128)} %pad_add_fusion.pos, bf16[1024,128]{1,0:T(8,128)(2,1)} %bitcast.81, bf16[1024,128]{1,0:T(8,128)(2,1)} %bitcast.85, bf16[8,320,128]{2,1,0:T(8,128)(2,1)} %copy-done.1, bf16[8,320,128]{2,1,0:T(8,128)(2,1)} %copy-done.9), custom_call_target="tpu_custom_call" | custom-call | flops 1000000000 | bytes 2000000 | tf_op jit(solution)/shard_map/sweep/pallas_call | solution.py:199
  49.7 3.3 %prefix_part.1 = (bf16[2,256,128]{2,1,0:T(8,128)(2,1)}, f32[2,1024]{1,0:T(2,128)}) custom-call(s32[3]{0:T(128)} %pad_add_fusion.pos, bf16[1024,128]{1,0:T(8,128)(2,1)} %bitcast.82, bf16[1024,128]{1,0:T(8,128)(2,1)} %bitcast.86, bf16[2,256,128]{2,1,0:T(8,128)(2,1)} %bitcast.96, f32[3,8,1024]{2,1,0:T(8,128)} %sweep.1.state, f32[3,1024]{1,0:T(4,128)} %copy-done.13), custom_call_target="tpu_custom_call" | custom-call | flops 300000000 | bytes 1000000 | tf_op jit(solution)/shard_map/prefix_part/pallas_call | solution.py:221
  53.0 17.8 %all_to_all.35 = bf16[32,16,128]{2,1,0:T(8,128)(2,1)S(1)} all-to-all(bf16[32,16,128]{2,1,0:T(8,128)(2,1)} %bitcast.98), channel_id=1, replica_groups=mesh['y'=2,'z'=8,'c'=2,'x'=4,'w'=2] {'y','z','c'}, dimensions={0} | all-to-all | bytes 262144 | tf_op jit(solution)/shard_map/all_to_all | solution.py:282
  70.9 13.3 %all_to_all.36 = bf16[32,16,128]{2,1,0:T(8,128)(2,1)S(1)} all-to-all(bf16[32,16,128]{2,1,0:T(8,128)(2,1)S(1)} %broadcast_in_dim.15), channel_id=1, replica_groups=mesh['y'=2,'z'=8,'c'=2,'x'=4,'w'=2] {'y','z','c'}, dimensions={0} | all-to-all | bytes 262144 | tf_op jit(solution)/shard_map/all_to_all | solution.py:282
  85.2 6.0 %all-to-all-start.4 = ((f32[8,32,256]{2,1,0:T(8,128)}), f32[8,32,256]{2,1,0:T(8,128)S(1)}, u32[]{:S(2)}, u32[]{:S(2)}) async-start(f32[8,32,256]{2,1,0:T(8,128)} %convolution_bitcast_fusion), calls=%async_computation.4 | async-start | bytes 524288 | tf_op jit(solution)/shard_map/all_to_all | solution.py:282
  91.2 3.7 %collective-permute-start.6 = (f32[2,1024]{1,0:T(2,128)S(1)}, f32[2,1024]{1,0:T(2,128)S(1)}, u32[]{:S(2)}, u32[]{:S(2)}) collective-permute-start(f32[2,1024]{1,0:T(2,128)S(1)} %copy-done.14), channel_id=1, source_target_pairs={{128,0},{129,1},{130,2},{131,3},{132,4},{133,5},{134,6},{135,7},{1... | collective-permute-start | bytes 24584 | tf_op jit(solution)/shard_map/ppermute | solution.py:338
  95.0 4.5 %all-to-all-done.4 = f32[8,32,256]{2,1,0:T(8,128)S(1)} async-done(((f32[8,32,256]{2,1,0:T(8,128)}), f32[8,32,256]{2,1,0:T(8,128)S(1)}, u32[]{:S(2)}, u32[]{:S(2)}) %all-to-all-start.4) | async-done | bytes 262176 | tf_op jit(solution)/shard_map/all_to_all | solution.py:282
  100.4 9.0 %all-to-all-start.5 = ((bf16[32,8,128]{2,1,0:T(8,128)(2,1)}), bf16[32,8,128]{2,1,0:T(8,128)(2,1)S(1)}, u32[]{:S(2)}, u32[]{:S(2)}) async-start(bf16[32,8,128]{2,1,0:T(8,128)(2,1)} %bitcast.48), calls=%async_computation.5 | async-start | bytes 131072 | tf_op jit(solution)/shard_map/all_to_all | solution.py:282
  110.1 2.1 %query_grad.6.refs_0_ = f32[1024,128]{1,0:T(8,128)} custom-call(s32[3]{0:T(128)} %pad_add_fusion.pos, bf16[1024,128]{1,0:T(8,128)(2,1)} %bitcast.90, bf16[1024,128]{1,0:T(8,128)(2,1)} %bitcast.93, f32[2,1024]{1,0:T(2,128)} %copy-done.15, bf16[8,320,128]{2,1,0:T(8,128)(2,1)} %copy-done.1, bf16[8,320,128]{2,1,0:T(8,128)(2,1)} %copy-done.9), custom_call_target="tpu_custom_call" | custom-call | flops 1000000000 | bytes 3000000 | tf_op jit(solution)/shard_map/query_grad/pallas_call | solution.py:242
  112.2 2.4 %query_grad.7 = bf16[1024,128]{1,0:T(8,128)(2,1)} custom-call(s32[3]{0:T(128)} %pad_add_fusion.pos, bf16[1024,128]{1,0:T(8,128)(2,1)} %bitcast.91, bf16[1024,128]{1,0:T(8,128)(2,1)} %bitcast.94, f32[2,1024]{1,0:T(2,128)} %copy-done.15, bf16[8,320,128]{2,1,0:T(8,128)(2,1)} %copy-done.1, bf16[8,320,128]{2,1,0:T(8,128)(2,1)} %copy-done.9, ...), custom_call_target="tpu_custom_call" | custom-call | flops 1000000000 | bytes 3000000 | tf_op jit(solution)/shard_map/query_grad/pallas_call | solution.py:242
  114.6 1.3 collective-permute-start.7
  116.7 17.4 %all-to-all-start.6 = ((bf16[128,8,128]{2,1,0:T(8,128)(2,1)}), bf16[128,8,128]{2,1,0:T(8,128)(2,1)S(1)}, u32[]{:S(2)}, u32[]{:S(2)}) async-start(bf16[128,8,128]{2,1,0:T(8,128)(2,1)} %broadcast_in_dim.16), calls=%async_computation.6 | async-start | bytes 524288 | tf_op jit(solution)/shard_map/all_to_all | solution.py:282
  134.7 6.8 %query_grad.4.refs_0_ = f32[1024,128]{1,0:T(8,128)} custom-call(s32[3]{0:T(128)} %pad_add_fusion.pos, bf16[1024,128]{1,0:T(8,128)(2,1)} %bitcast.83, bf16[1024,128]{1,0:T(8,128)(2,1)} %bitcast.87, f32[2,1024]{1,0:T(2,128)} %get-tuple-element.9.stats, bf16[8,320,128]{2,1,0:T(8,128)(2,1)} %copy-done.1, bf16[8,320,128]{2,1,0:T(8,128)(2,1)} %copy-done.9, ...), custom_call_target="tpu_custom_call" | custom-call | flops 1000000000 | bytes 3000000 | tf_op jit(solution)/shard_map/query_grad/pallas_call | solution.py:242
  141.5 6.4 %query_grad.5 = f32[1024,128]{1,0:T(8,128)} custom-call(s32[3]{0:T(128)} %pad_add_fusion.pos, bf16[1024,128]{1,0:T(8,128)(2,1)} %bitcast.84, bf16[1024,128]{1,0:T(8,128)(2,1)} %bitcast.88, f32[2,1024]{1,0:T(2,128)} %get-tuple-element.9.stats, bf16[8,320,128]{2,1,0:T(8,128)(2,1)} %copy-done.1, bf16[8,320,128]{2,1,0:T(8,128)(2,1)} %copy-done.9, ...), custom_call_target="tpu_custom_call" | custom-call | flops 1000000000 | bytes 3000000 | tf_op jit(solution)/shard_map/query_grad/pallas_call | solution.py:242
  147.9 1.9 %collective-permute-start.8 = (bf16[32,256]{1,0:T(8,128)(2,1)S(1)}, bf16[32,256]{1,0:T(8,128)(2,1)S(1)}, u32[]{:S(2)}, u32[]{:S(2)}) collective-permute-start(bf16[32,256]{1,0:T(8,128)(2,1)S(1)} %multiply_convert_fusion), channel_id=1, source_target_pairs={{0,1},{1,0},{2,3},{3,2},{4,5},{5,4},{6,7},{7,6},{8,9},{9,8},{10,11... | collective-permute-start | bytes 49160 | tf_op jit(solution)/shard_map/ppermute | solution.py:296
  149.8 1.1 add_convert_fusion
  151.7 1.1 collective-permute-start.12
  152.8 1.7 %collective-permute-start.9 = (bf16[64,256]{1,0:T(8,128)(2,1)S(1)}, bf16[64,256]{1,0:T(8,128)(2,1)S(1)}, u32[]{:S(2)}, u32[]{:S(2)}) collective-permute-start(bf16[64,256]{1,0:T(8,128)(2,1)S(1)} %pad_maximum_fusion.2.refs_0_), channel_id=1, source_target_pairs={{0,2},{2,4},{4,6},{6,0},{1,3},{3,5},{5,7},{7,1},{8,10},{10,12},{12... | collective-permute-start | bytes 98312 | tf_op jit(solution)/shard_map/ppermute | solution.py:296
  154.5 2.8 %collective-permute-start.10 = (bf16[64,256]{1,0:T(8,128)(2,1)S(1)}, bf16[64,256]{1,0:T(8,128)(2,1)S(1)}, u32[]{:S(2)}, u32[]{:S(2)}) collective-permute-start(bf16[64,256]{1,0:T(8,128)(2,1)S(1)} %pad_maximum_fusion.2.refs_0_), channel_id=1, source_target_pairs={{0,4},{2,6},{4,0},{6,2},{1,5},{3,7},{5,1},{7,3},{8,12},{10,14},{12... | collective-permute-start | bytes 98312 | tf_op jit(solution)/shard_map/ppermute | solution.py:296
  161.0 2.4 %w_hidden_grad.1 = (f32[1024,256]{1,0:T(8,128)}, f32[256]{0:T(256)}) custom-call(s32[2]{0:T(128)} %pad_add_fusion.1.place, bf16[256,1024]{1,0:T(8,128)(2,1)} %embed.1, bf16[64,256]{1,0:T(8,128)(2,1)} %copy-done.6, bf16[64,256]{1,0:T(8,128)(2,1)} %copy-done.10, bf16[64,256]{1,0:T(8,128)(2,1)} %copy-done.11, bf16[64,256]{1,0:T(8,128)(2,1)} %copy-done.12), custom_call_target="tpu_custom_call" | custom-call | flops 200000000 | bytes 2000000 | tf_op jit(solution)/shard_map/w_hidden_grad/pallas_call | solution.py:270
  163.7 1.0 maximum_convert_fusion
  (79 shorter events, 16.1 us)
Async XLA Ops:
  0.6 1.0 copy-start
  0.6 2.4 %copy-start.2 = (bf16[256,2,128]{2,1,0:T(2,128)(2,1)S(1)}, bf16[256,2,128]{2,1,0:T(2,128)(2,1)}, u32[]{:S(2)}) copy-start(bf16[256,2,128]{2,1,0:T(2,128)(2,1)} %param.11) | copy-start | bytes 393220
  0.7 2.6 %copy-start.7 = (bf16[128,128]{1,0:T(8,128)(2,1)S(1)}, bf16[128,128]{1,0:T(8,128)(2,1)}, u32[]{:S(2)}) copy-start(bf16[128,128]{1,0:T(8,128)(2,1)} %param.14) | copy-start | bytes 98308
  0.7 2.6 %copy-start.8 = (bf16[128,128]{1,0:T(8,128)(2,1)S(1)}, bf16[128,128]{1,0:T(8,128)(2,1)}, u32[]{:S(2)}) copy-start(bf16[128,128]{1,0:T(8,128)(2,1)} %param.13) | copy-start | bytes 98308
  3.4 6.2 %copy-start.3 = (bf16[128,1024]{1,0:T(8,128)(2,1)S(1)}, bf16[128,1024]{1,0:T(8,128)(2,1)}, u32[]{:S(2)}) copy-start(bf16[128,1024]{1,0:T(8,128)(2,1)} %param.12) | copy-start | bytes 786436
  3.4 8.3 %copy-start.4 = (bf16[128,1024]{1,0:T(8,128)(2,1)S(1)}, bf16[128,1024]{1,0:T(8,128)(2,1)}, u32[]{:S(2)}) copy-start(bf16[128,1024]{1,0:T(8,128)(2,1)} %param.15) | copy-start | bytes 786436
  4.3 17.3 %all-to-all-start = ((bf16[8,320,128]{2,1,0:T(8,128)(2,1)}), bf16[8,320,128]{2,1,0:T(8,128)(2,1)S(1)}, u32[]{:S(2)}, u32[]{:S(2)}) async-start(bf16[8,320,128]{2,1,0:T(8,128)(2,1)} %pad_maximum_fusion), calls=%async_computation | async-start | bytes 1310720 | tf_op jit(solution)/shard_map/all_to_all | solution.py:282
  9.5 18.4 %collective-permute-start.3 = (bf16[128,1024]{1,0:T(8,128)(2,1)S(1)}, bf16[128,1024]{1,0:T(8,128)(2,1)S(1)}, u32[]{:S(2)}, u32[]{:S(2)}) collective-permute-start(bf16[128,1024]{1,0:T(8,128)(2,1)S(1)} %copy-done.3), channel_id=1, source_target_pairs={{128,0},{129,1},{130,2},{131,3},{132,4},{133,5},{134,6},{135,7},{1... | collective-permute-start | bytes 786440 | tf_op jit(solution)/shard_map/ppermute | solution.py:325
  11.6 26.9 %collective-permute-start.4 = (bf16[128,1024]{1,0:T(8,128)(2,1)S(1)}, bf16[128,1024]{1,0:T(8,128)(2,1)S(1)}, u32[]{:S(2)}, u32[]{:S(2)}) collective-permute-start(bf16[128,1024]{1,0:T(8,128)(2,1)S(1)} %copy-done.4), channel_id=1, source_target_pairs={{128,0},{129,1},{130,2},{131,3},{132,4},{133,5},{134,6},{135,7},{1... | collective-permute-start | bytes 786440 | tf_op jit(solution)/shard_map/ppermute | solution.py:326
  21.5 17.8 %copy-start.1 = (bf16[8,320,128]{2,1,0:T(8,128)(2,1)}, bf16[8,320,128]{2,1,0:T(8,128)(2,1)S(1)}, u32[]{:S(2)}) copy-start(bf16[8,320,128]{2,1,0:T(8,128)(2,1)S(1)} %all-to-all-done.mine) | copy-start | bytes 1966084
  21.6 6.2 %collective-permute-start = (f32[64,128]{1,0:T(8,128)S(1)}, f32[64,128]{1,0:T(8,128)S(1)}, u32[]{:S(2)}, u32[]{:S(2)}) collective-permute-start(f32[64,128]{1,0:T(8,128)S(1)} %convert_reduce_fusion), channel_id=1, source_target_pairs={{0,8},{8,0},{1,9},{9,1},{2,10},{10,2},{3,11},{11,3},{4,12},{12,4},... | collective-permute-start | bytes 98312 | tf_op jit(solution)/shard_map/ppermute | solution.py:296
  27.5 11.8 %collective-permute-start.2 = (bf16[8,320,128]{2,1,0:T(8,128)(2,1)S(1)}, bf16[8,320,128]{2,1,0:T(8,128)(2,1)S(1)}, u32[]{:S(2)}, u32[]{:S(2)}) collective-permute-start(bf16[8,320,128]{2,1,0:T(8,128)(2,1)S(1)} %all-to-all-done.mine), channel_id=1, source_target_pairs={{0,8},{8,0},{1,9},{9,1},{2,10},{10,2},{3,11},{11,3},{4,12},{12,4},... | collective-permute-start | bytes 1966088 | tf_op jit(solution)/shard_map/ppermute | solution.py:296
  27.7 2.8 %collective-permute-start.1 = (f32[64,128]{1,0:T(8,128)S(1)}, f32[64,128]{1,0:T(8,128)S(1)}, u32[]{:S(2)}, u32[]{:S(2)}) collective-permute-start(f32[64,128]{1,0:T(8,128)S(1)} %add.25), channel_id=1, source_target_pairs={{0,128},{128,0},{1,129},{129,1},{2,130},{130,2},{3,131},{131,3},{4... | collective-permute-start | bytes 98312 | tf_op jit(solution)/shard_map/ppermute | solution.py:296
  31.2 17.9 %all-to-all-start.1 = ((bf16[8,64,128]{2,1,0:T(8,128)(2,1)}), bf16[8,64,128]{2,1,0:T(8,128)(2,1)S(1)}, u32[]{:S(2)}, u32[]{:S(2)}) async-start(bf16[8,64,128]{2,1,0:T(8,128)(2,1)} %broadcast_in_dim.14), calls=%async_computation.1 | async-start | bytes 262144 | tf_op jit(solution)/shard_map/all_to_all | solution.py:282
  39.3 0.8 copy-start.9
  42.3 6.8 %collective-permute-start.5 = (f32[3,1024]{1,0:T(4,128)}, f32[3,1024]{1,0:T(4,128)S(1)}, u32[]{:S(2)}, u32[]{:S(2)}) collective-permute-start(f32[3,1024]{1,0:T(4,128)} %lent_sweep.1), channel_id=1, source_target_pairs={{0,128},{1,129},{2,130},{3,131},{4,132},{5,133},{6,134},{7,135},{8... | collective-permute-start | bytes 36872 | tf_op jit(solution)/shard_map/ppermute | solution.py:335
  49.1 0.7 copy-start.5
  49.1 0.7 copy-start.13
  53.0 38.2 %copy-start.14 = (f32[2,1024]{1,0:T(2,128)S(1)}, f32[2,1024]{1,0:T(2,128)}, u32[]{:S(2)}) copy-start(f32[2,1024]{1,0:T(2,128)} %get-tuple-element.9.stats) | copy-start | bytes 24580
  85.2 14.3 %all-to-all-start.4 = ((f32[8,32,256]{2,1,0:T(8,128)}), f32[8,32,256]{2,1,0:T(8,128)S(1)}, u32[]{:S(2)}, u32[]{:S(2)}) async-start(f32[8,32,256]{2,1,0:T(8,128)} %convolution_bitcast_fusion), calls=%async_computation.4 | async-start | bytes 524288 | tf_op jit(solution)/shard_map/all_to_all | solution.py:282
  91.2 18.2 %collective-permute-start.6 = (f32[2,1024]{1,0:T(2,128)S(1)}, f32[2,1024]{1,0:T(2,128)S(1)}, u32[]{:S(2)}, u32[]{:S(2)}) collective-permute-start(f32[2,1024]{1,0:T(2,128)S(1)} %copy-done.14), channel_id=1, source_target_pairs={{128,0},{129,1},{130,2},{131,3},{132,4},{133,5},{134,6},{135,7},{1... | collective-permute-start | bytes 24584 | tf_op jit(solution)/shard_map/ppermute | solution.py:338
  100.4 15.5 %all-to-all-start.5 = ((bf16[32,8,128]{2,1,0:T(8,128)(2,1)}), bf16[32,8,128]{2,1,0:T(8,128)(2,1)S(1)}, u32[]{:S(2)}, u32[]{:S(2)}) async-start(bf16[32,8,128]{2,1,0:T(8,128)(2,1)} %bitcast.48), calls=%async_computation.5 | async-start | bytes 131072 | tf_op jit(solution)/shard_map/all_to_all | solution.py:282
  114.6 35.2 %collective-permute-start.7 = (bf16[1024,128]{1,0:T(8,128)(2,1)}, bf16[1024,128]{1,0:T(8,128)(2,1)S(1)}, u32[]{:S(2)}, u32[]{:S(2)}) collective-permute-start(bf16[1024,128]{1,0:T(8,128)(2,1)} %query_grad.7), channel_id=1, source_target_pairs={{0,128},{1,129},{2,130},{3,131},{4,132},{5,133},{6,134},{7,135},{8... | collective-permute-start | bytes 786440 | tf_op jit(solution)/shard_map/ppermute | solution.py:346
  116.7 35.0 %all-to-all-start.6 = ((bf16[128,8,128]{2,1,0:T(8,128)(2,1)}), bf16[128,8,128]{2,1,0:T(8,128)(2,1)S(1)}, u32[]{:S(2)}, u32[]{:S(2)}) async-start(bf16[128,8,128]{2,1,0:T(8,128)(2,1)} %broadcast_in_dim.16), calls=%async_computation.6 | async-start | bytes 524288 | tf_op jit(solution)/shard_map/all_to_all | solution.py:282
  147.9 4.9 %collective-permute-start.8 = (bf16[32,256]{1,0:T(8,128)(2,1)S(1)}, bf16[32,256]{1,0:T(8,128)(2,1)S(1)}, u32[]{:S(2)}, u32[]{:S(2)}) collective-permute-start(bf16[32,256]{1,0:T(8,128)(2,1)S(1)} %multiply_convert_fusion), channel_id=1, source_target_pairs={{0,1},{1,0},{2,3},{3,2},{4,5},{5,4},{6,7},{7,6},{8,9},{9,8},{10,11... | collective-permute-start | bytes 49160 | tf_op jit(solution)/shard_map/ppermute | solution.py:296
  151.7 11.8 %collective-permute-start.12 = (bf16[128,8,128]{2,1,0:T(8,128)(2,1)S(1)}, bf16[128,8,128]{2,1,0:T(8,128)(2,1)S(1)}, u32[]{:S(2)}, u32[]{:S(2)}) collective-permute-start(bf16[128,8,128]{2,1,0:T(8,128)(2,1)S(1)} %all-to-all-done.6), channel_id=1, source_target_pairs={{0,8},{8,0},{1,9},{9,1},{2,10},{10,2},{3,11},{11,3},{4,12},{12,4},... | collective-permute-start | bytes 786440 | tf_op jit(solution)/shard_map/ppermute | solution.py:296
  152.8 7.6 %copy-start.6 = (bf16[64,256]{1,0:T(8,128)(2,1)}, bf16[64,256]{1,0:T(8,128)(2,1)S(1)}, u32[]{:S(2)}) copy-start(bf16[64,256]{1,0:T(8,128)(2,1)S(1)} %pad_maximum_fusion.2.refs_0_) | copy-start | bytes 98308
  152.8 6.6 %collective-permute-start.9 = (bf16[64,256]{1,0:T(8,128)(2,1)S(1)}, bf16[64,256]{1,0:T(8,128)(2,1)S(1)}, u32[]{:S(2)}, u32[]{:S(2)}) collective-permute-start(bf16[64,256]{1,0:T(8,128)(2,1)S(1)} %pad_maximum_fusion.2.refs_0_), channel_id=1, source_target_pairs={{0,2},{2,4},{4,6},{6,0},{1,3},{3,5},{5,7},{7,1},{8,10},{10,12},{12... | collective-permute-start | bytes 98312 | tf_op jit(solution)/shard_map/ppermute | solution.py:296
  154.5 4.9 %collective-permute-start.10 = (bf16[64,256]{1,0:T(8,128)(2,1)S(1)}, bf16[64,256]{1,0:T(8,128)(2,1)S(1)}, u32[]{:S(2)}, u32[]{:S(2)}) collective-permute-start(bf16[64,256]{1,0:T(8,128)(2,1)S(1)} %pad_maximum_fusion.2.refs_0_), channel_id=1, source_target_pairs={{0,4},{2,6},{4,0},{6,2},{1,5},{3,7},{5,1},{7,3},{8,12},{10,14},{12... | collective-permute-start | bytes 98312 | tf_op jit(solution)/shard_map/ppermute | solution.py:296
  157.4 3.1 %collective-permute-start.11 = (bf16[64,256]{1,0:T(8,128)(2,1)S(1)}, bf16[64,256]{1,0:T(8,128)(2,1)S(1)}, u32[]{:S(2)}, u32[]{:S(2)}) collective-permute-start(bf16[64,256]{1,0:T(8,128)(2,1)S(1)} %pad_maximum_fusion.2.refs_0_), channel_id=1, source_target_pairs={{0,6},{2,0},{4,2},{6,4},{1,7},{3,1},{5,3},{7,5},{8,14},{10,8},{12,... | collective-permute-start | bytes 98312 | tf_op jit(solution)/shard_map/ppermute | solution.py:296
  159.5 1.0 copy-start.10
  159.5 1.0 copy-start.11
  (2 other events, 1.2 us)
where the time goes:
time: 168 us; the launch traced here: 165 us
  starting transfers between devices  68.8 us (41%)
  Pallas kernels  31.1 us (19%)
  blocking collectives  31.1 us (19%)
  waiting for transfers between devices  14.5 us (9%)
  local copies, waits for them, and re-layouts  10.9 us (6%)
  other arithmetic  4.51 us (3%)
  matrix products  2.93 us (2%)
    all_to_all x5, starting transfers between devices, exchange(): return lax.all_to_all(value, axes, 0, 0, tiled=True)  45.1 us
    all_to_all x2, blocking collectives, exchange(): return lax.all_to_all(value, axes, 0, 0, tiled=True)  31.1 us
    pallas_call x4, Pallas kernels, query_grad_piece(): pl.pallas_call(functools.partial(grad_kernel, lent, piece), out_shape=out...  17.7 us
    ppermute x8, starting transfers between devices, shift(): lax.ppermute(value, axis, [(i, (i + steps) % count) for i in range(count)])  14 us
    all_to_all x5, waiting for transfers between devices, exchange(): return lax.all_to_all(value, axes, 0, 0, tiled=True)  11.6 us
    pallas_call x1, Pallas kernels, sweep(): pl.pallas_call(sweep_kernel, out_shape=jax.ShapeDtypeStruct((3, 8, q.shap...  5.51 us
    unnamed x34, local copies, waits for them, and re-layouts  5.32 us
    ppermute x1, starting transfers between devices, on_device(): lent_stats = lax.ppermute(stats, 'y', [(1, 0)])  3.75 us
  transfers between devices with their start and end apart: 18, of which 5 were waited for; matrix products, arithmetic and copies ran while one was open for 6% of the time, Pallas kernels for 17%

commit v1 on v0

--- a/solution.py
+++ b/solution.py
@@ -192,7 +192,9 @@
     if piece < PIECES - 1:
         out[...] = total[...]
     else:
-        out[...] = (total[...] * SCALE).astype(out.dtype)
+        for h in range(rows // HD):
+            at = slice(h * HD, (h + 1) * HD)
+            out[:, at] = (total[at, :] * SCALE).astype(out.dtype)
 
 
 def sweep(pos, q, g, mine, other):
@@ -238,7 +240,9 @@
 def query_grad_piece(lent, piece, pos, q, g, stats, mine, other, *extra):
     blocks, *shape = mine.shape
     part = pl.BlockSpec((blocks // PIECES, *shape), lambda *_: (piece, 0, 0))
-    out = jax.ShapeDtypeStruct(q.shape, BF16 if lent and piece == PIECES - 1 else F32)
+    out = jax.ShapeDtypeStruct(q.shape, F32)
+    if piece == PIECES - 1:
+        out = jax.ShapeDtypeStruct(q.shape[::-1], BF16 if lent else F32)
     return pl.pallas_call(
         functools.partial(grad_kernel, lent, piece),
         out_shape=out,
@@ -251,31 +255,35 @@
     )(pos, q, g, stats, mine, other, *extra)
 
 
-def w_hidden_kernel(place, embed, *refs):
-    *parts, grad_w, grad_b, pre = refs
-    lines = len(parts)
-    share = parts[0].shape[0] // 2
-    for k, part in enumerate(parts):
-        line = (place[0] + lines - k) % lines
-        for side in range(2):
-            source = 2 * line + (place[1] + side) % 2
-            pre[pl.ds(pl.multiple_of(source * share, share), share), :] = part[side * share : (side + 1) * share]
-    grad_w[...] = dot_tn(embed[...], pre[...])
-    grad_b[...] = jnp.sum(pre[...].astype(F32), axis=0)
-
-
-def w_hidden_grad(place, embed, *parts):
-    npre, emb = embed.shape
-    units = parts[0].shape[1]
+def w_hidden_kernel(embed, pre, out):
+    out[...] = dot_tn(embed[...], pre[...])
+
+
+def w_hidden_grad(embed, pre):
     return pl.pallas_call(
         w_hidden_kernel,
-        out_shape=(jax.ShapeDtypeStruct((emb, units), F32), jax.ShapeDtypeStruct((units,), F32)),
-        in_specs=[SMEM] + [VMEM] * (1 + len(parts)),
-        out_specs=(VMEM, VMEM),
-        scratch_shapes=[pltpu.VMEM((npre, units), BF16)],
+        out_shape=jax.ShapeDtypeStruct((embed.shape[1], pre.shape[1]), F32),
+        in_specs=[VMEM] * 2,
+        out_specs=VMEM,
         cost_estimate=pl.CostEstimate(flops=2 * 10**8, bytes_accessed=2 * 10**6, transcendentals=0),
         name="w_hidden_grad",
-    )(place, embed, *parts)
+    )(embed, pre)
+
+
+def w_out_kernel(hidden, grads, out):
+    for c in range(grads.shape[0]):
+        out[:, c, :] = dot_tn(hidden[...], grads[c])
+
+
+def w_out_grad(hidden, grads):
+    return pl.pallas_call(
+        w_out_kernel,
+        out_shape=jax.ShapeDtypeStruct((hidden.shape[1], grads.shape[0], HD), F32),
+        in_specs=[VMEM] * 2,
+        out_specs=VMEM,
+        cost_estimate=pl.CostEstimate(flops=10**8, bytes_accessed=10**6, transcendentals=0),
+        name="w_out_grad",
+    )(hidden, grads)
 
 
 def exchange(value, axes):
@@ -348,24 +356,21 @@
     for piece in range(PIECES):
         query_grad = query_grad_piece(False, piece, pos, q, g, stats, mine, other, query_grad)
     query_grad = (query_grad + lent_grad.astype(F32)).astype(BF16)
-    query_grad = query_grad.reshape(-1, queries.shape[0], HD).transpose(1, 0, 2).reshape(queries.shape)
-    grad_w_out = jnp.einsum("ph,cpk->hck", hidden, prefix_grads, preferred_element_type=F32)
+    grad_w_out = w_out_grad(hidden, prefix_grads)
     hidden_part = jnp.einsum("cpk,hck->ph", prefix_grads, w_out, preferred_element_type=F32)
-    parts = exchange(hidden_part.reshape(heads, share, units), HEAD)
-    hidden_grad = jnp.sum(parts, axis=0)
-    own_tangent = lax.dynamic_slice_in_dim(tangent, head * share, share, 0)
-    pre_part = (hidden_grad * (1.0 - own_tangent * own_tangent)).astype(BF16)
-    embed_part = dot_nt(pre_part, w_hidden)
+    parts = to_all(hidden_part.astype(BF16), HEAD)
+    hidden_grad = jnp.sum(parts.reshape(heads, npre, units).astype(F32), axis=0)
+    pre_grad = hidden_grad * (1.0 - tangent * tangent)
+    pre_rounded = pre_grad.astype(BF16)
+    embed_part = dot_nt(lax.dynamic_slice_in_dim(pre_rounded, head * share, share, 0), w_hidden)
     own_embed = sum_parts(embed_part, CYZ).astype(BF16)
     near = to_all(own_embed, OWNERS)
     far = shift(near, "c", 1)
     sides = jnp.stack([jnp.where(core == 0, near, far), jnp.where(core == 0, far, near)], 0)
     sides = sides.reshape(2, heads, -1, emb).transpose(1, 0, 2, 3)
     grad_prefix = sides.reshape(npre, emb).astype(F32)
-    both = jnp.concatenate([pre_part, shift(pre_part, "w", 1)], 0)
-    turns = [shift(both, "x", k) for k in range(1, lax.axis_size("x"))]
-    place = jnp.stack([lax.axis_index("x"), lax.axis_index("w")]).astype(jnp.int32)
-    grad_w_hidden, grad_b_hidden = w_hidden_grad(place, prefix_embed, both, *turns)
+    grad_w_hidden = w_hidden_grad(prefix_embed, pre_rounded)
+    grad_b_hidden = jnp.sum(pre_grad, axis=0)
     return (query_grad, grad_w_out, grad_w_hidden, grad_b_hidden, grad_prefix)
 
 

time: 168 us -> 174 us (1.036)
  the two profiles are of different devices: /device:TPU:233 before, /device:TPU:199 now
where the time goes in v1:
time: 174 us
  Pallas kernels  44.6 us (26%)
  blocking collectives  41.2 us (24%)
  starting transfers between devices  40 us (23%)
  waiting for transfers between devices  30.6 us (18%)
  local copies, waits for them, and re-layouts  8.98 us (5%)
  other arithmetic  5.24 us (3%)
  matrix products  1.99 us (1%)
    all_to_all x3, blocking collectives, exchange(): return lax.all_to_all(value, axes, 0, 0, tiled=True)  41.2 us
    all_to_all x4, starting transfers between devices, exchange(): return lax.all_to_all(value, axes, 0, 0, tiled=True)  29.3 us
    all_to_all x4, waiting for transfers between devices, exchange(): return lax.all_to_all(value, axes, 0, 0, tiled=True)  26.2 us
    pallas_call x4, Pallas kernels, query_grad_piece(): pl.pallas_call(functools.partial(grad_kernel, lent, piece), out_shape=out...  25.9 us
    pallas_call x1, Pallas kernels, sweep(): pl.pallas_call(sweep_kernel, out_shape=jax.ShapeDtypeStruct((3, 8, q.shap...  5.52 us
    pallas_call x1, Pallas kernels, lent_sweep(): pl.pallas_call(lent_sweep_kernel, out_shape=jax.ShapeDtypeStruct((3, q.sh...  5.46 us
    ppermute x4, starting transfers between devices, shift(): lax.ppermute(value, axis, [(i, (i + steps) % count) for i in range(count)])  4.29 us
  transfers between devices with their start and end apart: 13, of which 5 were waited for; matrix products, arithmetic and copies ran while one was open for 4% of the time, Pallas kernels for 24%

profile of v1, /device:TPU:199, one launch (start us, length us, event | category | flops | bytes accessed | tf_op | source)
XLA Modules:
  0.0 173.5 jit_solution(1308057469111116876)
XLA Ops:
  0.7 1.0 copy-done
  1.7 1.4 fusion.10
  4.3 5.7 %all-to-all-start = ((bf16[8,320,128]{2,1,0:T(8,128)(2,1)}), bf16[8,320,128]{2,1,0:T(8,128)(2,1)S(1)}, u32[]{:S(2)}, u32[]{:S(2)}) async-start(bf16[8,320,128]{2,1,0:T(8,128)(2,1)} %pad_maximum_fusion), calls=%async_computation | async-start | bytes 1310720 | tf_op jit(solution)/shard_map/all_to_all | solution.py:290
  10.0 1.3 collective-permute-start.3
  11.3 1.3 collective-permute-start.4
  14.1 12.7 %all-to-all-done.mine = bf16[8,320,128]{2,1,0:T(8,128)(2,1)S(1)} async-done(((bf16[8,320,128]{2,1,0:T(8,128)(2,1)}), bf16[8,320,128]{2,1,0:T(8,128)(2,1)S(1)}, u32[]{:S(2)}, u32[]{:S(2)}) %all-to-all-start) | async-done | bytes 655392 | tf_op jit(solution)/shard_map/all_to_all | solution.py:290
  26.8 1.1 collective-permute-start
  28.8 1.3 collective-permute-start.1
  32.2 6.8 %all-to-all-start.1 = ((bf16[8,64,128]{2,1,0:T(8,128)(2,1)}), bf16[8,64,128]{2,1,0:T(8,128)(2,1)S(1)}, u32[]{:S(2)}, u32[]{:S(2)}) async-start(bf16[8,64,128]{2,1,0:T(8,128)(2,1)} %broadcast_in_dim.17), calls=%async_computation.1 | async-start | bytes 262144 | tf_op jit(solution)/shard_map/all_to_all | solution.py:290
  40.6 5.5 %lent_sweep.1 = f32[3,1024]{1,0:T(4,128)} custom-call(s32[3]{0:T(128)} %pad_add_fusion.pos, bf16[1024,128]{1,0:T(8,128)(2,1)} %bitcast.70, bf16[1024,128]{1,0:T(8,128)(2,1)} %bitcast.73, bf16[8,320,128]{2,1,0:T(8,128)(2,1)} %copy-done.3, bf16[8,320,128]{2,1,0:T(8,128)(2,1)} %copy-done.11), custom_call_target="tpu_custom_call" | custom-call | flops 1000000000 | bytes 2000000 | tf_op jit(solution)/shard_map/lent_sweep/pallas_call | solution.py:212
  46.1 1.3 collective-permute-start.5
  47.4 5.5 %sweep.1.state = f32[3,8,1024]{2,1,0:T(8,128)} custom-call(s32[3]{0:T(128)} %pad_add_fusion.pos, bf16[1024,128]{1,0:T(8,128)(2,1)} %bitcast.62, bf16[1024,128]{1,0:T(8,128)(2,1)} %bitcast.66, bf16[8,320,128]{2,1,0:T(8,128)(2,1)} %copy-done.3, bf16[8,320,128]{2,1,0:T(8,128)(2,1)} %copy-done.11), custom_call_target="tpu_custom_call" | custom-call | flops 1000000000 | bytes 2000000 | tf_op jit(solution)/shard_map/sweep/pallas_call | solution.py:201
  53.6 3.3 %prefix_part.1 = (bf16[2,256,128]{2,1,0:T(8,128)(2,1)}, f32[2,1024]{1,0:T(2,128)}) custom-call(s32[3]{0:T(128)} %pad_add_fusion.pos, bf16[1024,128]{1,0:T(8,128)(2,1)} %bitcast.63, bf16[1024,128]{1,0:T(8,128)(2,1)} %bitcast.67, bf16[2,256,128]{2,1,0:T(8,128)(2,1)} %bitcast.77, f32[3,8,1024]{2,1,0:T(8,128)} %sweep.1.state, f32[3,1024]{1,0:T(4,128)} %copy-done.12), custom_call_target="tpu_custom_call" | custom-call | flops 300000000 | bytes 1000000 | tf_op jit(solution)/shard_map/prefix_part/pallas_call | solution.py:223
  56.9 14.7 %all_to_all.35 = bf16[32,16,128]{2,1,0:T(8,128)(2,1)S(1)} all-to-all(bf16[32,16,128]{2,1,0:T(8,128)(2,1)} %bitcast.79), channel_id=1, replica_groups=mesh['y'=2,'z'=8,'c'=2,'x'=4,'w'=2] {'y','z','c'}, dimensions={0} | all-to-all | bytes 262144 | tf_op jit(solution)/shard_map/all_to_all | solution.py:290
  71.7 13.4 %all_to_all.36 = bf16[32,16,128]{2,1,0:T(8,128)(2,1)S(1)} all-to-all(bf16[32,16,128]{2,1,0:T(8,128)(2,1)S(1)} %broadcast_in_dim.18), channel_id=1, replica_groups=mesh['y'=2,'z'=8,'c'=2,'x'=4,'w'=2] {'y','z','c'}, dimensions={0} | all-to-all | bytes 262144 | tf_op jit(solution)/shard_map/all_to_all | solution.py:290
  85.3 1.0 broadcast_in_dim.19
  86.3 6.9 %all-to-all-start.4 = ((bf16[8,256,256]{2,1,0:T(8,128)(2,1)}), bf16[8,256,256]{2,1,0:T(8,128)(2,1)S(1)}, u32[]{:S(2)}, u32[]{:S(2)}) async-start(bf16[8,256,256]{2,1,0:T(8,128)(2,1)} %broadcast_in_dim.19), calls=%async_computation.4 | async-start | bytes 2097152 | tf_op jit(solution)/shard_map/all_to_all | solution.py:290
  93.2 13.5 %all-to-all-done.4 = bf16[8,256,256]{2,1,0:T(8,128)(2,1)S(1)} async-done(((bf16[8,256,256]{2,1,0:T(8,128)(2,1)}), bf16[8,256,256]{2,1,0:T(8,128)(2,1)S(1)}, u32[]{:S(2)}, u32[]{:S(2)}) %all-to-all-start.4) | async-done | bytes 1048608 | tf_op jit(solution)/shard_map/all_to_all | solution.py:290
  107.7 13.0 %all_to_all.37 = bf16[32,8,128]{2,1,0:T(8,128)(2,1)S(1)} all-to-all(bf16[32,8,128]{2,1,0:T(8,128)(2,1)S(1)} %bitcast.76), channel_id=1, replica_groups=mesh['y'=2,'z'=8,'c'=2,'x'=4,'w'=2] {'c','y','z'}, dimensions={0} | all-to-all | bytes 131072 | tf_op jit(solution)/shard_map/all_to_all | solution.py:290
  121.5 9.9 %all-to-all-start.6 = ((bf16[128,8,128]{2,1,0:T(8,128)(2,1)}), bf16[128,8,128]{2,1,0:T(8,128)(2,1)S(1)}, u32[]{:S(2)}, u32[]{:S(2)}) async-start(bf16[128,8,128]{2,1,0:T(8,128)(2,1)} %broadcast_in_dim.20), calls=%async_computation.6 | async-start | bytes 524288 | tf_op jit(solution)/shard_map/all_to_all | solution.py:290
  131.5 1.3 collective-permute-start.6
  132.8 3.5 %collective-permute-done.6.stats = f32[2,1024]{1,0:T(2,128)S(1)} collective-permute-done((f32[2,1024]{1,0:T(2,128)S(1)}, f32[2,1024]{1,0:T(2,128)S(1)}, u32[]{:S(2)}, u32[]{:S(2)}) %collective-permute-start.6) | collective-permute-done | bytes 8224 | tf_op jit(solution)/shard_map/ppermute | solution.py:346
  136.8 6.4 %query_grad.6.refs_0_ = f32[1024,128]{1,0:T(8,128)} custom-call(s32[3]{0:T(128)} %pad_add_fusion.pos, bf16[1024,128]{1,0:T(8,128)(2,1)} %bitcast.71, bf16[1024,128]{1,0:T(8,128)(2,1)} %bitcast.74, f32[2,1024]{1,0:T(2,128)} %copy-done.14, bf16[8,320,128]{2,1,0:T(8,128)(2,1)} %copy-done.3, bf16[8,320,128]{2,1,0:T(8,128)(2,1)} %copy-done.11), custom_call_target="tpu_custom_call" | custom-call | flops 1000000000 | bytes 3000000 | tf_op jit(solution)/shard_map/query_grad/pallas_call | solution.py:246
  143.2 6.3 %query_grad.7 = bf16[128,1024]{1,0:T(8,128)(2,1)} custom-call(s32[3]{0:T(128)} %pad_add_fusion.pos, bf16[1024,128]{1,0:T(8,128)(2,1)} %bitcast.72, bf16[1024,128]{1,0:T(8,128)(2,1)} %bitcast.75, f32[2,1024]{1,0:T(2,128)} %copy-done.14, bf16[8,320,128]{2,1,0:T(8,128)(2,1)} %copy-done.3, bf16[8,320,128]{2,1,0:T(8,128)(2,1)} %copy-done.11, ...), custom_call_target="tpu_custom_call" | custom-call | flops 1000000000 | bytes 3000000 | tf_op jit(solution)/shard_map/query_grad/pallas_call | solution.py:246
  149.6 1.3 collective-permute-start.7
  150.9 6.8 %query_grad.4.refs_0_ = f32[1024,128]{1,0:T(8,128)} custom-call(s32[3]{0:T(128)} %pad_add_fusion.pos, bf16[1024,128]{1,0:T(8,128)(2,1)} %bitcast.64, bf16[1024,128]{1,0:T(8,128)(2,1)} %bitcast.68, f32[2,1024]{1,0:T(2,128)} %get-tuple-element.7.stats, bf16[8,320,128]{2,1,0:T(8,128)(2,1)} %copy-done.3, bf16[8,320,128]{2,1,0:T(8,128)(2,1)} %copy-done.11, ...), custom_call_target="tpu_custom_call" | custom-call | flops 1000000000 | bytes 3000000 | tf_op jit(solution)/shard_map/query_grad/pallas_call | solution.py:246
  157.7 6.4 %query_grad.5 = f32[128,1024]{1,0:T(8,128)} custom-call(s32[3]{0:T(128)} %pad_add_fusion.pos, bf16[1024,128]{1,0:T(8,128)(2,1)} %bitcast.65, bf16[1024,128]{1,0:T(8,128)(2,1)} %bitcast.69, f32[2,1024]{1,0:T(2,128)} %get-tuple-element.7.stats, bf16[8,320,128]{2,1,0:T(8,128)(2,1)} %copy-done.3, bf16[8,320,128]{2,1,0:T(8,128)(2,1)} %copy-done.11, ...), custom_call_target="tpu_custom_call" | custom-call | flops 1000000000 | bytes 3000000 | tf_op jit(solution)/shard_map/query_grad/pallas_call | solution.py:246
  164.1 1.9 %collective-permute-start.8 = (bf16[128,8,128]{2,1,0:T(8,128)(2,1)S(1)}, bf16[128,8,128]{2,1,0:T(8,128)(2,1)S(1)}, u32[]{:S(2)}, u32[]{:S(2)}) collective-permute-start(bf16[128,8,128]{2,1,0:T(8,128)(2,1)S(1)} %all-to-all-done.6), channel_id=1, source_target_pairs={{0,8},{8,0},{1,9},{9,1},{2,10},{10,2},{3,11},{11,3},{4,12},{12,4},... | collective-permute-start | bytes 786440 | tf_op jit(solution)/shard_map/ppermute | solution.py:304
  166.0 1.8 %add_convert_fusion = bf16[128,1024]{1,0:T(8,128)(2,1)} fusion(f32[128,1024]{1,0:T(8,128)} %query_grad.5, bf16[128,1024]{1,0:T(8,128)(2,1)S(1)} %collective-permute-done.7), kind=kLoop, calls=%fused_computation.10 | loop fusion | flops 393216 | bytes 1048576 | tf_op jit(solution)/shard_map/convert_element_type | solution.py:358
  167.8 2.0 %w_out_grad.1 = f32[256,2,128]{2,1,0:T(2,128)} custom-call(bf16[256,256]{1,0:T(8,128)(2,1)} %copy-done.1, bf16[2,256,128]{2,1,0:T(8,128)(2,1)} %bitcast.59), custom_call_target="tpu_custom_call" | custom-call | flops 100000000 | bytes 1000000 | tf_op jit(solution)/shard_map/w_out_grad/pallas_call | solution.py:279
  169.8 2.4 %w_hidden_grad.1 = f32[1024,256]{1,0:T(8,128)} custom-call(bf16[256,1024]{1,0:T(8,128)(2,1)} %embed.1, bf16[256,256]{1,0:T(8,128)(2,1)} %copy-done.4), custom_call_target="tpu_custom_call" | custom-call | flops 200000000 | bytes 2000000 | tf_op jit(solution)/shard_map/w_hidden_grad/pallas_call | solution.py:263
  172.5 1.0 maximum_convert_fusion
  (65 shorter events, 11.0 us)
Async XLA Ops:
  0.6 1.0 copy-start
  0.6 2.4 %copy-start.5 = (bf16[256,2,128]{2,1,0:T(2,128)(2,1)S(1)}, bf16[256,2,128]{2,1,0:T(2,128)(2,1)}, u32[]{:S(2)}) copy-start(bf16[256,2,128]{2,1,0:T(2,128)(2,1)} %param.11) | copy-start | bytes 393220
  0.7 2.6 %copy-start.9 = (bf16[128,128]{1,0:T(8,128)(2,1)S(1)}, bf16[128,128]{1,0:T(8,128)(2,1)}, u32[]{:S(2)}) copy-start(bf16[128,128]{1,0:T(8,128)(2,1)} %param.14) | copy-start | bytes 98308
  0.7 2.6 %copy-start.10 = (bf16[128,128]{1,0:T(8,128)(2,1)S(1)}, bf16[128,128]{1,0:T(8,128)(2,1)}, u32[]{:S(2)}) copy-start(bf16[128,128]{1,0:T(8,128)(2,1)} %param.13) | copy-start | bytes 98308
  3.0 1.2 copy-start.1
  3.4 6.6 %copy-start.6 = (bf16[128,1024]{1,0:T(8,128)(2,1)S(1)}, bf16[128,1024]{1,0:T(8,128)(2,1)}, u32[]{:S(2)}) copy-start(bf16[128,1024]{1,0:T(8,128)(2,1)} %param.12) | copy-start | bytes 786436
  3.4 7.9 %copy-start.7 = (bf16[128,1024]{1,0:T(8,128)(2,1)S(1)}, bf16[128,1024]{1,0:T(8,128)(2,1)}, u32[]{:S(2)}) copy-start(bf16[128,1024]{1,0:T(8,128)(2,1)} %param.15) | copy-start | bytes 786436
  4.3 22.5 %all-to-all-start = ((bf16[8,320,128]{2,1,0:T(8,128)(2,1)}), bf16[8,320,128]{2,1,0:T(8,128)(2,1)S(1)}, u32[]{:S(2)}, u32[]{:S(2)}) async-start(bf16[8,320,128]{2,1,0:T(8,128)(2,1)} %pad_maximum_fusion), calls=%async_computation | async-start | bytes 1310720 | tf_op jit(solution)/shard_map/all_to_all | solution.py:290
  10.0 20.1 %collective-permute-start.3 = (bf16[128,1024]{1,0:T(8,128)(2,1)S(1)}, bf16[128,1024]{1,0:T(8,128)(2,1)S(1)}, u32[]{:S(2)}, u32[]{:S(2)}) collective-permute-start(bf16[128,1024]{1,0:T(8,128)(2,1)S(1)} %copy-done.6), channel_id=1, source_target_pairs={{128,0},{129,1},{130,2},{131,3},{132,4},{133,5},{134,6},{135,7},{1... | collective-permute-start | bytes 786440 | tf_op jit(solution)/shard_map/ppermute | solution.py:333
  11.3 27.7 %collective-permute-start.4 = (bf16[128,1024]{1,0:T(8,128)(2,1)S(1)}, bf16[128,1024]{1,0:T(8,128)(2,1)S(1)}, u32[]{:S(2)}, u32[]{:S(2)}) collective-permute-start(bf16[128,1024]{1,0:T(8,128)(2,1)S(1)} %copy-done.7), channel_id=1, source_target_pairs={{128,0},{129,1},{130,2},{131,3},{132,4},{133,5},{134,6},{135,7},{1... | collective-permute-start | bytes 786440 | tf_op jit(solution)/shard_map/ppermute | solution.py:334
  26.8 13.0 %copy-start.3 = (bf16[8,320,128]{2,1,0:T(8,128)(2,1)}, bf16[8,320,128]{2,1,0:T(8,128)(2,1)S(1)}, u32[]{:S(2)}) copy-start(bf16[8,320,128]{2,1,0:T(8,128)(2,1)S(1)} %all-to-all-done.mine) | copy-start | bytes 1966084
  26.8 1.9 %collective-permute-start = (f32[64,128]{1,0:T(8,128)S(1)}, f32[64,128]{1,0:T(8,128)S(1)}, u32[]{:S(2)}, u32[]{:S(2)}) collective-permute-start(f32[64,128]{1,0:T(8,128)S(1)} %convert_reduce_fusion.1), channel_id=1, source_target_pairs={{0,8},{8,0},{1,9},{9,1},{2,10},{10,2},{3,11},{11,3},{4,12},{12,4},... | collective-permute-start | bytes 98312 | tf_op jit(solution)/shard_map/ppermute | solution.py:304
  28.5 11.3 %collective-permute-start.2 = (bf16[8,320,128]{2,1,0:T(8,128)(2,1)S(1)}, bf16[8,320,128]{2,1,0:T(8,128)(2,1)S(1)}, u32[]{:S(2)}, u32[]{:S(2)}) collective-permute-start(bf16[8,320,128]{2,1,0:T(8,128)(2,1)S(1)} %all-to-all-done.mine), channel_id=1, source_target_pairs={{0,8},{8,0},{1,9},{9,1},{2,10},{10,2},{3,11},{11,3},{4,12},{12,4},... | collective-permute-start | bytes 1966088 | tf_op jit(solution)/shard_map/ppermute | solution.py:304
  28.8 2.8 %collective-permute-start.1 = (f32[64,128]{1,0:T(8,128)S(1)}, f32[64,128]{1,0:T(8,128)S(1)}, u32[]{:S(2)}, u32[]{:S(2)}) collective-permute-start(f32[64,128]{1,0:T(8,128)S(1)} %add.25), channel_id=1, source_target_pairs={{0,128},{128,0},{1,129},{129,1},{2,130},{130,2},{3,131},{131,3},{4... | collective-permute-start | bytes 98312 | tf_op jit(solution)/shard_map/ppermute | solution.py:304
  32.2 20.7 %all-to-all-start.1 = ((bf16[8,64,128]{2,1,0:T(8,128)(2,1)}), bf16[8,64,128]{2,1,0:T(8,128)(2,1)S(1)}, u32[]{:S(2)}, u32[]{:S(2)}) async-start(bf16[8,64,128]{2,1,0:T(8,128)(2,1)} %broadcast_in_dim.17), calls=%async_computation.1 | async-start | bytes 262144 | tf_op jit(solution)/shard_map/all_to_all | solution.py:290
  39.8 0.9 copy-start.11
  46.1 6.8 %collective-permute-start.5 = (f32[3,1024]{1,0:T(4,128)}, f32[3,1024]{1,0:T(4,128)S(1)}, u32[]{:S(2)}, u32[]{:S(2)}) collective-permute-start(f32[3,1024]{1,0:T(4,128)} %lent_sweep.1), channel_id=1, source_target_pairs={{0,128},{1,129},{2,130},{3,131},{4,132},{5,133},{6,134},{7,135},{8... | collective-permute-start | bytes 36872 | tf_op jit(solution)/shard_map/ppermute | solution.py:343
  52.9 0.6 copy-start.8
  52.9 0.7 copy-start.12
  85.1 1.3 copy-start.2
  86.3 20.3 %all-to-all-start.4 = ((bf16[8,256,256]{2,1,0:T(8,128)(2,1)}), bf16[8,256,256]{2,1,0:T(8,128)(2,1)S(1)}, u32[]{:S(2)}, u32[]{:S(2)}) async-start(bf16[8,256,256]{2,1,0:T(8,128)(2,1)} %broadcast_in_dim.19), calls=%async_computation.4 | async-start | bytes 2097152 | tf_op jit(solution)/shard_map/all_to_all | solution.py:290
  106.8 24.7 %copy-start.13 = (f32[2,1024]{1,0:T(2,128)S(1)}, f32[2,1024]{1,0:T(2,128)}, u32[]{:S(2)}) copy-start(f32[2,1024]{1,0:T(2,128)} %get-tuple-element.7.stats) | copy-start | bytes 24580
  107.5 35.8 %copy-start.4 = (bf16[256,256]{1,0:T(8,128)(2,1)}, bf16[256,256]{1,0:T(8,128)(2,1)S(1)}, u32[]{:S(2)}) copy-start(bf16[256,256]{1,0:T(8,128)(2,1)S(1)} %get-tuple-element.12.pre) | copy-start | bytes 393220
  121.5 42.6 %all-to-all-start.6 = ((bf16[128,8,128]{2,1,0:T(8,128)(2,1)}), bf16[128,8,128]{2,1,0:T(8,128)(2,1)S(1)}, u32[]{:S(2)}, u32[]{:S(2)}) async-start(bf16[128,8,128]{2,1,0:T(8,128)(2,1)} %broadcast_in_dim.20), calls=%async_computation.6 | async-start | bytes 524288 | tf_op jit(solution)/shard_map/all_to_all | solution.py:290
  131.5 4.8 %collective-permute-start.6 = (f32[2,1024]{1,0:T(2,128)S(1)}, f32[2,1024]{1,0:T(2,128)S(1)}, u32[]{:S(2)}, u32[]{:S(2)}) collective-permute-start(f32[2,1024]{1,0:T(2,128)S(1)} %copy-done.13), channel_id=1, source_target_pairs={{128,0},{129,1},{130,2},{131,3},{132,4},{133,5},{134,6},{135,7},{1... | collective-permute-start | bytes 24584 | tf_op jit(solution)/shard_map/ppermute | solution.py:346
  136.2 0.6 copy-start.14
  149.6 16.4 %collective-permute-start.7 = (bf16[128,1024]{1,0:T(8,128)(2,1)}, bf16[128,1024]{1,0:T(8,128)(2,1)S(1)}, u32[]{:S(2)}, u32[]{:S(2)}) collective-permute-start(bf16[128,1024]{1,0:T(8,128)(2,1)} %query_grad.7), channel_id=1, source_target_pairs={{0,128},{1,129},{2,130},{3,131},{4,132},{5,133},{6,134},{7,135},{8... | collective-permute-start | bytes 786440 | tf_op jit(solution)/shard_map/ppermute | solution.py:354
  164.1 8.1 %collective-permute-start.8 = (bf16[128,8,128]{2,1,0:T(8,128)(2,1)S(1)}, bf16[128,8,128]{2,1,0:T(8,128)(2,1)S(1)}, u32[]{:S(2)}, u32[]{:S(2)}) collective-permute-start(bf16[128,8,128]{2,1,0:T(8,128)(2,1)S(1)} %all-to-all-done.6), channel_id=1, source_target_pairs={{0,8},{8,0},{1,9},{9,1},{2,10},{10,2},{3,11},{11,3},{4,12},{12,4},... | collective-permute-start | bytes 786440 | tf_op jit(solution)/shard_map/ppermute | solution.py:304

commit v2 on v0

--- a/solution.py
+++ b/solution.py
@@ -23,6 +23,7 @@
 BF16 = jnp.bfloat16
 SMEM = pl.BlockSpec(memory_space=pltpu.SMEM)
 VMEM = pl.BlockSpec(memory_space=pltpu.VMEM)
+GRANT = 16 * 2**20
 
 
 def dot_nt(a, b):
@@ -140,7 +141,7 @@
 def grad_kernel(lent, piece, pos, q, g, stats, mine, other, *refs):
     *extra, out, total, log_total, delta = refs
     rows = q.shape[0]
-    pairs = mine.shape[0] // 2
+    pairs = mine.shape[0] // 2 // PIECES
     first = piece * pairs
 
     def part(k, v, seen=None):
@@ -158,7 +159,7 @@
 
     def step(i, masked=False):
         for own, kv in ((True, mine), (False, other)):
-            k, v = pair_of(kv, i)
+            k, v = pair_of(kv, first + i)
             seen = visible(pos, own, first + i, (TILE, 2 * HD), 1) if masked else None
             part(k, v, seen)
 
@@ -167,10 +168,12 @@
         log_total[...] = jnp.broadcast_to(columns[:, 0:1], (rows, HD))
         delta[...] = jnp.broadcast_to(columns[:, 1:2], (rows, HD))
 
-    if piece == 0:
+    if lent and piece > 0:
+        for h in range(rows // HD):
+            at = slice(h * HD, (h + 1) * HD)
+            total[at, :] = extra[0][:, at].astype(F32) * (1.0 / SCALE)
+    else:
         total[...] = jnp.zeros((rows, HD), F32)
-    else:
-        total[...] = extra[0][...]
     if lent:
 
         @pl.when(pos[2] == 0)
@@ -189,66 +192,43 @@
         def _():
             step(half - first, True)
 
-    if piece < PIECES - 1:
-        out[...] = total[...]
-    else:
-        out[...] = (total[...] * SCALE).astype(out.dtype)
+    for h in range(rows // HD):
+        at = slice(h * HD, (h + 1) * HD)
+        out[:, at] = (total[at, :] * SCALE).astype(out.dtype)
+
+
+def call(kernel, out_shape, flops, *values, scratch=()):
+    held = [v if v.dtype == jnp.int32 else pltpu.with_memory_space_constraint(v, pltpu.VMEM) for v in values]
+    return pl.pallas_call(
+        kernel,
+        out_shape=out_shape,
+        in_specs=[SMEM if v.dtype == jnp.int32 else VMEM for v in values],
+        out_specs=jax.tree.map(lambda _: VMEM, out_shape),
+        scratch_shapes=list(scratch),
+        compiler_params=pltpu.CompilerParams(vmem_limit_bytes=GRANT),
+        cost_estimate=pl.CostEstimate(flops=flops, bytes_accessed=10**6, transcendentals=10**6),
+    )(*held)
 
 
 def sweep(pos, q, g, mine, other):
-    return pl.pallas_call(
-        sweep_kernel,
-        out_shape=jax.ShapeDtypeStruct((3, 8, q.shape[0]), F32),
-        in_specs=[SMEM] + [VMEM] * 4,
-        out_specs=VMEM,
-        cost_estimate=pl.CostEstimate(flops=10**9, bytes_accessed=2 * 10**6, transcendentals=2 * 10**6),
-        name="sweep",
-    )(pos, q, g, mine, other)
+    return call(sweep_kernel, jax.ShapeDtypeStruct((3, 8, q.shape[0]), F32), 10**9, pos, q, g, mine, other)
 
 
 def lent_sweep(pos, q, g, mine, other):
-    return pl.pallas_call(
-        lent_sweep_kernel,
-        out_shape=jax.ShapeDtypeStruct((3, q.shape[0]), F32),
-        in_specs=[SMEM] + [VMEM] * 4,
-        out_specs=VMEM,
-        cost_estimate=pl.CostEstimate(flops=10**9, bytes_accessed=2 * 10**6, transcendentals=2 * 10**6),
-        name="lent_sweep",
-    )(pos, q, g, mine, other)
+    out = jax.ShapeDtypeStruct((3, q.shape[0]), F32)
+    return call(lent_sweep_kernel, out, 10**9, pos, q, g, mine, other)
 
 
 def prefix_part(pos, q, g, pkv, state, lent):
-    return pl.pallas_call(
-        prefix_kernel,
-        out_shape=(
-            jax.ShapeDtypeStruct(pkv.shape, BF16),
-            jax.ShapeDtypeStruct((2, q.shape[0]), F32),
-        ),
-        in_specs=[SMEM] + [VMEM] * 5,
-        out_specs=(VMEM, VMEM),
-        cost_estimate=pl.CostEstimate(flops=3 * 10**8, bytes_accessed=10**6, transcendentals=5 * 10**5),
-        name="prefix_part",
-    )(pos, q, g, pkv, state, lent)
-
-
-def whole(value):
-    return pl.BlockSpec(value.shape, lambda *_: (0,) * value.ndim)
+    out = (jax.ShapeDtypeStruct(pkv.shape, BF16), jax.ShapeDtypeStruct((2, q.shape[0]), F32))
+    return call(prefix_kernel, out, 3 * 10**8, pos, q, g, pkv, state, lent)
 
 
 def query_grad_piece(lent, piece, pos, q, g, stats, mine, other, *extra):
-    blocks, *shape = mine.shape
-    part = pl.BlockSpec((blocks // PIECES, *shape), lambda *_: (piece, 0, 0))
-    out = jax.ShapeDtypeStruct(q.shape, BF16 if lent and piece == PIECES - 1 else F32)
-    return pl.pallas_call(
-        functools.partial(grad_kernel, lent, piece),
-        out_shape=out,
-        in_specs=[SMEM, whole(q), whole(g), whole(stats), part, part] + [whole(v) for v in extra],
-        out_specs=whole(out),
-        grid=(1,),
-        scratch_shapes=[pltpu.VMEM(q.shape, F32)] * 3,
-        cost_estimate=pl.CostEstimate(flops=10**9, bytes_accessed=3 * 10**6, transcendentals=10**6),
-        name="query_grad",
-    )(pos, q, g, stats, mine, other, *extra)
+    out = jax.ShapeDtypeStruct(q.shape[::-1], BF16)
+    scratch = [pltpu.VMEM(q.shape, F32)] * 3
+    kernel = functools.partial(grad_kernel, lent, piece)
+    return call(kernel, out, 10**9, pos, q, g, stats, mine, other, *extra, scratch=scratch)
 
 
 def w_hidden_kernel(place, embed, *refs):
@@ -267,15 +247,19 @@
 def w_hidden_grad(place, embed, *parts):
     npre, emb = embed.shape
     units = parts[0].shape[1]
-    return pl.pallas_call(
-        w_hidden_kernel,
-        out_shape=(jax.ShapeDtypeStruct((emb, units), F32), jax.ShapeDtypeStruct((units,), F32)),
-        in_specs=[SMEM] + [VMEM] * (1 + len(parts)),
-        out_specs=(VMEM, VMEM),
-        scratch_shapes=[pltpu.VMEM((npre, units), BF16)],
-        cost_estimate=pl.CostEstimate(flops=2 * 10**8, bytes_accessed=2 * 10**6, transcendentals=0),
-        name="w_hidden_grad",
-    )(place, embed, *parts)
+    out = (jax.ShapeDtypeStruct((emb, units), F32), jax.ShapeDtypeStruct((units,), F32))
+    scratch = [pltpu.VMEM((npre, units), BF16)]
+    return call(w_hidden_kernel, out, 2 * 10**8, place, embed, *parts, scratch=scratch)
+
+
+def w_out_kernel(hidden, grads, out):
+    for c in range(grads.shape[0]):
+        out[:, c, :] = dot_tn(hidden[...], grads[c])
+
+
+def w_out_grad(hidden, grads):
+    out = jax.ShapeDtypeStruct((hidden.shape[1], grads.shape[0], HD), F32)
+    return call(w_out_kernel, out, 10**8, hidden, grads)
 
 
 def exchange(value, axes):
@@ -336,20 +320,20 @@
     state = sweep(pos, q, g, mine, other)
     grads, stats = prefix_part(pos, q, g, pkv, state, lent_state)
     lent_stats = lax.ppermute(stats, "y", [(1, 0)])
-    own_grads = sum_parts(grads, SEQ).astype(BF16)
-    prefix_grads = to_all(own_grads, SEQ).reshape(2, npre, HD)
+    prefix_share = sum_parts(grads, SEQ).astype(BF16)
+    prefix_grads = to_all(prefix_share, SEQ).reshape(2, npre, HD)
     lent_grad = ()
     for piece in range(PIECES):
         lent_grad = (
             query_grad_piece(True, piece, pos, lent_q, lent_g, lent_stats, mine, other, *lent_grad),
         )
     lent_grad = lax.ppermute(*lent_grad, "y", [(0, 1)])
-    query_grad = pkv
+    own_grads = []
     for piece in range(PIECES):
-        query_grad = query_grad_piece(False, piece, pos, q, g, stats, mine, other, query_grad)
-    query_grad = (query_grad + lent_grad.astype(F32)).astype(BF16)
-    query_grad = query_grad.reshape(-1, queries.shape[0], HD).transpose(1, 0, 2).reshape(queries.shape)
-    grad_w_out = jnp.einsum("ph,cpk->hck", hidden, prefix_grads, preferred_element_type=F32)
+        first = (pkv,) if piece == 0 else ()
+        own_grads.append(query_grad_piece(False, piece, pos, q, g, stats, mine, other, *first))
+    query_grad = sum(v.astype(F32) for v in (*own_grads, lent_grad)).astype(BF16)
+    grad_w_out = w_out_grad(hidden, prefix_grads)
     hidden_part = jnp.einsum("cpk,hck->ph", prefix_grads, w_out, preferred_element_type=F32)
     parts = exchange(hidden_part.reshape(heads, share, units), HEAD)
     hidden_grad = jnp.sum(parts, axis=0)

time: 168 us -> 163 us (0.970)
  the two profiles are of different devices: /device:TPU:233 before, /device:TPU:193 now
where the time goes in v2:
time: 163 us; the launch traced here: 162 us
  starting transfers between devices  56.2 us (34%)
  Pallas kernels  32.5 us (20%)
  blocking collectives  27.9 us (17%)
  waiting for transfers between devices  27.6 us (17%)
  local copies, waits for them, and re-layouts  6.83 us (4%)
  other arithmetic  6.38 us (4%)
  matrix products  3.42 us (2%)
    all_to_all x5, starting transfers between devices, exchange(): return lax.all_to_all(value, axes, 0, 0, tiled=True)  36.3 us
    pallas_call x9, Pallas kernels, call(): pl.pallas_call(kernel, out_shape=out_shape, in_specs=[SMEM if v.dtype ==...  32.5 us
    all_to_all x2, blocking collectives, exchange(): return lax.all_to_all(value, axes, 0, 0, tiled=True)  27.9 us
    all_to_all x5, waiting for transfers between devices, exchange(): return lax.all_to_all(value, axes, 0, 0, tiled=True)  26.4 us
    ppermute x8, starting transfers between devices, shift(): lax.ppermute(value, axis, [(i, (i + steps) % count) for i in range(count)])  12.8 us
  transfers between devices with their start and end apart: 18, of which 5 were waited for; matrix products, arithmetic and copies ran while one was open for 3% of the time, Pallas kernels for 19%

profile of v2, /device:TPU:193, one launch (start us, length us, event | category | flops | bytes accessed | tf_op | source)
XLA Modules:
  0.0 161.9 jit_solution(11507093346489282078)
XLA Ops:
  1.7 2.1 %fusion.5 = (bf16[256,256]{1,0:T(8,128)(2,1)S(1)}, f32[256,256]{1,0:T(8,128)}) fusion(f32[256]{0:T(256)} %param.10, bf16[256,1024]{1,0:T(8,128)(2,1)} %embed.1, bf16[1024,256]{1,0:T(8,128)(2,1)S(1)} %copy-done), kind=kOutput, calls=%fused_computation.25 | convolution fusion | flops 134348800 | bytes 1442816 | tf_op jit(solution)/shard_map/dot_general | solution.py:297
  5.0 5.7 %all-to-all-start = ((bf16[8,320,128]{2,1,0:T(8,128)(2,1)}), bf16[8,320,128]{2,1,0:T(8,128)(2,1)S(1)}, u32[]{:S(2)}, u32[]{:S(2)}) async-start(bf16[8,320,128]{2,1,0:T(8,128)(2,1)} %pad_maximum_fusion), calls=%async_computation | async-start | bytes 1310720 | tf_op jit(solution)/shard_map/all_to_all | solution.py:266
  10.7 1.3 collective-permute-start.3
  12.0 1.3 collective-permute-start.4
  13.4 14.1 %all-to-all-done.mine = bf16[8,320,128]{2,1,0:T(8,128)(2,1)S(1)} async-done(((bf16[8,320,128]{2,1,0:T(8,128)(2,1)}), bf16[8,320,128]{2,1,0:T(8,128)(2,1)S(1)}, u32[]{:S(2)}, u32[]{:S(2)}) %all-to-all-start) | async-done | bytes 655392 | tf_op jit(solution)/shard_map/all_to_all | solution.py:266
  27.5 1.1 collective-permute-start
  29.5 1.3 collective-permute-start.1
  32.9 6.8 %all-to-all-start.1 = ((bf16[8,64,128]{2,1,0:T(8,128)(2,1)}), bf16[8,64,128]{2,1,0:T(8,128)(2,1)S(1)}, u32[]{:S(2)}, u32[]{:S(2)}) async-start(bf16[8,64,128]{2,1,0:T(8,128)(2,1)} %broadcast_in_dim.14), calls=%async_computation.1 | async-start | bytes 262144 | tf_op jit(solution)/shard_map/all_to_all | solution.py:266
  40.7 4.1 %shard_map.120 = f32[3,1024]{1,0:T(4,128)S(1)} custom-call(s32[3]{0:T(128)S(1)} %pad_add_fusion.pos, bf16[1024,128]{1,0:T(8,128)(2,1)S(1)} %bitcast.74, bf16[1024,128]{1,0:T(8,128)(2,1)S(1)} %bitcast.77, bf16[8,320,128]{2,1,0:T(8,128)(2,1)S(1)} %all-to-all-done.mine, bf16[8,320,128]{2,1,0:T(8,128)(2,1)S(1)} %collective-permute-done.2.other), custom_call_target="tpu_custom_call" | custom-call | flops 1000000000 | bytes 1000000 | tf_op jit(solution)/shard_map/pallas_call | solution.py:202
  44.8 1.3 collective-permute-start.5
  46.1 4.0 %shard_map.119.state = f32[3,8,1024]{2,1,0:T(8,128)S(1)} custom-call(s32[3]{0:T(128)S(1)} %pad_add_fusion.pos, bf16[1024,128]{1,0:T(8,128)(2,1)S(1)} %bitcast.66, bf16[1024,128]{1,0:T(8,128)(2,1)S(1)} %bitcast.70, bf16[8,320,128]{2,1,0:T(8,128)(2,1)S(1)} %all-to-all-done.mine, bf16[8,320,128]{2,1,0:T(8,128)(2,1)S(1)} %collective-permute-done.2.other), custom_call_target="tpu_custom_call" | custom-call | flops 1000000000 | bytes 1000000 | tf_op jit(solution)/shard_map/pallas_call | solution.py:202
  50.1 2.1 %shard_map.121 = (bf16[2,256,128]{2,1,0:T(8,128)(2,1)S(1)}, f32[2,1024]{1,0:T(2,128)S(1)}) custom-call(s32[3]{0:T(128)S(1)} %pad_add_fusion.pos, bf16[1024,128]{1,0:T(8,128)(2,1)S(1)} %bitcast.67, bf16[1024,128]{1,0:T(8,128)(2,1)S(1)} %bitcast.71, bf16[2,256,128]{2,1,0:T(8,128)(2,1)S(1)} %bitcast.80, f32[3,8,1024]{2,1,0:T(8,128)S(1)} %shard_map.119.state, ...), custom_call_target="tpu_custom_call" | custom-call | flops 300000000 | bytes 1000000 | tf_op jit(solution)/shard_map/pallas_call | solution.py:202
  52.2 14.5 %all_to_all.35 = bf16[32,16,128]{2,1,0:T(8,128)(2,1)S(1)} all-to-all(bf16[32,16,128]{2,1,0:T(8,128)(2,1)S(1)} %bitcast.82), channel_id=1, replica_groups=mesh['y'=2,'z'=8,'c'=2,'x'=4,'w'=2] {'y','z','c'}, dimensions={0} | all-to-all | bytes 262144 | tf_op jit(solution)/shard_map/all_to_all | solution.py:266
  66.8 13.4 %all_to_all.36 = bf16[32,16,128]{2,1,0:T(8,128)(2,1)S(1)} all-to-all(bf16[32,16,128]{2,1,0:T(8,128)(2,1)S(1)} %broadcast_in_dim.15), channel_id=1, replica_groups=mesh['y'=2,'z'=8,'c'=2,'x'=4,'w'=2] {'y','z','c'}, dimensions={0} | all-to-all | bytes 262144 | tf_op jit(solution)/shard_map/all_to_all | solution.py:266
  81.1 6.7 %all-to-all-start.4 = ((f32[8,32,256]{2,1,0:T(8,128)}), f32[8,32,256]{2,1,0:T(8,128)S(1)}, u32[]{:S(2)}, u32[]{:S(2)}) async-start(f32[8,32,256]{2,1,0:T(8,128)} %convolution_bitcast_fusion), calls=%async_computation.4 | async-start | bytes 524288 | tf_op jit(solution)/shard_map/all_to_all | solution.py:266
  87.8 8.0 %all-to-all-done.4 = f32[8,32,256]{2,1,0:T(8,128)S(1)} async-done(((f32[8,32,256]{2,1,0:T(8,128)}), f32[8,32,256]{2,1,0:T(8,128)S(1)}, u32[]{:S(2)}, u32[]{:S(2)}) %all-to-all-start.4) | async-done | bytes 262176 | tf_op jit(solution)/shard_map/all_to_all | solution.py:266
  98.1 8.2 %all-to-all-start.5 = ((bf16[32,8,128]{2,1,0:T(8,128)(2,1)}), bf16[32,8,128]{2,1,0:T(8,128)(2,1)S(1)}, u32[]{:S(2)}, u32[]{:S(2)}) async-start(bf16[32,8,128]{2,1,0:T(8,128)(2,1)} %bitcast.42), calls=%async_computation.5 | async-start | bytes 131072 | tf_op jit(solution)/shard_map/all_to_all | solution.py:266
  106.3 1.3 collective-permute-start.6
  107.6 4.3 %all-to-all-done.5 = bf16[32,8,128]{2,1,0:T(8,128)(2,1)S(1)} async-done(((bf16[32,8,128]{2,1,0:T(8,128)(2,1)}), bf16[32,8,128]{2,1,0:T(8,128)(2,1)S(1)}, u32[]{:S(2)}, u32[]{:S(2)}) %all-to-all-start.5) | async-done | bytes 65568 | tf_op jit(solution)/shard_map/all_to_all | solution.py:266
  112.7 8.9 %all-to-all-start.6 = ((bf16[128,8,128]{2,1,0:T(8,128)(2,1)}), bf16[128,8,128]{2,1,0:T(8,128)(2,1)}, u32[]{:S(2)}, u32[]{:S(2)}) async-start(bf16[128,8,128]{2,1,0:T(8,128)(2,1)} %broadcast_in_dim.16), calls=%async_computation.6 | async-start | bytes 524288 | tf_op jit(solution)/shard_map/all_to_all | solution.py:266
  121.7 4.8 %shard_map.124.refs_0_ = bf16[128,1024]{1,0:T(8,128)(2,1)S(1)} custom-call(s32[3]{0:T(128)S(1)} %pad_add_fusion.pos, bf16[1024,128]{1,0:T(8,128)(2,1)S(1)} %bitcast.75, bf16[1024,128]{1,0:T(8,128)(2,1)S(1)} %bitcast.78, f32[2,1024]{1,0:T(2,128)S(1)} %collective-permute-done.6.stats, bf16[8,320,128]{2,1,0:T(8,128)(2,1)S(1)} %all-to-all-done.mine, ...), custom_call_target="tpu_custom_call" | custom-call | flops 1000000000 | bytes 1000000 | tf_op jit(solution)/shard_map/pallas_call | solution.py:202
  127.9 4.7 %shard_map.125 = bf16[128,1024]{1,0:T(8,128)(2,1)S(1)} custom-call(s32[3]{0:T(128)S(1)} %pad_add_fusion.pos, bf16[1024,128]{1,0:T(8,128)(2,1)S(1)} %bitcast.76, bf16[1024,128]{1,0:T(8,128)(2,1)S(1)} %bitcast.79, f32[2,1024]{1,0:T(2,128)S(1)} %copy-done.3, bf16[8,320,128]{2,1,0:T(8,128)(2,1)S(1)} %all-to-all-done.mine, ...), custom_call_target="tpu_custom_call" | custom-call | flops 1000000000 | bytes 1000000 | tf_op jit(solution)/shard_map/pallas_call | solution.py:202
  132.6 2.0 %collective-permute-start.7 = (bf16[128,1024]{1,0:T(8,128)(2,1)S(1)}, bf16[128,1024]{1,0:T(8,128)(2,1)}, u32[]{:S(2)}, u32[]{:S(2)}) collective-permute-start(bf16[128,1024]{1,0:T(8,128)(2,1)S(1)} %shard_map.125), channel_id=1, source_target_pairs={{0,128},{1,129},{2,130},{3,131},{4,132},{5,133},{6,134},{7,135},{8... | collective-permute-start | bytes 786440 | tf_op jit(solution)/shard_map/ppermute | solution.py:330
  134.6 4.6 %shard_map.123 = bf16[128,1024]{1,0:T(8,128)(2,1)S(1)} custom-call(s32[3]{0:T(128)S(1)} %pad_add_fusion.pos, bf16[1024,128]{1,0:T(8,128)(2,1)S(1)} %bitcast.68, bf16[1024,128]{1,0:T(8,128)(2,1)S(1)} %bitcast.72, f32[2,1024]{1,0:T(2,128)S(1)} %get-tuple-element.9.stats, bf16[8,320,128]{2,1,0:T(8,128)(2,1)S(1)} %all-to-all-done.mine, ...), custom_call_target="tpu_custom_call" | custom-call | flops 1000000000 | bytes 1000000 | tf_op jit(solution)/shard_map/pallas_call | solution.py:202
  139.2 2.9 %collective-permute-start.8 = (bf16[32,256]{1,0:T(8,128)(2,1)S(1)}, bf16[32,256]{1,0:T(8,128)(2,1)S(1)}, u32[]{:S(2)}, u32[]{:S(2)}) collective-permute-start(bf16[32,256]{1,0:T(8,128)(2,1)S(1)} %copy-done.8), channel_id=1, source_target_pairs={{0,1},{1,0},{2,3},{3,2},{4,5},{5,4},{6,7},{7,6},{8,9},{9,8},{10,11... | collective-permute-start | bytes 49160 | tf_op jit(solution)/shard_map/ppermute | solution.py:280
  142.1 5.2 %shard_map.122 = bf16[128,1024]{1,0:T(8,128)(2,1)S(1)} custom-call(s32[3]{0:T(128)S(1)} %pad_add_fusion.pos, bf16[1024,128]{1,0:T(8,128)(2,1)S(1)} %bitcast.69, bf16[1024,128]{1,0:T(8,128)(2,1)S(1)} %bitcast.73, f32[2,1024]{1,0:T(2,128)S(1)} %get-tuple-element.9.stats, bf16[8,320,128]{2,1,0:T(8,128)(2,1)S(1)} %all-to-all-done.mine, ...), custom_call_target="tpu_custom_call" | custom-call | flops 1000000000 | bytes 1000000 | tf_op jit(solution)/shard_map/pallas_call | solution.py:202
  147.4 1.5 collective-permute-start.9
  148.8 2.8 %collective-permute-start.10 = (bf16[64,256]{1,0:T(8,128)(2,1)S(1)}, bf16[64,256]{1,0:T(8,128)(2,1)S(1)}, u32[]{:S(2)}, u32[]{:S(2)}) collective-permute-start(bf16[64,256]{1,0:T(8,128)(2,1)S(1)} %pad_maximum_fusion.2.refs_0_), channel_id=1, source_target_pairs={{0,4},{2,6},{4,0},{6,2},{1,5},{3,7},{5,1},{7,3},{8,12},{10,14},{12... | collective-permute-start | bytes 98312 | tf_op jit(solution)/shard_map/ppermute | solution.py:280
  152.6 2.2 %collective-permute-start.12 = (bf16[128,8,128]{2,1,0:T(8,128)(2,1)}, bf16[128,8,128]{2,1,0:T(8,128)(2,1)S(1)}, u32[]{:S(2)}, u32[]{:S(2)}) collective-permute-start(bf16[128,8,128]{2,1,0:T(8,128)(2,1)} %all-to-all-done.6), channel_id=1, source_target_pairs={{0,8},{8,0},{1,9},{9,1},{2,10},{10,2},{3,11},{11,3},{4,12},{12,4},... | collective-permute-start | bytes 786440 | tf_op jit(solution)/shard_map/ppermute | solution.py:280
  154.9 1.8 %add_convert_fusion = bf16[128,1024]{1,0:T(8,128)(2,1)} fusion(bf16[128,1024]{1,0:T(8,128)(2,1)} %collective-permute-done.7, bf16[128,1024]{1,0:T(8,128)(2,1)S(1)} %shard_map.123, bf16[128,1024]{1,0:T(8,128)(2,1)S(1)} %shard_map.122), kind=kLoop, calls=%fused_computation.8 | loop fusion | flops 786432 | bytes 1048576 | tf_op jit(solution)/shard_map/convert_element_type | solution.py:335
  156.6 1.1 shard_map.126
  157.7 1.9 %shard_map.127 = (f32[1024,256]{1,0:T(8,128)}, f32[256]{0:T(256)}) custom-call(s32[2]{0:T(128)S(1)} %pad_add_fusion.1.place, bf16[256,1024]{1,0:T(8,128)(2,1)S(1)} %copy-done.1, bf16[64,256]{1,0:T(8,128)(2,1)S(1)} %pad_maximum_fusion.2.refs_0_, bf16[64,256]{1,0:T(8,128)(2,1)S(1)} %collective-permute-done.9.refs_1_, ...), custom_call_target="tpu_custom_call" | custom-call | flops 200000000 | bytes 1000000 | tf_op jit(solution)/shard_map/pallas_call | solution.py:202
  (67 shorter events, 15.0 us)
Async XLA Ops:
  0.6 1.0 copy-start
  0.6 3.1 %copy-start.4 = (bf16[256,2,128]{2,1,0:T(2,128)(2,1)S(1)}, bf16[256,2,128]{2,1,0:T(2,128)(2,1)}, u32[]{:S(2)}) copy-start(bf16[256,2,128]{2,1,0:T(2,128)(2,1)} %param.11) | copy-start | bytes 393220
  0.7 3.3 %copy-start.9 = (bf16[128,128]{1,0:T(8,128)(2,1)S(1)}, bf16[128,128]{1,0:T(8,128)(2,1)}, u32[]{:S(2)}) copy-start(bf16[128,128]{1,0:T(8,128)(2,1)} %param.14) | copy-start | bytes 98308
  0.7 3.3 %copy-start.10 = (bf16[128,128]{1,0:T(8,128)(2,1)S(1)}, bf16[128,128]{1,0:T(8,128)(2,1)}, u32[]{:S(2)}) copy-start(bf16[128,128]{1,0:T(8,128)(2,1)} %param.13) | copy-start | bytes 98308
  4.0 6.6 %copy-start.5 = (bf16[128,1024]{1,0:T(8,128)(2,1)S(1)}, bf16[128,1024]{1,0:T(8,128)(2,1)}, u32[]{:S(2)}) copy-start(bf16[128,1024]{1,0:T(8,128)(2,1)} %param.12) | copy-start | bytes 786436
  4.1 7.9 %copy-start.6 = (bf16[128,1024]{1,0:T(8,128)(2,1)S(1)}, bf16[128,1024]{1,0:T(8,128)(2,1)}, u32[]{:S(2)}) copy-start(bf16[128,1024]{1,0:T(8,128)(2,1)} %param.15) | copy-start | bytes 786436
  5.0 22.5 %all-to-all-start = ((bf16[8,320,128]{2,1,0:T(8,128)(2,1)}), bf16[8,320,128]{2,1,0:T(8,128)(2,1)S(1)}, u32[]{:S(2)}, u32[]{:S(2)}) async-start(bf16[8,320,128]{2,1,0:T(8,128)(2,1)} %pad_maximum_fusion), calls=%async_computation | async-start | bytes 1310720 | tf_op jit(solution)/shard_map/all_to_all | solution.py:266
  10.7 20.1 %collective-permute-start.3 = (bf16[128,1024]{1,0:T(8,128)(2,1)S(1)}, bf16[128,1024]{1,0:T(8,128)(2,1)}, u32[]{:S(2)}, u32[]{:S(2)}) collective-permute-start(bf16[128,1024]{1,0:T(8,128)(2,1)S(1)} %copy-done.5), channel_id=1, source_target_pairs={{128,0},{129,1},{130,2},{131,3},{132,4},{133,5},{134,6},{135,7},{1... | collective-permute-start | bytes 786440 | tf_op jit(solution)/shard_map/ppermute | solution.py:309
  12.0 27.7 %collective-permute-start.4 = (bf16[128,1024]{1,0:T(8,128)(2,1)S(1)}, bf16[128,1024]{1,0:T(8,128)(2,1)}, u32[]{:S(2)}, u32[]{:S(2)}) collective-permute-start(bf16[128,1024]{1,0:T(8,128)(2,1)S(1)} %copy-done.6), channel_id=1, source_target_pairs={{128,0},{129,1},{130,2},{131,3},{132,4},{133,5},{134,6},{135,7},{1... | collective-permute-start | bytes 786440 | tf_op jit(solution)/shard_map/ppermute | solution.py:310
  27.5 1.9 %collective-permute-start = (f32[64,128]{1,0:T(8,128)S(1)}, f32[64,128]{1,0:T(8,128)S(1)}, u32[]{:S(2)}, u32[]{:S(2)}) collective-permute-start(f32[64,128]{1,0:T(8,128)S(1)} %convert_reduce_fusion), channel_id=1, source_target_pairs={{0,8},{8,0},{1,9},{9,1},{2,10},{10,2},{3,11},{11,3},{4,12},{12,4},... | collective-permute-start | bytes 98312 | tf_op jit(solution)/shard_map/ppermute | solution.py:280
  28.7 12.0 %collective-permute-start.2 = (bf16[8,320,128]{2,1,0:T(8,128)(2,1)S(1)}, bf16[8,320,128]{2,1,0:T(8,128)(2,1)S(1)}, u32[]{:S(2)}, u32[]{:S(2)}) collective-permute-start(bf16[8,320,128]{2,1,0:T(8,128)(2,1)S(1)} %all-to-all-done.mine), channel_id=1, source_target_pairs={{0,8},{8,0},{1,9},{9,1},{2,10},{10,2},{3,11},{11,3},{4,12},{12,4},... | collective-permute-start | bytes 1966088 | tf_op jit(solution)/shard_map/ppermute | solution.py:280
  29.5 2.8 %collective-permute-start.1 = (f32[64,128]{1,0:T(8,128)S(1)}, f32[64,128]{1,0:T(8,128)S(1)}, u32[]{:S(2)}, u32[]{:S(2)}) collective-permute-start(f32[64,128]{1,0:T(8,128)S(1)} %add.28), channel_id=1, source_target_pairs={{0,128},{128,0},{1,129},{129,1},{2,130},{130,2},{3,131},{131,3},{4... | collective-permute-start | bytes 98312 | tf_op jit(solution)/shard_map/ppermute | solution.py:280
  32.9 17.2 %all-to-all-start.1 = ((bf16[8,64,128]{2,1,0:T(8,128)(2,1)}), bf16[8,64,128]{2,1,0:T(8,128)(2,1)S(1)}, u32[]{:S(2)}, u32[]{:S(2)}) async-start(bf16[8,64,128]{2,1,0:T(8,128)(2,1)} %broadcast_in_dim.14), calls=%async_computation.1 | async-start | bytes 262144 | tf_op jit(solution)/shard_map/all_to_all | solution.py:266
  44.8 5.3 %collective-permute-start.5 = (f32[3,1024]{1,0:T(4,128)S(1)}, f32[3,1024]{1,0:T(4,128)S(1)}, u32[]{:S(2)}, u32[]{:S(2)}) collective-permute-start(f32[3,1024]{1,0:T(4,128)S(1)} %shard_map.120), channel_id=1, source_target_pairs={{0,128},{1,129},{2,130},{3,131},{4,132},{5,133},{6,134},{7,135},{8... | collective-permute-start | bytes 36872 | tf_op jit(solution)/shard_map/ppermute | solution.py:319
  81.1 14.7 %all-to-all-start.4 = ((f32[8,32,256]{2,1,0:T(8,128)}), f32[8,32,256]{2,1,0:T(8,128)S(1)}, u32[]{:S(2)}, u32[]{:S(2)}) async-start(f32[8,32,256]{2,1,0:T(8,128)} %convolution_bitcast_fusion), calls=%async_computation.4 | async-start | bytes 524288 | tf_op jit(solution)/shard_map/all_to_all | solution.py:266
  97.2 0.9 copy-start.7
  98.1 13.8 %all-to-all-start.5 = ((bf16[32,8,128]{2,1,0:T(8,128)(2,1)}), bf16[32,8,128]{2,1,0:T(8,128)(2,1)S(1)}, u32[]{:S(2)}, u32[]{:S(2)}) async-start(bf16[32,8,128]{2,1,0:T(8,128)(2,1)} %bitcast.42), calls=%async_computation.5 | async-start | bytes 131072 | tf_op jit(solution)/shard_map/all_to_all | solution.py:266
  106.3 15.4 %collective-permute-start.6 = (f32[2,1024]{1,0:T(2,128)S(1)}, f32[2,1024]{1,0:T(2,128)S(1)}, u32[]{:S(2)}, u32[]{:S(2)}) collective-permute-start(f32[2,1024]{1,0:T(2,128)S(1)} %get-tuple-element.9.stats), channel_id=1, source_target_pairs={{128,0},{129,1},{130,2},{131,3},{132,4},{133,5},{134,6},{135,7},{1... | collective-permute-start | bytes 24584 | tf_op jit(solution)/shard_map/ppermute | solution.py:322
  112.7 39.9 %all-to-all-start.6 = ((bf16[128,8,128]{2,1,0:T(8,128)(2,1)}), bf16[128,8,128]{2,1,0:T(8,128)(2,1)}, u32[]{:S(2)}, u32[]{:S(2)}) async-start(bf16[128,8,128]{2,1,0:T(8,128)(2,1)} %broadcast_in_dim.16), calls=%async_computation.6 | async-start | bytes 524288 | tf_op jit(solution)/shard_map/all_to_all | solution.py:266
  126.6 0.6 copy-start.2
  127.2 0.7 copy-start.3
  132.6 6.7 %copy-start.8 = (bf16[32,256]{1,0:T(8,128)(2,1)S(1)}, bf16[32,256]{1,0:T(8,128)(2,1)}, u32[]{:S(2)}) copy-start(bf16[32,256]{1,0:T(8,128)(2,1)} %copy-done.7) | copy-start | bytes 49156
  132.6 22.3 %collective-permute-start.7 = (bf16[128,1024]{1,0:T(8,128)(2,1)S(1)}, bf16[128,1024]{1,0:T(8,128)(2,1)}, u32[]{:S(2)}, u32[]{:S(2)}) collective-permute-start(bf16[128,1024]{1,0:T(8,128)(2,1)S(1)} %shard_map.125), channel_id=1, source_target_pairs={{0,128},{1,129},{2,130},{3,131},{4,132},{5,133},{6,134},{7,135},{8... | collective-permute-start | bytes 786440 | tf_op jit(solution)/shard_map/ppermute | solution.py:330
  139.2 8.1 %collective-permute-start.8 = (bf16[32,256]{1,0:T(8,128)(2,1)S(1)}, bf16[32,256]{1,0:T(8,128)(2,1)S(1)}, u32[]{:S(2)}, u32[]{:S(2)}) collective-permute-start(bf16[32,256]{1,0:T(8,128)(2,1)S(1)} %copy-done.8), channel_id=1, source_target_pairs={{0,1},{1,0},{2,3},{3,2},{4,5},{5,4},{6,7},{7,6},{8,9},{9,8},{10,11... | collective-permute-start | bytes 49160 | tf_op jit(solution)/shard_map/ppermute | solution.py:280
  147.4 10.3 %collective-permute-start.9 = (bf16[64,256]{1,0:T(8,128)(2,1)S(1)}, bf16[64,256]{1,0:T(8,128)(2,1)S(1)}, u32[]{:S(2)}, u32[]{:S(2)}) collective-permute-start(bf16[64,256]{1,0:T(8,128)(2,1)S(1)} %pad_maximum_fusion.2.refs_0_), channel_id=1, source_target_pairs={{0,2},{2,4},{4,6},{6,0},{1,3},{3,5},{5,7},{7,1},{8,10},{10,12},{12... | collective-permute-start | bytes 98312 | tf_op jit(solution)/shard_map/ppermute | solution.py:280
  148.8 8.9 %collective-permute-start.10 = (bf16[64,256]{1,0:T(8,128)(2,1)S(1)}, bf16[64,256]{1,0:T(8,128)(2,1)S(1)}, u32[]{:S(2)}, u32[]{:S(2)}) collective-permute-start(bf16[64,256]{1,0:T(8,128)(2,1)S(1)} %pad_maximum_fusion.2.refs_0_), channel_id=1, source_target_pairs={{0,4},{2,6},{4,0},{6,2},{1,5},{3,7},{5,1},{7,3},{8,12},{10,14},{12... | collective-permute-start | bytes 98312 | tf_op jit(solution)/shard_map/ppermute | solution.py:280
  151.7 6.0 %collective-permute-start.11 = (bf16[64,256]{1,0:T(8,128)(2,1)S(1)}, bf16[64,256]{1,0:T(8,128)(2,1)S(1)}, u32[]{:S(2)}, u32[]{:S(2)}) collective-permute-start(bf16[64,256]{1,0:T(8,128)(2,1)S(1)} %pad_maximum_fusion.2.refs_0_), channel_id=1, source_target_pairs={{0,6},{2,0},{4,2},{6,4},{1,7},{3,1},{5,3},{7,5},{8,14},{10,8},{12,... | collective-permute-start | bytes 98312 | tf_op jit(solution)/shard_map/ppermute | solution.py:280
  152.6 7.0 %collective-permute-start.12 = (bf16[128,8,128]{2,1,0:T(8,128)(2,1)}, bf16[128,8,128]{2,1,0:T(8,128)(2,1)S(1)}, u32[]{:S(2)}, u32[]{:S(2)}) collective-permute-start(bf16[128,8,128]{2,1,0:T(8,128)(2,1)} %all-to-all-done.6), channel_id=1, source_target_pairs={{0,8},{8,0},{1,9},{9,1},{2,10},{10,2},{3,11},{11,3},{4,12},{12,4},... | collective-permute-start | bytes 786440 | tf_op jit(solution)/shard_map/ppermute | solution.py:280
  156.6 1.1 copy-start.1

commit v3 on v2

--- a/solution.py
+++ b/solution.py
@@ -168,7 +168,7 @@
         log_total[...] = jnp.broadcast_to(columns[:, 0:1], (rows, HD))
         delta[...] = jnp.broadcast_to(columns[:, 1:2], (rows, HD))
 
-    if lent and piece > 0:
+    if piece > 0:
         for h in range(rows // HD):
             at = slice(h * HD, (h + 1) * HD)
             total[at, :] = extra[0][:, at].astype(F32) * (1.0 / SCALE)
@@ -231,6 +231,22 @@
     return call(kernel, out, 10**9, pos, q, g, stats, mine, other, *extra, scratch=scratch)
 
 
+def embed_kernel(parts, factor, w_hidden, pre, embed):
+    pre[...] = (jnp.sum(parts[...], axis=0) * factor[...]).astype(BF16)
+    rows = dot_nt(pre[...], w_hidden[...])
+    for k in range(embed.shape[1]):
+        embed[:, k, :] = rows[:, k * HD : (k + 1) * HD].astype(BF16)
+
+
+def embed_rows(parts, factor, w_hidden):
+    share = factor.shape[0]
+    out = (
+        jax.ShapeDtypeStruct(factor.shape, BF16),
+        jax.ShapeDtypeStruct((share, w_hidden.shape[0] // HD, HD), BF16),
+    )
+    return call(embed_kernel, out, 2 * 10**7, parts, factor, w_hidden)
+
+
 def w_hidden_kernel(place, embed, *refs):
     *parts, grad_w, grad_b, pre = refs
     lines = len(parts)
@@ -298,6 +314,8 @@
     tangent = jnp.tanh(hidden_pre)
     hidden = tangent.astype(BF16)
     partial_kv = jnp.einsum("ph,hck->cpk", hidden, w_out, preferred_element_type=F32)
+    own_tangent = lax.dynamic_slice_in_dim(tangent, head * share, share, 0)
+    factor = lax.optimization_barrier(1.0 - own_tangent * own_tangent)
     groups = lax.axis_size("z")
     kv = jnp.concatenate([keys, values], 0)
     partial_kv = partial_kv.reshape(groups, -1, HD).astype(BF16)
@@ -311,8 +329,8 @@
     lent_q = by_head(lent_q)
     lent_g = by_head(lent_g)
     other = shift(mine, "c", 1)
-    own = jnp.sum(mine[:, kv.shape[0] :].astype(F32), axis=0)
-    own = own + shift(own, "c", 1)
+    sides = [jnp.sum(v[:, kv.shape[0] :].astype(F32), axis=0) for v in (mine, other)]
+    own = sides[0] + sides[1]
     own = (own + shift(own, "y", 1)).astype(BF16)
     pkv = to_all(own, "z").reshape(2, npre, HD)
     lent_state = lent_sweep(pos, lent_q, lent_g, mine, other)
@@ -328,19 +346,15 @@
             query_grad_piece(True, piece, pos, lent_q, lent_g, lent_stats, mine, other, *lent_grad),
         )
     lent_grad = lax.ppermute(*lent_grad, "y", [(0, 1)])
-    own_grads = []
+    own_grad = pkv
     for piece in range(PIECES):
-        first = (pkv,) if piece == 0 else ()
-        own_grads.append(query_grad_piece(False, piece, pos, q, g, stats, mine, other, *first))
-    query_grad = sum(v.astype(F32) for v in (*own_grads, lent_grad)).astype(BF16)
+        own_grad = query_grad_piece(False, piece, pos, q, g, stats, mine, other, own_grad)
+    query_grad = (own_grad.astype(F32) + lent_grad.astype(F32)).astype(BF16)
     grad_w_out = w_out_grad(hidden, prefix_grads)
     hidden_part = jnp.einsum("cpk,hck->ph", prefix_grads, w_out, preferred_element_type=F32)
     parts = exchange(hidden_part.reshape(heads, share, units), HEAD)
-    hidden_grad = jnp.sum(parts, axis=0)
-    own_tangent = lax.dynamic_slice_in_dim(tangent, head * share, share, 0)
-    pre_part = (hidden_grad * (1.0 - own_tangent * own_tangent)).astype(BF16)
-    embed_part = dot_nt(pre_part, w_hidden)
-    own_embed = sum_parts(embed_part, CYZ).astype(BF16)
+    pre_part, embed_part = embed_rows(parts, factor, w_hidden)
+    own_embed = jnp.sum(exchange(embed_part, CYZ).astype(F32), axis=0).astype(BF16)
     near = to_all(own_embed, OWNERS)
     far = shift(near, "c", 1)
     sides = jnp.stack([jnp.where(core == 0, near, far), jnp.where(core == 0, far, near)], 0)

time: 163 us -> 160 us (0.982)
  the two profiles are of different devices: /device:TPU:193 before, /device:TPU:64 now
where the time goes in v3:
time: 160 us; the launch traced here: 159 us
  starting transfers between devices  51 us (32%)
  waiting for transfers between devices  39.5 us (25%)
  blocking collectives  29.4 us (18%)
  Pallas kernels  28.1 us (18%)
  local copies, waits for them, and re-layouts  3.99 us (2%)
  other arithmetic  3.87 us (2%)
  matrix products  2.62 us (2%)
    all_to_all x5, starting transfers between devices, exchange(): return lax.all_to_all(value, axes, 0, 0, tiled=True)  34.9 us
    all_to_all x2, blocking collectives, exchange(): return lax.all_to_all(value, axes, 0, 0, tiled=True)  29.4 us
    all_to_all x5, waiting for transfers between devices, exchange(): return lax.all_to_all(value, axes, 0, 0, tiled=True)  28.9 us
    pallas_call x10, Pallas kernels, call(): pl.pallas_call(kernel, out_shape=out_shape, in_specs=[SMEM if v.dtype ==...  28.1 us
    ppermute x7, waiting for transfers between devices, shift(): lax.ppermute(value, axis, [(i, (i + steps) % count) for i in range(count)])  10.6 us
    ppermute x7, starting transfers between devices, shift(): lax.ppermute(value, axis, [(i, (i + steps) % count) for i in range(count)])  9.66 us
  transfers between devices with their start and end apart: 17, of which 8 were waited for; matrix products, arithmetic and copies ran while one was open for 2% of the time, Pallas kernels for 16%

profile of v3, /device:TPU:64, one launch (start us, length us, event | category | flops | bytes accessed | tf_op | source)
XLA Modules:
  0.0 159.4 jit_solution(986300687689357260)
XLA Ops:
  1.5 1.5 fusion.4
  4.2 8.1 %all-to-all-start = ((bf16[8,320,128]{2,1,0:T(8,128)(2,1)}), bf16[8,320,128]{2,1,0:T(8,128)(2,1)S(1)}, u32[]{:S(2)}, u32[]{:S(2)}) async-start(bf16[8,320,128]{2,1,0:T(8,128)(2,1)} %pad_maximum_fusion), calls=%async_computation | async-start | bytes 1310720 | tf_op jit(solution)/shard_map/all_to_all | solution.py:282
  12.3 1.3 collective-permute-start.2
  13.6 1.3 collective-permute-start.3
  14.9 14.3 %all-to-all-done.mine = bf16[8,320,128]{2,1,0:T(8,128)(2,1)S(1)} async-done(((bf16[8,320,128]{2,1,0:T(8,128)(2,1)}), bf16[8,320,128]{2,1,0:T(8,128)(2,1)S(1)}, u32[]{:S(2)}, u32[]{:S(2)}) %all-to-all-start) | async-done | bytes 655392 | tf_op jit(solution)/shard_map/all_to_all | solution.py:282
  29.4 1.9 %collective-permute-done.other = bf16[8,320,128]{2,1,0:T(8,128)(2,1)S(1)} collective-permute-done((bf16[8,320,128]{2,1,0:T(8,128)(2,1)S(1)}, bf16[8,320,128]{2,1,0:T(8,128)(2,1)S(1)}, u32[]{:S(2)}, u32[]{:S(2)}) %collective-permute-start) | collective-permute-done | bytes 655392 | tf_op jit(solution)/shard_map/ppermute | solution.py:296
  31.3 1.7 %collective-permute-start.1 = (f32[64,128]{1,0:T(8,128)S(1)}, f32[64,128]{1,0:T(8,128)S(1)}, u32[]{:S(2)}, u32[]{:S(2)}) collective-permute-start(f32[64,128]{1,0:T(8,128)S(1)} %add.25), channel_id=1, source_target_pairs={{0,128},{128,0},{1,129},{129,1},{2,130},{130,2},{3,131},{131,3},{4... | collective-permute-start | bytes 98312 | tf_op jit(solution)/shard_map/ppermute | solution.py:296
  34.0 1.3 collective-permute-done.1
  36.0 6.7 %all-to-all-start.1 = ((bf16[8,64,128]{2,1,0:T(8,128)(2,1)}), bf16[8,64,128]{2,1,0:T(8,128)(2,1)S(1)}, u32[]{:S(2)}, u32[]{:S(2)}) async-start(bf16[8,64,128]{2,1,0:T(8,128)(2,1)} %broadcast_in_dim.14), calls=%async_computation.1 | async-start | bytes 262144 | tf_op jit(solution)/shard_map/all_to_all | solution.py:282
  42.8 3.9 %shard_map.120 = f32[3,1024]{1,0:T(4,128)S(1)} custom-call(s32[3]{0:T(128)S(1)} %pad_add_fusion.pos, bf16[1024,128]{1,0:T(8,128)(2,1)S(1)} %bitcast.70, bf16[1024,128]{1,0:T(8,128)(2,1)S(1)} %bitcast.73, bf16[8,320,128]{2,1,0:T(8,128)(2,1)S(1)} %all-to-all-done.mine, bf16[8,320,128]{2,1,0:T(8,128)(2,1)S(1)} %collective-permute-done.other), custom_call_target="tpu_custom_call" | custom-call | flops 1000000000 | bytes 1000000 | tf_op jit(solution)/shard_map/pallas_call | solution.py:202
  46.7 1.3 collective-permute-start.4
  48.0 2.3 %shard_map.119.state = f32[3,8,1024]{2,1,0:T(8,128)S(1)} custom-call(s32[3]{0:T(128)S(1)} %pad_add_fusion.pos, bf16[1024,128]{1,0:T(8,128)(2,1)S(1)} %bitcast.62, bf16[1024,128]{1,0:T(8,128)(2,1)S(1)} %bitcast.66, bf16[8,320,128]{2,1,0:T(8,128)(2,1)S(1)} %all-to-all-done.mine, bf16[8,320,128]{2,1,0:T(8,128)(2,1)S(1)} %collective-permute-done.other), custom_call_target="tpu_custom_call" | custom-call | flops 1000000000 | bytes 1000000 | tf_op jit(solution)/shard_map/pallas_call | solution.py:202
  50.3 2.1 %shard_map.121 = (bf16[2,256,128]{2,1,0:T(8,128)(2,1)S(1)}, f32[2,1024]{1,0:T(2,128)S(1)}) custom-call(s32[3]{0:T(128)S(1)} %pad_add_fusion.pos, bf16[1024,128]{1,0:T(8,128)(2,1)S(1)} %bitcast.63, bf16[1024,128]{1,0:T(8,128)(2,1)S(1)} %bitcast.67, bf16[2,256,128]{2,1,0:T(8,128)(2,1)S(1)} %bitcast.76, f32[3,8,1024]{2,1,0:T(8,128)S(1)} %shard_map.119.state, ...), custom_call_target="tpu_custom_call" | custom-call | flops 300000000 | bytes 1000000 | tf_op jit(solution)/shard_map/pallas_call | solution.py:202
  52.4 16.0 %all_to_all.35 = bf16[32,16,128]{2,1,0:T(8,128)(2,1)S(1)} all-to-all(bf16[32,16,128]{2,1,0:T(8,128)(2,1)S(1)} %bitcast.78), channel_id=1, replica_groups=mesh['y'=2,'z'=8,'c'=2,'x'=4,'w'=2] {'y','z','c'}, dimensions={0} | all-to-all | bytes 262144 | tf_op jit(solution)/shard_map/all_to_all | solution.py:282
  68.5 13.4 %all_to_all.36 = bf16[32,16,128]{2,1,0:T(8,128)(2,1)S(1)} all-to-all(bf16[32,16,128]{2,1,0:T(8,128)(2,1)S(1)} %broadcast_in_dim.15), channel_id=1, replica_groups=mesh['y'=2,'z'=8,'c'=2,'x'=4,'w'=2] {'y','z','c'}, dimensions={0} | all-to-all | bytes 262144 | tf_op jit(solution)/shard_map/all_to_all | solution.py:282
  82.8 6.9 %all-to-all-start.4 = ((f32[8,32,256]{2,1,0:T(8,128)}), f32[8,32,256]{2,1,0:T(8,128)S(1)}, u32[]{:S(2)}, u32[]{:S(2)}) async-start(f32[8,32,256]{2,1,0:T(8,128)} %convolution_bitcast_fusion), calls=%async_computation.4 | async-start | bytes 524288 | tf_op jit(solution)/shard_map/all_to_all | solution.py:282
  89.7 8.8 %all-to-all-done.4.parts = f32[8,32,256]{2,1,0:T(8,128)S(1)} async-done(((f32[8,32,256]{2,1,0:T(8,128)}), f32[8,32,256]{2,1,0:T(8,128)S(1)}, u32[]{:S(2)}, u32[]{:S(2)}) %all-to-all-start.4) | async-done | bytes 262176 | tf_op jit(solution)/shard_map/all_to_all | solution.py:282
  99.5 6.0 %all-to-all-start.5 = ((bf16[32,8,128]{2,1,0:T(8,128)(2,1)}), bf16[32,8,128]{2,1,0:T(8,128)(2,1)S(1)}, u32[]{:S(2)}, u32[]{:S(2)}) async-start(bf16[32,8,128]{2,1,0:T(8,128)(2,1)} %get-tuple-element.16), calls=%async_computation.5 | async-start | bytes 131072 | tf_op jit(solution)/shard_map/all_to_all | solution.py:282
  105.6 1.3 collective-permute-start.5
  106.9 5.7 %all-to-all-done.5 = bf16[32,8,128]{2,1,0:T(8,128)(2,1)S(1)} async-done(((bf16[32,8,128]{2,1,0:T(8,128)(2,1)}), bf16[32,8,128]{2,1,0:T(8,128)(2,1)S(1)}, u32[]{:S(2)}, u32[]{:S(2)}) %all-to-all-start.5) | async-done | bytes 65568 | tf_op jit(solution)/shard_map/all_to_all | solution.py:282
  113.4 7.2 %all-to-all-start.6 = ((bf16[128,8,128]{2,1,0:T(8,128)(2,1)}), bf16[128,8,128]{2,1,0:T(8,128)(2,1)S(1)}, u32[]{:S(2)}, u32[]{:S(2)}) async-start(bf16[128,8,128]{2,1,0:T(8,128)(2,1)} %broadcast_in_dim.16), calls=%async_computation.6 | async-start | bytes 524288 | tf_op jit(solution)/shard_map/all_to_all | solution.py:282
  120.6 1.1 copy-done.4
  121.7 5.4 %shard_map.122.refs_0_ = bf16[128,1024]{1,0:T(8,128)(2,1)S(1)} custom-call(s32[3]{0:T(128)S(1)} %pad_add_fusion.pos, bf16[1024,128]{1,0:T(8,128)(2,1)S(1)} %bitcast.64, bf16[1024,128]{1,0:T(8,128)(2,1)S(1)} %bitcast.68, f32[2,1024]{1,0:T(2,128)S(1)} %get-tuple-element.11.stats, bf16[8,320,128]{2,1,0:T(8,128)(2,1)S(1)} %all-to-all-done.mine, ...), custom_call_target="tpu_custom_call" | custom-call | flops 1000000000 | bytes 1000000 | tf_op jit(solution)/shard_map/pallas_call | solution.py:202
  127.1 4.7 %shard_map.124.refs_0_ = bf16[128,1024]{1,0:T(8,128)(2,1)S(1)} custom-call(s32[3]{0:T(128)S(1)} %pad_add_fusion.pos, bf16[1024,128]{1,0:T(8,128)(2,1)S(1)} %bitcast.71, bf16[1024,128]{1,0:T(8,128)(2,1)S(1)} %bitcast.74, f32[2,1024]{1,0:T(2,128)S(1)} %collective-permute-done.5.stats, bf16[8,320,128]{2,1,0:T(8,128)(2,1)S(1)} %all-to-all-done.mine, ...), custom_call_target="tpu_custom_call" | custom-call | flops 1000000000 | bytes 1000000 | tf_op jit(solution)/shard_map/pallas_call | solution.py:202
  131.8 4.7 %shard_map.125 = bf16[128,1024]{1,0:T(8,128)(2,1)S(1)} custom-call(s32[3]{0:T(128)S(1)} %pad_add_fusion.pos, bf16[1024,128]{1,0:T(8,128)(2,1)S(1)} %bitcast.72, bf16[1024,128]{1,0:T(8,128)(2,1)S(1)} %bitcast.75, f32[2,1024]{1,0:T(2,128)S(1)} %collective-permute-done.5.stats, bf16[8,320,128]{2,1,0:T(8,128)(2,1)S(1)} %all-to-all-done.mine, ...), custom_call_target="tpu_custom_call" | custom-call | flops 1000000000 | bytes 1000000 | tf_op jit(solution)/shard_map/pallas_call | solution.py:202
  136.5 1.3 collective-permute-start.6
  137.8 1.1 shard_map.123
  138.9 3.2 %collective-permute-start.7 = (bf16[32,256]{1,0:T(8,128)(2,1)S(1)}, bf16[32,256]{1,0:T(8,128)(2,1)S(1)}, u32[]{:S(2)}, u32[]{:S(2)}) collective-permute-start(bf16[32,256]{1,0:T(8,128)(2,1)S(1)} %get-tuple-element.13), channel_id=1, source_target_pairs={{0,1},{1,0},{2,3},{3,2},{4,5},{5,4},{6,7},{7,6},{8,9},{9,8},{10,11... | collective-permute-start | bytes 49160 | tf_op jit(solution)/shard_map/ppermute | solution.py:296
  142.1 4.9 %collective-permute-done.7 = bf16[32,256]{1,0:T(8,128)(2,1)S(1)} collective-permute-done((bf16[32,256]{1,0:T(8,128)(2,1)S(1)}, bf16[32,256]{1,0:T(8,128)(2,1)S(1)}, u32[]{:S(2)}, u32[]{:S(2)}) %collective-permute-start.7) | collective-permute-done | bytes 16416 | tf_op jit(solution)/shard_map/ppermute | solution.py:296
  147.1 3.3 %collective-permute-start.10 = (bf16[64,256]{1,0:T(8,128)(2,1)S(1)}, bf16[64,256]{1,0:T(8,128)(2,1)S(1)}, u32[]{:S(2)}, u32[]{:S(2)}) collective-permute-start(bf16[64,256]{1,0:T(8,128)(2,1)S(1)} %constant_dynamic-update-slice_fusion.refs_0_), channel_id=1, source_target_pairs={{0,6},{2,0},{4,2},{6,4},{1,7},{3,1},{5,3},{7,5},{8,14},{10,8},{12,... | collective-permute-start | bytes 98312 | tf_op jit(solution)/shard_map/ppermute | solution.py:296
  153.7 2.1 %collective-permute-done.9.refs_2_ = bf16[64,256]{1,0:T(8,128)(2,1)S(1)} collective-permute-done((bf16[64,256]{1,0:T(8,128)(2,1)S(1)}, bf16[64,256]{1,0:T(8,128)(2,1)S(1)}, u32[]{:S(2)}, u32[]{:S(2)}) %collective-permute-start.9) | collective-permute-done | bytes 32800 | tf_op jit(solution)/shard_map/ppermute | solution.py:296
  156.1 1.9 %shard_map.128 = (f32[1024,256]{1,0:T(8,128)}, f32[256]{0:T(256)}) custom-call(s32[2]{0:T(128)S(1)} %pad_add_fusion.1.place, bf16[256,1024]{1,0:T(8,128)(2,1)S(1)} %copy-done.2, bf16[64,256]{1,0:T(8,128)(2,1)S(1)} %constant_dynamic-update-slice_fusion.refs_0_, bf16[64,256]{1,0:T(8,128)(2,1)S(1)} %collective-permute-done.8.refs_1_, ...), custom_call_target="tpu_custom_call" | custom-call | flops 200000000 | bytes 1000000 | tf_op jit(solution)/shard_map/pallas_call | solution.py:202
  (57 shorter events, 11.8 us)
Async XLA Ops:
  0.6 2.3 %copy-start = (bf16[256,2,128]{2,1,0:T(2,128)(2,1)S(1)}, bf16[256,2,128]{2,1,0:T(2,128)(2,1)}, u32[]{:S(2)}) copy-start(bf16[256,2,128]{2,1,0:T(2,128)(2,1)} %param.11) | copy-start | bytes 393220
  3.3 9.0 %copy-start.5 = (bf16[128,1024]{1,0:T(8,128)(2,1)S(1)}, bf16[128,1024]{1,0:T(8,128)(2,1)}, u32[]{:S(2)}) copy-start(bf16[128,1024]{1,0:T(8,128)(2,1)} %param.12) | copy-start | bytes 786436
  3.3 10.3 %copy-start.6 = (bf16[128,1024]{1,0:T(8,128)(2,1)S(1)}, bf16[128,1024]{1,0:T(8,128)(2,1)}, u32[]{:S(2)}) copy-start(bf16[128,1024]{1,0:T(8,128)(2,1)} %param.15) | copy-start | bytes 786436
  4.2 25.0 %all-to-all-start = ((bf16[8,320,128]{2,1,0:T(8,128)(2,1)}), bf16[8,320,128]{2,1,0:T(8,128)(2,1)S(1)}, u32[]{:S(2)}, u32[]{:S(2)}) async-start(bf16[8,320,128]{2,1,0:T(8,128)(2,1)} %pad_maximum_fusion), calls=%async_computation | async-start | bytes 1310720 | tf_op jit(solution)/shard_map/all_to_all | solution.py:282
  12.3 20.7 %collective-permute-start.2 = (bf16[128,1024]{1,0:T(8,128)(2,1)S(1)}, bf16[128,1024]{1,0:T(8,128)(2,1)}, u32[]{:S(2)}, u32[]{:S(2)}) collective-permute-start(bf16[128,1024]{1,0:T(8,128)(2,1)S(1)} %copy-done.5), channel_id=1, source_target_pairs={{128,0},{129,1},{130,2},{131,3},{132,4},{133,5},{134,6},{135,7},{1... | collective-permute-start | bytes 786440 | tf_op jit(solution)/shard_map/ppermute | solution.py:327
  13.6 29.1 %collective-permute-start.3 = (bf16[128,1024]{1,0:T(8,128)(2,1)S(1)}, bf16[128,1024]{1,0:T(8,128)(2,1)S(1)}, u32[]{:S(2)}, u32[]{:S(2)}) collective-permute-start(bf16[128,1024]{1,0:T(8,128)(2,1)S(1)} %copy-done.6), channel_id=1, source_target_pairs={{128,0},{129,1},{130,2},{131,3},{132,4},{133,5},{134,6},{135,7},{1... | collective-permute-start | bytes 786440 | tf_op jit(solution)/shard_map/ppermute | solution.py:328
  29.2 2.1 %collective-permute-start = (bf16[8,320,128]{2,1,0:T(8,128)(2,1)S(1)}, bf16[8,320,128]{2,1,0:T(8,128)(2,1)S(1)}, u32[]{:S(2)}, u32[]{:S(2)}) collective-permute-start(bf16[8,320,128]{2,1,0:T(8,128)(2,1)S(1)} %all-to-all-done.mine), channel_id=1, source_target_pairs={{0,8},{8,0},{1,9},{9,1},{2,10},{10,2},{3,11},{11,3},{4,12},{12,4},... | collective-permute-start | bytes 1966088 | tf_op jit(solution)/shard_map/ppermute | solution.py:296
  31.3 16.7 %copy-start.3 = (bf16[8,320,128]{2,1,0:T(8,128)(2,1)}, bf16[8,320,128]{2,1,0:T(8,128)(2,1)S(1)}, u32[]{:S(2)}) copy-start(bf16[8,320,128]{2,1,0:T(8,128)(2,1)S(1)} %collective-permute-done.other) | copy-start | bytes 1966084
  31.3 4.0 %collective-permute-start.1 = (f32[64,128]{1,0:T(8,128)S(1)}, f32[64,128]{1,0:T(8,128)S(1)}, u32[]{:S(2)}, u32[]{:S(2)}) collective-permute-start(f32[64,128]{1,0:T(8,128)S(1)} %add.25), channel_id=1, source_target_pairs={{0,128},{128,0},{1,129},{129,1},{2,130},{130,2},{3,131},{131,3},{4... | collective-permute-start | bytes 98312 | tf_op jit(solution)/shard_map/ppermute | solution.py:296
  36.0 14.3 %all-to-all-start.1 = ((bf16[8,64,128]{2,1,0:T(8,128)(2,1)}), bf16[8,64,128]{2,1,0:T(8,128)(2,1)S(1)}, u32[]{:S(2)}, u32[]{:S(2)}) async-start(bf16[8,64,128]{2,1,0:T(8,128)(2,1)} %broadcast_in_dim.14), calls=%async_computation.1 | async-start | bytes 262144 | tf_op jit(solution)/shard_map/all_to_all | solution.py:282
  46.7 3.6 %collective-permute-start.4 = (f32[3,1024]{1,0:T(4,128)S(1)}, f32[3,1024]{1,0:T(4,128)S(1)}, u32[]{:S(2)}, u32[]{:S(2)}) collective-permute-start(f32[3,1024]{1,0:T(4,128)S(1)} %shard_map.120), channel_id=1, source_target_pairs={{0,128},{1,129},{2,130},{3,131},{4,132},{5,133},{6,134},{7,135},{8... | collective-permute-start | bytes 36872 | tf_op jit(solution)/shard_map/ppermute | solution.py:337
  52.4 46.1 %copy-start.1 = (bf16[1024,256]{1,0:T(8,128)(2,1)S(1)}, bf16[1024,256]{1,0:T(8,128)(2,1)}, u32[]{:S(2)}) copy-start(bf16[1024,256]{1,0:T(8,128)(2,1)} %w_hidden.1) | copy-start | bytes 1572868
  82.8 15.7 %all-to-all-start.4 = ((f32[8,32,256]{2,1,0:T(8,128)}), f32[8,32,256]{2,1,0:T(8,128)S(1)}, u32[]{:S(2)}, u32[]{:S(2)}) async-start(f32[8,32,256]{2,1,0:T(8,128)} %convolution_bitcast_fusion), calls=%async_computation.4 | async-start | bytes 524288 | tf_op jit(solution)/shard_map/all_to_all | solution.py:282
  99.5 13.1 %all-to-all-start.5 = ((bf16[32,8,128]{2,1,0:T(8,128)(2,1)}), bf16[32,8,128]{2,1,0:T(8,128)(2,1)S(1)}, u32[]{:S(2)}, u32[]{:S(2)}) async-start(bf16[32,8,128]{2,1,0:T(8,128)(2,1)} %get-tuple-element.16), calls=%async_computation.5 | async-start | bytes 131072 | tf_op jit(solution)/shard_map/all_to_all | solution.py:282
  105.6 21.5 %collective-permute-start.5 = (f32[2,1024]{1,0:T(2,128)S(1)}, f32[2,1024]{1,0:T(2,128)S(1)}, u32[]{:S(2)}, u32[]{:S(2)}) collective-permute-start(f32[2,1024]{1,0:T(2,128)S(1)} %get-tuple-element.11.stats), channel_id=1, source_target_pairs={{128,0},{129,1},{130,2},{131,3},{132,4},{133,5},{134,6},{135,7},{1... | collective-permute-start | bytes 24584 | tf_op jit(solution)/shard_map/ppermute | solution.py:340
  113.4 38.5 %all-to-all-start.6 = ((bf16[128,8,128]{2,1,0:T(8,128)(2,1)}), bf16[128,8,128]{2,1,0:T(8,128)(2,1)S(1)}, u32[]{:S(2)}, u32[]{:S(2)}) async-start(bf16[128,8,128]{2,1,0:T(8,128)(2,1)} %broadcast_in_dim.16), calls=%async_computation.6 | async-start | bytes 524288 | tf_op jit(solution)/shard_map/all_to_all | solution.py:282
  120.6 1.1 copy-start.4
  136.5 15.4 %collective-permute-start.6 = (bf16[128,1024]{1,0:T(8,128)(2,1)S(1)}, bf16[128,1024]{1,0:T(8,128)(2,1)S(1)}, u32[]{:S(2)}, u32[]{:S(2)}) collective-permute-start(bf16[128,1024]{1,0:T(8,128)(2,1)S(1)} %shard_map.125), channel_id=1, source_target_pairs={{0,128},{1,129},{2,130},{3,131},{4,132},{5,133},{6,134},{7,135},{8... | collective-permute-start | bytes 786440 | tf_op jit(solution)/shard_map/ppermute | solution.py:348
  138.9 8.1 %collective-permute-start.7 = (bf16[32,256]{1,0:T(8,128)(2,1)S(1)}, bf16[32,256]{1,0:T(8,128)(2,1)S(1)}, u32[]{:S(2)}, u32[]{:S(2)}) collective-permute-start(bf16[32,256]{1,0:T(8,128)(2,1)S(1)} %get-tuple-element.13), channel_id=1, source_target_pairs={{0,1},{1,0},{2,3},{3,2},{4,5},{5,4},{6,7},{7,6},{8,9},{9,8},{10,11... | collective-permute-start | bytes 49160 | tf_op jit(solution)/shard_map/ppermute | solution.py:296
  147.1 6.7 %collective-permute-start.10 = (bf16[64,256]{1,0:T(8,128)(2,1)S(1)}, bf16[64,256]{1,0:T(8,128)(2,1)S(1)}, u32[]{:S(2)}, u32[]{:S(2)}) collective-permute-start(bf16[64,256]{1,0:T(8,128)(2,1)S(1)} %constant_dynamic-update-slice_fusion.refs_0_), channel_id=1, source_target_pairs={{0,6},{2,0},{4,2},{6,4},{1,7},{3,1},{5,3},{7,5},{8,14},{10,8},{12,... | collective-permute-start | bytes 98312 | tf_op jit(solution)/shard_map/ppermute | solution.py:296
  150.4 5.4 %collective-permute-start.9 = (bf16[64,256]{1,0:T(8,128)(2,1)S(1)}, bf16[64,256]{1,0:T(8,128)(2,1)S(1)}, u32[]{:S(2)}, u32[]{:S(2)}) collective-permute-start(bf16[64,256]{1,0:T(8,128)(2,1)S(1)} %constant_dynamic-update-slice_fusion.refs_0_), channel_id=1, source_target_pairs={{0,4},{2,6},{4,0},{6,2},{1,5},{3,7},{5,1},{7,3},{8,12},{10,14},{12... | collective-permute-start | bytes 98312 | tf_op jit(solution)/shard_map/ppermute | solution.py:296
  150.8 5.3 %collective-permute-start.8 = (bf16[64,256]{1,0:T(8,128)(2,1)S(1)}, bf16[64,256]{1,0:T(8,128)(2,1)S(1)}, u32[]{:S(2)}, u32[]{:S(2)}) collective-permute-start(bf16[64,256]{1,0:T(8,128)(2,1)S(1)} %constant_dynamic-update-slice_fusion.refs_0_), channel_id=1, source_target_pairs={{0,2},{2,4},{4,6},{6,0},{1,3},{3,5},{5,7},{7,1},{8,10},{10,12},{12... | collective-permute-start | bytes 98312 | tf_op jit(solution)/shard_map/ppermute | solution.py:296
  151.9 6.1 %collective-permute-start.11 = (bf16[128,8,128]{2,1,0:T(8,128)(2,1)S(1)}, bf16[128,8,128]{2,1,0:T(8,128)(2,1)S(1)}, u32[]{:S(2)}, u32[]{:S(2)}) collective-permute-start(bf16[128,8,128]{2,1,0:T(8,128)(2,1)S(1)} %all-to-all-done.6), channel_id=1, source_target_pairs={{0,8},{8,0},{1,9},{9,1},{2,10},{10,2},{3,11},{11,3},{4,12},{12,4},... | collective-permute-start | bytes 786440 | tf_op jit(solution)/shard_map/ppermute | solution.py:296
  152.7 3.5 %copy-start.2 = (bf16[256,1024]{1,0:T(8,128)(2,1)S(1)}, bf16[256,1024]{1,0:T(8,128)(2,1)}, u32[]{:S(2)}) copy-start(bf16[256,1024]{1,0:T(8,128)(2,1)} %embed.1) | copy-start | bytes 1572868

commit v4 on v3

--- a/solution.py
+++ b/solution.py
@@ -15,7 +15,9 @@
 NEG = -1e30
 TILE = 256
 PIECES = 2
+TALL = 8
 SEQ = ("y", "z", "c")
+YZ = ("y", "z")
 CYZ = ("c", "y", "z")
 HEAD = ("x", "w")
 OWNERS = ("x", "w", "y", "z")
@@ -111,8 +113,9 @@
             out[a : a + 1, span(r)] = value
 
 
-def prefix_kernel(pos, q, g, pkv, state, lent, grads, stats):
+def prefix_kernel(pos, q, g, halves, state, lent, grads, stats, pkv):
     npre = pkv.shape[1]
+    pkv[...] = (halves[0].astype(F32) + halves[1].astype(F32)).astype(BF16)
     kg = jnp.zeros((npre, HD), F32)
     vg = jnp.zeros((npre, HD), F32)
     late = pos[2] == 1
@@ -219,9 +222,10 @@
     return call(lent_sweep_kernel, out, 10**9, pos, q, g, mine, other)
 
 
-def prefix_part(pos, q, g, pkv, state, lent):
-    out = (jax.ShapeDtypeStruct(pkv.shape, BF16), jax.ShapeDtypeStruct((2, q.shape[0]), F32))
-    return call(prefix_kernel, out, 3 * 10**8, pos, q, g, pkv, state, lent)
+def prefix_part(pos, q, g, halves, state, lent):
+    pair = jax.ShapeDtypeStruct(halves.shape[1:], BF16)
+    out = (pair, jax.ShapeDtypeStruct((2, q.shape[0]), F32), pair)
+    return call(prefix_kernel, out, 3 * 10**8, pos, q, g, halves, state, lent)
 
 
 def query_grad_piece(lent, piece, pos, q, g, stats, mine, other, *extra):
@@ -234,17 +238,38 @@
 def embed_kernel(parts, factor, w_hidden, pre, embed):
     pre[...] = (jnp.sum(parts[...], axis=0) * factor[...]).astype(BF16)
     rows = dot_nt(pre[...], w_hidden[...])
-    for k in range(embed.shape[1]):
-        embed[:, k, :] = rows[:, k * HD : (k + 1) * HD].astype(BF16)
+    tall = embed.shape[1]
+    wide = rows.shape[1] // HD
+    for t in range(embed.shape[0]):
+        down, right = t // wide * tall, t % wide * HD
+        embed[t] = rows[down : down + tall, right : right + HD].astype(BF16)
 
 
 def embed_rows(parts, factor, w_hidden):
     share = factor.shape[0]
     out = (
         jax.ShapeDtypeStruct(factor.shape, BF16),
-        jax.ShapeDtypeStruct((share, w_hidden.shape[0] // HD, HD), BF16),
+        jax.ShapeDtypeStruct((share * w_hidden.shape[0] // HD // TALL, TALL, HD), BF16),
     )
     return call(embed_kernel, out, 2 * 10**7, parts, factor, w_hidden)
+
+
+def joined_kernel(heads, pos, near, far, out):
+    wide = out.shape[1] // HD
+    per_head = near.shape[0] // heads
+    first = pos[1] == 0
+    for t in range(near.shape[0]):
+        pair = (near[t].astype(F32), far[t].astype(F32))
+        for side in range(2):
+            tile = t // per_head * 2 * per_head + side * per_head + t % per_head
+            down, right = tile // wide * TALL, tile % wide * HD
+            value = jnp.where(first, pair[side], pair[1 - side])
+            out[down : down + TALL, right : right + HD] = value
+
+
+def joined(pos, near, far, heads, npre, emb):
+    out = jax.ShapeDtypeStruct((npre, emb), F32)
+    return call(functools.partial(joined_kernel, heads), out, 10**6, pos, near, far)
 
 
 def w_hidden_kernel(place, embed, *refs):
@@ -330,13 +355,12 @@
     lent_g = by_head(lent_g)
     other = shift(mine, "c", 1)
     sides = [jnp.sum(v[:, kv.shape[0] :].astype(F32), axis=0) for v in (mine, other)]
-    own = sides[0] + sides[1]
-    own = (own + shift(own, "y", 1)).astype(BF16)
-    pkv = to_all(own, "z").reshape(2, npre, HD)
+    own = (sides[0] + sides[1]).astype(BF16)
+    halves = to_all(own, YZ).reshape(lax.axis_size("y"), 2, npre, HD)
     lent_state = lent_sweep(pos, lent_q, lent_g, mine, other)
     lent_state = lax.ppermute(lent_state, "y", [(0, 1)])
     state = sweep(pos, q, g, mine, other)
-    grads, stats = prefix_part(pos, q, g, pkv, state, lent_state)
+    grads, stats, pkv = prefix_part(pos, q, g, halves, state, lent_state)
     lent_stats = lax.ppermute(stats, "y", [(1, 0)])
     prefix_share = sum_parts(grads, SEQ).astype(BF16)
     prefix_grads = to_all(prefix_share, SEQ).reshape(2, npre, HD)
@@ -357,9 +381,7 @@
     own_embed = jnp.sum(exchange(embed_part, CYZ).astype(F32), axis=0).astype(BF16)
     near = to_all(own_embed, OWNERS)
     far = shift(near, "c", 1)
-    sides = jnp.stack([jnp.where(core == 0, near, far), jnp.where(core == 0, far, near)], 0)
-    sides = sides.reshape(2, heads, -1, emb).transpose(1, 0, 2, 3)
-    grad_prefix = sides.reshape(npre, emb).astype(F32)
+    grad_prefix = joined(pos, near, far, heads, npre, emb)
     both = jnp.concatenate([pre_part, shift(pre_part, "w", 1)], 0)
     turns = [shift(both, "x", k) for k in range(1, lax.axis_size("x"))]
     place = jnp.stack([lax.axis_index("x"), lax.axis_index("w")]).astype(jnp.int32)

time: 160 us -> 158 us (0.988)
  starting transfers between devices: 51 us -> 49.4 us
    ppermute x7 -> x6, starting transfers between devices: 9.66 us -> 8 us  [shift(): lax.ppermute(value, axis, [(i, (i + steps) % count) for i in range(count)])]
    pallas_call x10 -> x11, Pallas kernels: 28.1 us -> 29.6 us  [call(): pl.pallas_call(kernel, out_shape=out_shape, in_specs=[SMEM if v.dtype ==...]
    ppermute x7 -> x6, waiting for transfers between devices: 10.6 us -> 9.26 us  [shift(): lax.ppermute(value, axis, [(i, (i + steps) % count) for i in range(count)])]
  transfers between devices with their start and end apart: 17 -> 16, of which waited for: 8 -> 8; matrix products, arithmetic and copies ran while one was open for 2% -> 3% of each run, Pallas kernels for 16% -> 16%
where the time goes in v4:
time: 158 us; the launch traced here: 157 us
  starting transfers between devices  49.4 us (31%)
  waiting for transfers between devices  38.5 us (24%)
  Pallas kernels  29.6 us (19%)
  blocking collectives  28.3 us (18%)
  local copies, waits for them, and re-layouts  3.96 us (3%)
  other arithmetic  3.51 us (2%)
  matrix products  3.32 us (2%)
    all_to_all x5, starting transfers between devices, exchange(): return lax.all_to_all(value, axes, 0, 0, tiled=True)  34.9 us
    pallas_call x11, Pallas kernels, call(): pl.pallas_call(kernel, out_shape=out_shape, in_specs=[SMEM if v.dtype ==...  29.6 us
    all_to_all x5, waiting for transfers between devices, exchange(): return lax.all_to_all(value, axes, 0, 0, tiled=True)  29.2 us
    all_to_all x2, blocking collectives, exchange(): return lax.all_to_all(value, axes, 0, 0, tiled=True)  28.3 us
    ppermute x6, waiting for transfers between devices, shift(): lax.ppermute(value, axis, [(i, (i + steps) % count) for i in range(count)])  9.26 us
    ppermute x6, starting transfers between devices, shift(): lax.ppermute(value, axis, [(i, (i + steps) % count) for i in range(count)])  8 us
  transfers between devices with their start and end apart: 16, of which 8 were waited for; matrix products, arithmetic and copies ran while one was open for 3% of the time, Pallas kernels for 16%

profile of v4, /device:TPU:64, one launch (start us, length us, event | category | flops | bytes accessed | tf_op | source)
XLA Modules:
  0.0 157.5 jit_solution(4009946635996110027)
XLA Ops:
  1.5 2.2 %fusion.4 = (bf16[256,256]{1,0:T(8,128)(2,1)S(1)}, f32[256,256]{1,0:T(8,128)}) fusion(f32[256]{0:T(256)} %param.10, bf16[256,1024]{1,0:T(8,128)(2,1)} %embed.1, bf16[1024,256]{1,0:T(8,128)(2,1)} %w_hidden.1), kind=kOutput, calls=%fused_computation.22 | convolution fusion | flops 134348800 | bytes 1442816 | tf_op jit(solution)/shard_map/dot_general | solution.py:338
  4.9 8.1 %all-to-all-start = ((bf16[8,320,128]{2,1,0:T(8,128)(2,1)}), bf16[8,320,128]{2,1,0:T(8,128)(2,1)S(1)}, u32[]{:S(2)}, u32[]{:S(2)}) async-start(bf16[8,320,128]{2,1,0:T(8,128)(2,1)} %pad_maximum_fusion), calls=%async_computation | async-start | bytes 1310720 | tf_op jit(solution)/shard_map/all_to_all | solution.py:307
  13.0 1.3 collective-permute-start.1
  14.3 1.3 collective-permute-start.2
  15.6 14.3 %all-to-all-done.mine = bf16[8,320,128]{2,1,0:T(8,128)(2,1)S(1)} async-done(((bf16[8,320,128]{2,1,0:T(8,128)(2,1)}), bf16[8,320,128]{2,1,0:T(8,128)(2,1)S(1)}, u32[]{:S(2)}, u32[]{:S(2)}) %all-to-all-start) | async-done | bytes 655392 | tf_op jit(solution)/shard_map/all_to_all | solution.py:307
  30.1 1.9 %collective-permute-done.other = bf16[8,320,128]{2,1,0:T(8,128)(2,1)S(1)} collective-permute-done((bf16[8,320,128]{2,1,0:T(8,128)(2,1)S(1)}, bf16[8,320,128]{2,1,0:T(8,128)(2,1)S(1)}, u32[]{:S(2)}, u32[]{:S(2)}) %collective-permute-start) | collective-permute-done | bytes 655392 | tf_op jit(solution)/shard_map/ppermute | solution.py:321
  32.9 6.7 %all-to-all-start.1 = ((bf16[16,64,128]{2,1,0:T(8,128)(2,1)}), bf16[16,64,128]{2,1,0:T(8,128)(2,1)S(1)}, u32[]{:S(2)}, u32[]{:S(2)}) async-start(bf16[16,64,128]{2,1,0:T(8,128)(2,1)} %broadcast_in_dim.14), calls=%async_computation.1 | async-start | bytes 524288 | tf_op jit(solution)/shard_map/all_to_all | solution.py:307
  40.7 3.9 %shard_map.120 = f32[3,1024]{1,0:T(4,128)S(1)} custom-call(s32[3]{0:T(128)S(1)} %pad_add_fusion.pos, bf16[1024,128]{1,0:T(8,128)(2,1)S(1)} %bitcast.67, bf16[1024,128]{1,0:T(8,128)(2,1)S(1)} %bitcast.70, bf16[8,320,128]{2,1,0:T(8,128)(2,1)S(1)} %all-to-all-done.mine, bf16[8,320,128]{2,1,0:T(8,128)(2,1)S(1)} %collective-permute-done.other), custom_call_target="tpu_custom_call" | custom-call | flops 1000000000 | bytes 1000000 | tf_op jit(solution)/shard_map/pallas_call | solution.py:205
  44.6 1.3 collective-permute-start.3
  46.0 2.3 %shard_map.119.state = f32[3,8,1024]{2,1,0:T(8,128)S(1)} custom-call(s32[3]{0:T(128)S(1)} %pad_add_fusion.pos, bf16[1024,128]{1,0:T(8,128)(2,1)S(1)} %bitcast.59, bf16[1024,128]{1,0:T(8,128)(2,1)S(1)} %bitcast.63, bf16[8,320,128]{2,1,0:T(8,128)(2,1)S(1)} %all-to-all-done.mine, bf16[8,320,128]{2,1,0:T(8,128)(2,1)S(1)} %collective-permute-done.other), custom_call_target="tpu_custom_call" | custom-call | flops 1000000000 | bytes 1000000 | tf_op jit(solution)/shard_map/pallas_call | solution.py:205
  48.3 1.1 all-to-all-done.1
  49.4 2.1 %shard_map.121 = (bf16[2,256,128]{2,1,0:T(8,128)(2,1)S(1)}, f32[2,1024]{1,0:T(2,128)S(1)}, bf16[2,256,128]{2,1,0:T(8,128)(2,1)S(1)}) custom-call(s32[3]{0:T(128)S(1)} %pad_add_fusion.pos, bf16[1024,128]{1,0:T(8,128)(2,1)S(1)} %bitcast.60, bf16[1024,128]{1,0:T(8,128)(2,1)S(1)} %bitcast.64, bf16[2,2,256,128]{3,2,1,0:T(8,128)(2,1)S(1)} %bitcast.73, ...), custom_call_target="tpu_custom_call" | custom-call | flops 300000000 | bytes 1000000 | tf_op jit(solution)/shard_map/pallas_call | solution.py:205
  51.5 14.9 %all_to_all.35 = bf16[32,16,128]{2,1,0:T(8,128)(2,1)S(1)} all-to-all(bf16[32,16,128]{2,1,0:T(8,128)(2,1)S(1)} %bitcast.74), channel_id=1, replica_groups=mesh['y'=2,'z'=8,'c'=2,'x'=4,'w'=2] {'y','z','c'}, dimensions={0} | all-to-all | bytes 262144 | tf_op jit(solution)/shard_map/all_to_all | solution.py:307
  66.4 13.4 %all_to_all.36 = bf16[32,16,128]{2,1,0:T(8,128)(2,1)S(1)} all-to-all(bf16[32,16,128]{2,1,0:T(8,128)(2,1)S(1)} %broadcast_in_dim.15), channel_id=1, replica_groups=mesh['y'=2,'z'=8,'c'=2,'x'=4,'w'=2] {'y','z','c'}, dimensions={0} | all-to-all | bytes 262144 | tf_op jit(solution)/shard_map/all_to_all | solution.py:307
  80.8 6.9 %all-to-all-start.4 = ((f32[8,32,256]{2,1,0:T(8,128)}), f32[8,32,256]{2,1,0:T(8,128)S(1)}, u32[]{:S(2)}, u32[]{:S(2)}) async-start(f32[8,32,256]{2,1,0:T(8,128)} %convolution_bitcast_fusion), calls=%async_computation.4 | async-start | bytes 524288 | tf_op jit(solution)/shard_map/all_to_all | solution.py:307
  88.5 8.0 %all-to-all-done.4.parts = f32[8,32,256]{2,1,0:T(8,128)S(1)} async-done(((f32[8,32,256]{2,1,0:T(8,128)}), f32[8,32,256]{2,1,0:T(8,128)S(1)}, u32[]{:S(2)}, u32[]{:S(2)}) %all-to-all-start.4) | async-done | bytes 262176 | tf_op jit(solution)/shard_map/all_to_all | solution.py:307
  97.4 6.0 %all-to-all-start.5 = ((bf16[32,8,128]{2,1,0:T(8,128)(2,1)}), bf16[32,8,128]{2,1,0:T(8,128)(2,1)S(1)}, u32[]{:S(2)}, u32[]{:S(2)}) async-start(bf16[32,8,128]{2,1,0:T(8,128)(2,1)} %get-tuple-element.18), calls=%async_computation.5 | async-start | bytes 131072 | tf_op jit(solution)/shard_map/all_to_all | solution.py:307
  103.5 1.3 collective-permute-start.4
  104.7 5.8 %all-to-all-done.5 = bf16[32,8,128]{2,1,0:T(8,128)(2,1)S(1)} async-done(((bf16[32,8,128]{2,1,0:T(8,128)(2,1)}), bf16[32,8,128]{2,1,0:T(8,128)(2,1)S(1)}, u32[]{:S(2)}, u32[]{:S(2)}) %all-to-all-start.5) | async-done | bytes 65568 | tf_op jit(solution)/shard_map/all_to_all | solution.py:307
  111.3 7.2 %all-to-all-start.6 = ((bf16[128,8,128]{2,1,0:T(8,128)(2,1)}), bf16[128,8,128]{2,1,0:T(8,128)(2,1)S(1)}, u32[]{:S(2)}, u32[]{:S(2)}) async-start(bf16[128,8,128]{2,1,0:T(8,128)(2,1)} %broadcast_in_dim.16), calls=%async_computation.6 | async-start | bytes 524288 | tf_op jit(solution)/shard_map/all_to_all | solution.py:307
  118.5 1.1 copy-done.4
  119.6 5.4 %shard_map.122.refs_0_ = bf16[128,1024]{1,0:T(8,128)(2,1)S(1)} custom-call(s32[3]{0:T(128)S(1)} %pad_add_fusion.pos, bf16[1024,128]{1,0:T(8,128)(2,1)S(1)} %bitcast.61, bf16[1024,128]{1,0:T(8,128)(2,1)S(1)} %bitcast.65, f32[2,1024]{1,0:T(2,128)S(1)} %get-tuple-element.12.stats, bf16[8,320,128]{2,1,0:T(8,128)(2,1)S(1)} %all-to-all-done.mine, ...), custom_call_target="tpu_custom_call" | custom-call | flops 1000000000 | bytes 1000000 | tf_op jit(solution)/shard_map/pallas_call | solution.py:205
  125.0 4.7 %shard_map.124.refs_0_ = bf16[128,1024]{1,0:T(8,128)(2,1)S(1)} custom-call(s32[3]{0:T(128)S(1)} %pad_add_fusion.pos, bf16[1024,128]{1,0:T(8,128)(2,1)S(1)} %bitcast.68, bf16[1024,128]{1,0:T(8,128)(2,1)S(1)} %bitcast.71, f32[2,1024]{1,0:T(2,128)S(1)} %collective-permute-done.4.stats, bf16[8,320,128]{2,1,0:T(8,128)(2,1)S(1)} %all-to-all-done.mine, ...), custom_call_target="tpu_custom_call" | custom-call | flops 1000000000 | bytes 1000000 | tf_op jit(solution)/shard_map/pallas_call | solution.py:205
  129.7 4.7 %shard_map.125 = bf16[128,1024]{1,0:T(8,128)(2,1)S(1)} custom-call(s32[3]{0:T(128)S(1)} %pad_add_fusion.pos, bf16[1024,128]{1,0:T(8,128)(2,1)S(1)} %bitcast.69, bf16[1024,128]{1,0:T(8,128)(2,1)S(1)} %bitcast.72, f32[2,1024]{1,0:T(2,128)S(1)} %collective-permute-done.4.stats, bf16[8,320,128]{2,1,0:T(8,128)(2,1)S(1)} %all-to-all-done.mine, ...), custom_call_target="tpu_custom_call" | custom-call | flops 1000000000 | bytes 1000000 | tf_op jit(solution)/shard_map/pallas_call | solution.py:205
  134.4 1.3 collective-permute-start.5
  135.7 1.1 shard_map.123
  136.8 3.2 %collective-permute-start.6 = (bf16[32,256]{1,0:T(8,128)(2,1)S(1)}, bf16[32,256]{1,0:T(8,128)(2,1)S(1)}, u32[]{:S(2)}, u32[]{:S(2)}) collective-permute-start(bf16[32,256]{1,0:T(8,128)(2,1)S(1)} %get-tuple-element.15), channel_id=1, source_target_pairs={{0,1},{1,0},{2,3},{3,2},{4,5},{5,4},{6,7},{7,6},{8,9},{9,8},{10,11... | collective-permute-start | bytes 49160 | tf_op jit(solution)/shard_map/ppermute | solution.py:321
  140.0 4.9 %collective-permute-done.6 = bf16[32,256]{1,0:T(8,128)(2,1)S(1)} collective-permute-done((bf16[32,256]{1,0:T(8,128)(2,1)S(1)}, bf16[32,256]{1,0:T(8,128)(2,1)S(1)}, u32[]{:S(2)}, u32[]{:S(2)}) %collective-permute-start.6) | collective-permute-done | bytes 16416 | tf_op jit(solution)/shard_map/ppermute | solution.py:321
  144.9 3.3 %collective-permute-start.9 = (bf16[64,256]{1,0:T(8,128)(2,1)S(1)}, bf16[64,256]{1,0:T(8,128)(2,1)S(1)}, u32[]{:S(2)}, u32[]{:S(2)}) collective-permute-start(bf16[64,256]{1,0:T(8,128)(2,1)S(1)} %constant_dynamic-update-slice_fusion.refs_0_), channel_id=1, source_target_pairs={{0,6},{2,0},{4,2},{6,4},{1,7},{3,1},{5,3},{7,5},{8,14},{10,8},{12,... | collective-permute-start | bytes 98312 | tf_op jit(solution)/shard_map/ppermute | solution.py:321
  151.6 2.1 %collective-permute-done.8.refs_2_ = bf16[64,256]{1,0:T(8,128)(2,1)S(1)} collective-permute-done((bf16[64,256]{1,0:T(8,128)(2,1)S(1)}, bf16[64,256]{1,0:T(8,128)(2,1)S(1)}, u32[]{:S(2)}, u32[]{:S(2)}) %collective-permute-start.8) | collective-permute-done | bytes 32800 | tf_op jit(solution)/shard_map/ppermute | solution.py:321
  154.0 1.9 %shard_map.128 = (f32[1024,256]{1,0:T(8,128)}, f32[256]{0:T(256)}) custom-call(s32[2]{0:T(128)S(1)} %pad_add_fusion.1.place, bf16[256,1024]{1,0:T(8,128)(2,1)S(1)} %copy-done.2, bf16[64,256]{1,0:T(8,128)(2,1)S(1)} %constant_dynamic-update-slice_fusion.refs_0_, bf16[64,256]{1,0:T(8,128)(2,1)S(1)} %collective-permute-done.7.refs_1_, ...), custom_call_target="tpu_custom_call" | custom-call | flops 200000000 | bytes 1000000 | tf_op jit(solution)/shard_map/pallas_call | solution.py:205
  155.9 1.6 %shard_map.129 = f32[256,1024]{1,0:T(8,128)} custom-call(s32[3]{0:T(128)S(1)} %pad_add_fusion.pos, bf16[128,8,128]{2,1,0:T(8,128)(2,1)S(1)} %all-to-all-done.6.near, bf16[128,8,128]{2,1,0:T(8,128)(2,1)S(1)} %collective-permute-done.10.far), custom_call_target="tpu_custom_call" | custom-call | flops 1000000 | bytes 1000000 | tf_op jit(solution)/shard_map/pallas_call | solution.py:205
  (51 shorter events, 11.3 us)
Async XLA Ops:
  0.6 3.0 %copy-start = (bf16[256,2,128]{2,1,0:T(2,128)(2,1)S(1)}, bf16[256,2,128]{2,1,0:T(2,128)(2,1)}, u32[]{:S(2)}) copy-start(bf16[256,2,128]{2,1,0:T(2,128)(2,1)} %param.11) | copy-start | bytes 393220
  4.0 9.0 %copy-start.5 = (bf16[128,1024]{1,0:T(8,128)(2,1)S(1)}, bf16[128,1024]{1,0:T(8,128)(2,1)}, u32[]{:S(2)}) copy-start(bf16[128,1024]{1,0:T(8,128)(2,1)} %param.12) | copy-start | bytes 786436
  4.0 10.3 %copy-start.6 = (bf16[128,1024]{1,0:T(8,128)(2,1)S(1)}, bf16[128,1024]{1,0:T(8,128)(2,1)}, u32[]{:S(2)}) copy-start(bf16[128,1024]{1,0:T(8,128)(2,1)} %param.15) | copy-start | bytes 786436
  4.9 25.0 %all-to-all-start = ((bf16[8,320,128]{2,1,0:T(8,128)(2,1)}), bf16[8,320,128]{2,1,0:T(8,128)(2,1)S(1)}, u32[]{:S(2)}, u32[]{:S(2)}) async-start(bf16[8,320,128]{2,1,0:T(8,128)(2,1)} %pad_maximum_fusion), calls=%async_computation | async-start | bytes 1310720 | tf_op jit(solution)/shard_map/all_to_all | solution.py:307
  13.0 26.6 %collective-permute-start.1 = (bf16[128,1024]{1,0:T(8,128)(2,1)S(1)}, bf16[128,1024]{1,0:T(8,128)(2,1)}, u32[]{:S(2)}, u32[]{:S(2)}) collective-permute-start(bf16[128,1024]{1,0:T(8,128)(2,1)S(1)} %copy-done.5), channel_id=1, source_target_pairs={{128,0},{129,1},{130,2},{131,3},{132,4},{133,5},{134,6},{135,7},{1... | collective-permute-start | bytes 786440 | tf_op jit(solution)/shard_map/ppermute | solution.py:352
  14.3 26.4 %collective-permute-start.2 = (bf16[128,1024]{1,0:T(8,128)(2,1)S(1)}, bf16[128,1024]{1,0:T(8,128)(2,1)S(1)}, u32[]{:S(2)}, u32[]{:S(2)}) collective-permute-start(bf16[128,1024]{1,0:T(8,128)(2,1)S(1)} %copy-done.6), channel_id=1, source_target_pairs={{128,0},{129,1},{130,2},{131,3},{132,4},{133,5},{134,6},{135,7},{1... | collective-permute-start | bytes 786440 | tf_op jit(solution)/shard_map/ppermute | solution.py:353
  29.9 2.1 %collective-permute-start = (bf16[8,320,128]{2,1,0:T(8,128)(2,1)S(1)}, bf16[8,320,128]{2,1,0:T(8,128)(2,1)S(1)}, u32[]{:S(2)}, u32[]{:S(2)}) collective-permute-start(bf16[8,320,128]{2,1,0:T(8,128)(2,1)S(1)} %all-to-all-done.mine), channel_id=1, source_target_pairs={{0,8},{8,0},{1,9},{9,1},{2,10},{10,2},{3,11},{11,3},{4,12},{12,4},... | collective-permute-start | bytes 1966088 | tf_op jit(solution)/shard_map/ppermute | solution.py:321
  32.0 14.0 %copy-start.3 = (bf16[8,320,128]{2,1,0:T(8,128)(2,1)}, bf16[8,320,128]{2,1,0:T(8,128)(2,1)S(1)}, u32[]{:S(2)}) copy-start(bf16[8,320,128]{2,1,0:T(8,128)(2,1)S(1)} %collective-permute-done.other) | copy-start | bytes 1966084
  32.9 16.5 %all-to-all-start.1 = ((bf16[16,64,128]{2,1,0:T(8,128)(2,1)}), bf16[16,64,128]{2,1,0:T(8,128)(2,1)S(1)}, u32[]{:S(2)}, u32[]{:S(2)}) async-start(bf16[16,64,128]{2,1,0:T(8,128)(2,1)} %broadcast_in_dim.14), calls=%async_computation.1 | async-start | bytes 524288 | tf_op jit(solution)/shard_map/all_to_all | solution.py:307
  44.6 3.6 %collective-permute-start.3 = (f32[3,1024]{1,0:T(4,128)S(1)}, f32[3,1024]{1,0:T(4,128)S(1)}, u32[]{:S(2)}, u32[]{:S(2)}) collective-permute-start(f32[3,1024]{1,0:T(4,128)S(1)} %shard_map.120), channel_id=1, source_target_pairs={{0,128},{1,129},{2,130},{3,131},{4,132},{5,133},{6,134},{7,135},{8... | collective-permute-start | bytes 36872 | tf_op jit(solution)/shard_map/ppermute | solution.py:361
  51.5 45.0 %copy-start.1 = (bf16[1024,256]{1,0:T(8,128)(2,1)S(1)}, bf16[1024,256]{1,0:T(8,128)(2,1)}, u32[]{:S(2)}) copy-start(bf16[1024,256]{1,0:T(8,128)(2,1)} %w_hidden.1) | copy-start | bytes 1572868
  80.8 15.7 %all-to-all-start.4 = ((f32[8,32,256]{2,1,0:T(8,128)}), f32[8,32,256]{2,1,0:T(8,128)S(1)}, u32[]{:S(2)}, u32[]{:S(2)}) async-start(f32[8,32,256]{2,1,0:T(8,128)} %convolution_bitcast_fusion), calls=%async_computation.4 | async-start | bytes 524288 | tf_op jit(solution)/shard_map/all_to_all | solution.py:307
  97.4 13.1 %all-to-all-start.5 = ((bf16[32,8,128]{2,1,0:T(8,128)(2,1)}), bf16[32,8,128]{2,1,0:T(8,128)(2,1)S(1)}, u32[]{:S(2)}, u32[]{:S(2)}) async-start(bf16[32,8,128]{2,1,0:T(8,128)(2,1)} %get-tuple-element.18), calls=%async_computation.5 | async-start | bytes 131072 | tf_op jit(solution)/shard_map/all_to_all | solution.py:307
  103.5 21.6 %collective-permute-start.4 = (f32[2,1024]{1,0:T(2,128)S(1)}, f32[2,1024]{1,0:T(2,128)S(1)}, u32[]{:S(2)}, u32[]{:S(2)}) collective-permute-start(f32[2,1024]{1,0:T(2,128)S(1)} %get-tuple-element.12.stats), channel_id=1, source_target_pairs={{128,0},{129,1},{130,2},{131,3},{132,4},{133,5},{134,6},{135,7},{1... | collective-permute-start | bytes 24584 | tf_op jit(solution)/shard_map/ppermute | solution.py:364
  111.3 38.5 %all-to-all-start.6 = ((bf16[128,8,128]{2,1,0:T(8,128)(2,1)}), bf16[128,8,128]{2,1,0:T(8,128)(2,1)S(1)}, u32[]{:S(2)}, u32[]{:S(2)}) async-start(bf16[128,8,128]{2,1,0:T(8,128)(2,1)} %broadcast_in_dim.16), calls=%async_computation.6 | async-start | bytes 524288 | tf_op jit(solution)/shard_map/all_to_all | solution.py:307
  118.5 1.1 copy-start.4
  134.4 15.4 %collective-permute-start.5 = (bf16[128,1024]{1,0:T(8,128)(2,1)S(1)}, bf16[128,1024]{1,0:T(8,128)(2,1)S(1)}, u32[]{:S(2)}, u32[]{:S(2)}) collective-permute-start(bf16[128,1024]{1,0:T(8,128)(2,1)S(1)} %shard_map.125), channel_id=1, source_target_pairs={{0,128},{1,129},{2,130},{3,131},{4,132},{5,133},{6,134},{7,135},{8... | collective-permute-start | bytes 786440 | tf_op jit(solution)/shard_map/ppermute | solution.py:372
  136.8 8.1 %collective-permute-start.6 = (bf16[32,256]{1,0:T(8,128)(2,1)S(1)}, bf16[32,256]{1,0:T(8,128)(2,1)S(1)}, u32[]{:S(2)}, u32[]{:S(2)}) collective-permute-start(bf16[32,256]{1,0:T(8,128)(2,1)S(1)} %get-tuple-element.15), channel_id=1, source_target_pairs={{0,1},{1,0},{2,3},{3,2},{4,5},{5,4},{6,7},{7,6},{8,9},{9,8},{10,11... | collective-permute-start | bytes 49160 | tf_op jit(solution)/shard_map/ppermute | solution.py:321
  144.9 6.7 %collective-permute-start.9 = (bf16[64,256]{1,0:T(8,128)(2,1)S(1)}, bf16[64,256]{1,0:T(8,128)(2,1)S(1)}, u32[]{:S(2)}, u32[]{:S(2)}) collective-permute-start(bf16[64,256]{1,0:T(8,128)(2,1)S(1)} %constant_dynamic-update-slice_fusion.refs_0_), channel_id=1, source_target_pairs={{0,6},{2,0},{4,2},{6,4},{1,7},{3,1},{5,3},{7,5},{8,14},{10,8},{12,... | collective-permute-start | bytes 98312 | tf_op jit(solution)/shard_map/ppermute | solution.py:321
  148.3 5.4 %collective-permute-start.8 = (bf16[64,256]{1,0:T(8,128)(2,1)S(1)}, bf16[64,256]{1,0:T(8,128)(2,1)S(1)}, u32[]{:S(2)}, u32[]{:S(2)}) collective-permute-start(bf16[64,256]{1,0:T(8,128)(2,1)S(1)} %constant_dynamic-update-slice_fusion.refs_0_), channel_id=1, source_target_pairs={{0,4},{2,6},{4,0},{6,2},{1,5},{3,7},{5,1},{7,3},{8,12},{10,14},{12... | collective-permute-start | bytes 98312 | tf_op jit(solution)/shard_map/ppermute | solution.py:321
  148.7 5.4 %collective-permute-start.7 = (bf16[64,256]{1,0:T(8,128)(2,1)S(1)}, bf16[64,256]{1,0:T(8,128)(2,1)S(1)}, u32[]{:S(2)}, u32[]{:S(2)}) collective-permute-start(bf16[64,256]{1,0:T(8,128)(2,1)S(1)} %constant_dynamic-update-slice_fusion.refs_0_), channel_id=1, source_target_pairs={{0,2},{2,4},{4,6},{6,0},{1,3},{3,5},{5,7},{7,1},{8,10},{10,12},{12... | collective-permute-start | bytes 98312 | tf_op jit(solution)/shard_map/ppermute | solution.py:321
  149.8 6.1 %collective-permute-start.10 = (bf16[128,8,128]{2,1,0:T(8,128)(2,1)S(1)}, bf16[128,8,128]{2,1,0:T(8,128)(2,1)S(1)}, u32[]{:S(2)}, u32[]{:S(2)}) collective-permute-start(bf16[128,8,128]{2,1,0:T(8,128)(2,1)S(1)} %all-to-all-done.6.near), channel_id=1, source_target_pairs={{0,8},{8,0},{1,9},{9,1},{2,10},{10,2},{3,11},{11,3},{4,12},{12,4},... | collective-permute-start | bytes 786440 | tf_op jit(solution)/shard_map/ppermute | solution.py:321
  150.5 3.5 %copy-start.2 = (bf16[256,1024]{1,0:T(8,128)(2,1)S(1)}, bf16[256,1024]{1,0:T(8,128)(2,1)}, u32[]{:S(2)}) copy-start(bf16[256,1024]{1,0:T(8,128)(2,1)} %embed.1) | copy-start | bytes 1572868

commit v5 on v4

--- a/solution.py
+++ b/solution.py
@@ -68,8 +68,54 @@
     return key < (pos[0] + pos[1] - 2 * j) * HD
 
 
-def sweep_step(pos, q, g, mine, other, j, states, masked=False):
-    for own, kv in ((True, mine), (False, other)):
+def generate_kernel(place, embed, w_hidden, bias, w_out, keys, values, hidden, factor, payload, tangent):
+    tangent[...] = jnp.tanh(dot_nn(embed[...], w_hidden[...]) + bias[...])
+    hidden[...] = tangent[...].astype(BF16)
+    share = factor.shape[0]
+    first = pl.multiple_of((2 * place[0] + place[1]) * share, share)
+    own = tangent[pl.ds(first, share), :]
+    factor[...] = 1.0 - own * own
+    groups = payload.shape[0]
+    rows = keys.shape[0]
+    npre = hidden.shape[0]
+    size = 2 * npre // groups
+    for c in range(2):
+        part = dot_nn(hidden[...], w_out[:, c, :]).astype(BF16)
+        for k in range(groups // 2):
+            payload[c * groups // 2 + k, 2 * rows :, :] = part[k * size : (k + 1) * size]
+    for k in range(groups):
+        payload[k, :rows, :] = keys[...]
+        payload[k, rows : 2 * rows, :] = values[...]
+
+
+def generated(place, embed, w_hidden, bias, w_out, keys, values):
+    npre, units = embed.shape[0], w_hidden.shape[1]
+    groups = lax.axis_size("z")
+    out = (
+        jax.ShapeDtypeStruct((npre, units), BF16),
+        jax.ShapeDtypeStruct((npre // lax.axis_size(HEAD), units), F32),
+        jax.ShapeDtypeStruct((groups, 2 * keys.shape[0] + 2 * npre // groups, HD), BF16),
+    )
+    values_in = (embed, w_hidden, bias, w_out, keys, values)
+    return pl.pallas_call(
+        generate_kernel,
+        out_shape=out,
+        in_specs=[SMEM] + [whole(v) for v in values_in],
+        out_specs=tuple(whole(v) for v in out),
+        grid=(1,),
+        scratch_shapes=[pltpu.VMEM((npre, units), F32)],
+        compiler_params=pltpu.CompilerParams(vmem_limit_bytes=GRANT),
+        cost_estimate=pl.CostEstimate(flops=2 * 10**8, bytes_accessed=2 * 10**6, transcendentals=10**5),
+        name="generate",
+    )(place, *(pltpu.with_memory_space_constraint(v, pltpu.HBM) for v in values_in))
+
+
+def whole(value):
+    return pl.BlockSpec(value.shape, lambda *_: (0,) * len(value.shape))
+
+
+def sweep_step(pos, q, g, sources, j, states, masked=False):
+    for own, kv in sources:
         k, v = pair_of(kv, j)
         seen = visible(pos, own, j, (2 * HD, TILE), 0) if masked else None
         new = []
@@ -89,7 +135,7 @@
 
 def sweep_kernel(pos, q, g, mine, other, out):
     tiles = q.shape[0] // TILE
-    step = functools.partial(sweep_step, pos, q, g, mine, other)
+    step = functools.partial(sweep_step, pos, q, g, ((True, mine), (False, other)))
     half = pos[0] // 2
     states = step(half, lax.fori_loop(0, half, step, empty_states(tiles)), True)
     for r in range(tiles):
@@ -103,14 +149,22 @@
     return top, jnp.sum(l * fade, axis=0, keepdims=True), jnp.sum(t * fade, axis=0, keepdims=True)
 
 
-def lent_sweep_kernel(pos, q, g, mine, other, out):
+def lent_sweep_kernel(last, pos, q, g, kv, *refs):
+    *begun, out = refs
     tiles = q.shape[0] // TILE
-    step = functools.partial(sweep_step, pos, q, g, mine, other)
-    pairs = jnp.where(pos[2] == 0, mine.shape[0] // 2, 0)
-    states = lax.fori_loop(0, pairs, step, empty_states(tiles))
+    states = empty_states(tiles)
+    if begun:
+        states = tuple(tuple(begun[0][a, :, span(r)] for a in range(3)) for r in range(tiles))
+    step = functools.partial(sweep_step, pos, q, g, ((True, kv),))
+    pairs = jnp.where(pos[2] == 0, kv.shape[0] // 2, 0)
+    states = lax.fori_loop(0, pairs, step, states)
     for r in range(tiles):
-        for a, value in enumerate(merged(*states[r])):
-            out[a : a + 1, span(r)] = value
+        if last:
+            for a, value in enumerate(merged(*states[r])):
+                out[a : a + 1, span(r)] = value
+        else:
+            for a in range(3):
+                out[a, :, span(r)] = states[r][a]
 
 
 def prefix_kernel(pos, q, g, halves, state, lent, grads, stats, pkv):
@@ -217,9 +271,11 @@
     return call(sweep_kernel, jax.ShapeDtypeStruct((3, 8, q.shape[0]), F32), 10**9, pos, q, g, mine, other)
 
 
-def lent_sweep(pos, q, g, mine, other):
-    out = jax.ShapeDtypeStruct((3, q.shape[0]), F32)
-    return call(lent_sweep_kernel, out, 10**9, pos, q, g, mine, other)
+def lent_sweep(pos, q, g, kv, *begun):
+    last = bool(begun)
+    out = jax.ShapeDtypeStruct((3, q.shape[0]) if last else (3, 8, q.shape[0]), F32)
+    kernel = functools.partial(lent_sweep_kernel, last)
+    return call(kernel, out, 5 * 10**8, pos, q, g, kv, *begun)
 
 
 def prefix_part(pos, q, g, halves, state, lent):
@@ -330,23 +386,14 @@
     units = w_hidden.shape[1]
     core = lax.axis_index("c")
     late = lax.axis_index("y")
-    head = lax.axis_index(HEAD)
     heads = lax.axis_size(HEAD)
     share = npre // heads
+    place = jnp.stack([lax.axis_index("x"), lax.axis_index("w")]).astype(jnp.int32)
     pos = jnp.stack([lax.axis_index("z"), core, late]).astype(jnp.int32)
 
-    hidden_pre = jnp.dot(prefix_embed, w_hidden, preferred_element_type=F32) + b_hidden
-    tangent = jnp.tanh(hidden_pre)
-    hidden = tangent.astype(BF16)
-    partial_kv = jnp.einsum("ph,hck->cpk", hidden, w_out, preferred_element_type=F32)
-    own_tangent = lax.dynamic_slice_in_dim(tangent, head * share, share, 0)
-    factor = lax.optimization_barrier(1.0 - own_tangent * own_tangent)
-    groups = lax.axis_size("z")
-    kv = jnp.concatenate([keys, values], 0)
-    partial_kv = partial_kv.reshape(groups, -1, HD).astype(BF16)
-    mine = exchange(
-        jnp.concatenate([jnp.broadcast_to(kv, (groups, *kv.shape)), partial_kv], 1), "z"
-    )
+    hidden, factor, payload = generated(place, prefix_embed, w_hidden, b_hidden.reshape(1, units), w_out, keys, values)
+    kv_rows = 2 * keys.shape[0]
+    mine = exchange(payload, "z")
     q = by_head(queries)
     g = by_head(out_grad)
     lent_q = lax.ppermute(queries, "y", [(1, 0)])
@@ -354,10 +401,11 @@
     lent_q = by_head(lent_q)
     lent_g = by_head(lent_g)
     other = shift(mine, "c", 1)
-    sides = [jnp.sum(v[:, kv.shape[0] :].astype(F32), axis=0) for v in (mine, other)]
+    lent_state = lent_sweep(pos, lent_q, lent_g, mine)
+    sides = [jnp.sum(v[:, kv_rows:].astype(F32), axis=0) for v in (mine, other)]
     own = (sides[0] + sides[1]).astype(BF16)
     halves = to_all(own, YZ).reshape(lax.axis_size("y"), 2, npre, HD)
-    lent_state = lent_sweep(pos, lent_q, lent_g, mine, other)
+    lent_state = lent_sweep(pos, lent_q, lent_g, other, lent_state)
     lent_state = lax.ppermute(lent_state, "y", [(0, 1)])
     state = sweep(pos, q, g, mine, other)
     grads, stats, pkv = prefix_part(pos, q, g, halves, state, lent_state)
@@ -384,7 +432,6 @@
     grad_prefix = joined(pos, near, far, heads, npre, emb)
     both = jnp.concatenate([pre_part, shift(pre_part, "w", 1)], 0)
     turns = [shift(both, "x", k) for k in range(1, lax.axis_size("x"))]
-    place = jnp.stack([lax.axis_index("x"), lax.axis_index("w")]).astype(jnp.int32)
     grad_w_hidden, grad_b_hidden = w_hidden_grad(place, prefix_embed, both, *turns)
     return (query_grad, grad_w_out, grad_w_hidden, grad_b_hidden, grad_prefix)
 

time: 158 us -> 157 us (level)
  blocking collectives: 28.3 us -> 44.9 us
  waiting for transfers between devices: 38.5 us -> 29.4 us
  starting transfers between devices: 49.4 us -> 42.6 us
  Pallas kernels: 29.6 us -> 33.9 us
  matrix products: 3.32 us -> 0.22 us
  other arithmetic: 3.51 us -> 1.05 us
    all_to_all x2 -> x3, blocking collectives: 28.3 us -> 44.9 us  [exchange(): return lax.all_to_all(value, axes, 0, 0, tiled=True)]
    all_to_all x5 -> x4, waiting for transfers between devices: 29.2 us -> 20.1 us  [exchange(): return lax.all_to_all(value, axes, 0, 0, tiled=True)]
    all_to_all x5 -> x4, starting transfers between devices: 34.9 us -> 28.1 us  [exchange(): return lax.all_to_all(value, axes, 0, 0, tiled=True)]
    pallas_call x0 -> x1, Pallas kernels: none -> 2.86 us  [generated(): pl.pallas_call(generate_kernel, out_shape=out, in_specs=[SMEM] + [whole(v...]
    dot_general x2 -> x0, matrix products: 2.4 us -> none  [the longest x1 2.21 us: on_device(): jnp.dot(prefix_embed, w_hidden, preferred_element_type=F32) + b_hidden]
    concatenate x2 -> x0, other arithmetic: 1.7 us -> none  [the longest x1 0.88 us: on_device(): jnp.concatenate([jnp.broadcast_to(kv, (groups, *kv.shape)), partial_kv], 1)]
    pallas_call x11 -> x12, Pallas kernels: 29.6 us -> 31.1 us  [call(): pl.pallas_call(kernel, out_shape=out_shape, in_specs=[SMEM if v.dtype ==...]
  transfers between devices with their start and end apart: 16 -> 15, of which waited for: 8 -> 6; matrix products, arithmetic and copies ran while one was open for 3% -> 3% of each run, Pallas kernels for 16% -> 17%
where the time goes in v5:
time: 157 us
  blocking collectives  44.9 us (29%)
  starting transfers between devices  42.6 us (27%)
  Pallas kernels  33.9 us (22%)
  waiting for transfers between devices  29.4 us (19%)
  local copies, waits for them, and re-layouts  3.62 us (2%)
    all_to_all x3, blocking collectives, exchange(): return lax.all_to_all(value, axes, 0, 0, tiled=True)  44.9 us
    pallas_call x12, Pallas kernels, call(): pl.pallas_call(kernel, out_shape=out_shape, in_specs=[SMEM if v.dtype ==...  31.1 us
    all_to_all x4, starting transfers between devices, exchange(): return lax.all_to_all(value, axes, 0, 0, tiled=True)  28.1 us
    all_to_all x4, waiting for transfers between devices, exchange(): return lax.all_to_all(value, axes, 0, 0, tiled=True)  20.1 us
    ppermute x6, waiting for transfers between devices, shift(): lax.ppermute(value, axis, [(i, (i + steps) % count) for i in range(count)])  9.27 us
    ppermute x6, starting transfers between devices, shift(): lax.ppermute(value, axis, [(i, (i + steps) % count) for i in range(count)])  7.99 us
  transfers between devices with their start and end apart: 15, of which 6 were waited for; matrix products, arithmetic and copies ran while one was open for 3% of the time, Pallas kernels for 17%

profile of v5, /device:TPU:64, one launch (start us, length us, event | category | flops | bytes accessed | tf_op | source)
XLA Modules:
  0.0 156.6 jit_solution(10145002143637567552)
XLA Ops:
  0.7 2.9 %generate.1 = (bf16[256,256]{1,0:T(8,128)(2,1)S(1)}, f32[32,256]{1,0:T(8,128)S(1)}, bf16[8,320,128]{2,1,0:T(8,128)(2,1)}) custom-call(s32[2]{0:T(128)S(1)} %pad_add_fusion.1.place, bf16[256,1024]{1,0:T(8,128)(2,1)} %embed.3, bf16[1024,256]{1,0:T(8,128)(2,1)} %w_hidden.3, f32[1,256]{1,0:T(1,128)} %bitcast.70, bf16[256,2,128]{2,1,0:T(2,128)(2,1)} %w_out.1, ...), custom_call_target="tpu_custom_call" | custom-call | flops 200000000 | bytes 2000000 | tf_op jit(solution)/shard_map/generate/pallas_call | solution.py:100
  3.6 8.2 %all-to-all-start = ((bf16[8,320,128]{2,1,0:T(8,128)(2,1)}), bf16[8,320,128]{2,1,0:T(8,128)(2,1)S(1)}, u32[]{:S(2)}, u32[]{:S(2)}) async-start(bf16[8,320,128]{2,1,0:T(8,128)(2,1)} %get-tuple-element.15), calls=%async_computation | async-start | bytes 1310720 | tf_op jit(solution)/shard_map/all_to_all | solution.py:363
  11.8 1.3 collective-permute-start.1
  13.1 1.3 collective-permute-start.2
  14.4 14.3 %all-to-all-done.mine.kv = bf16[8,320,128]{2,1,0:T(8,128)(2,1)S(1)} async-done(((bf16[8,320,128]{2,1,0:T(8,128)(2,1)}), bf16[8,320,128]{2,1,0:T(8,128)(2,1)S(1)}, u32[]{:S(2)}, u32[]{:S(2)}) %all-to-all-start) | async-done | bytes 655392 | tf_op jit(solution)/shard_map/all_to_all | solution.py:363
  28.9 1.9 %collective-permute-done.other.kv = bf16[8,320,128]{2,1,0:T(8,128)(2,1)S(1)} collective-permute-done((bf16[8,320,128]{2,1,0:T(8,128)(2,1)S(1)}, bf16[8,320,128]{2,1,0:T(8,128)(2,1)S(1)}, u32[]{:S(2)}, u32[]{:S(2)}) %collective-permute-start) | collective-permute-done | bytes 655392 | tf_op jit(solution)/shard_map/ppermute | solution.py:377
  31.6 6.7 %all-to-all-start.1 = ((bf16[16,64,128]{2,1,0:T(8,128)(2,1)}), bf16[16,64,128]{2,1,0:T(8,128)(2,1)S(1)}, u32[]{:S(2)}, u32[]{:S(2)}) async-start(bf16[16,64,128]{2,1,0:T(8,128)(2,1)} %broadcast_in_dim.9), calls=%async_computation.1 | async-start | bytes 524288 | tf_op jit(solution)/shard_map/all_to_all | solution.py:363
  40.4 2.7 %shard_map.120.refs_0_ = f32[3,8,1024]{2,1,0:T(8,128)S(1)} custom-call(s32[3]{0:T(128)S(1)} %pad_add_fusion.pos, bf16[1024,128]{1,0:T(8,128)(2,1)S(1)} %bitcast.59, bf16[1024,128]{1,0:T(8,128)(2,1)S(1)} %bitcast.63, bf16[8,320,128]{2,1,0:T(8,128)(2,1)S(1)} %all-to-all-done.mine.kv), custom_call_target="tpu_custom_call" | custom-call | flops 500000000 | bytes 1000000 | tf_op jit(solution)/shard_map/pallas_call | solution.py:259
  43.1 2.7 %shard_map.121 = f32[3,1024]{1,0:T(4,128)S(1)} custom-call(s32[3]{0:T(128)S(1)} %pad_add_fusion.pos, bf16[1024,128]{1,0:T(8,128)(2,1)S(1)} %bitcast.60, bf16[1024,128]{1,0:T(8,128)(2,1)S(1)} %bitcast.64, bf16[8,320,128]{2,1,0:T(8,128)(2,1)S(1)} %collective-permute-done.other.kv, f32[3,8,1024]{2,1,0:T(8,128)S(1)} %shard_map.120.refs_0_), custom_call_target="tpu_custom_call" | custom-call | flops 500000000 | bytes 1000000 | tf_op jit(solution)/shard_map/pallas_call | solution.py:259
  45.8 1.3 collective-permute-start.3
  47.1 2.3 %shard_map.119.state = f32[3,8,1024]{2,1,0:T(8,128)S(1)} custom-call(s32[3]{0:T(128)S(1)} %pad_add_fusion.pos, bf16[1024,128]{1,0:T(8,128)(2,1)S(1)} %bitcast.51, bf16[1024,128]{1,0:T(8,128)(2,1)S(1)} %bitcast.55, bf16[8,320,128]{2,1,0:T(8,128)(2,1)S(1)} %all-to-all-done.mine.kv, bf16[8,320,128]{2,1,0:T(8,128)(2,1)S(1)} %collective-permute-done.other.kv), custom_call_target="tpu_custom_call" | custom-call | flops 1000000000 | bytes 1000000 | tf_op jit(solution)/shard_map/pallas_call | solution.py:259
  49.4 2.1 %shard_map.122 = (bf16[2,256,128]{2,1,0:T(8,128)(2,1)S(1)}, f32[2,1024]{1,0:T(2,128)S(1)}, bf16[2,256,128]{2,1,0:T(8,128)(2,1)S(1)}) custom-call(s32[3]{0:T(128)S(1)} %pad_add_fusion.pos, bf16[1024,128]{1,0:T(8,128)(2,1)S(1)} %bitcast.52, bf16[1024,128]{1,0:T(8,128)(2,1)S(1)} %bitcast.56, bf16[2,2,256,128]{3,2,1,0:T(8,128)(2,1)S(1)} %bitcast.67, ...), custom_call_target="tpu_custom_call" | custom-call | flops 300000000 | bytes 1000000 | tf_op jit(solution)/shard_map/pallas_call | solution.py:259
  51.5 15.9 %all_to_all.35 = bf16[32,16,128]{2,1,0:T(8,128)(2,1)S(1)} all-to-all(bf16[32,16,128]{2,1,0:T(8,128)(2,1)S(1)} %bitcast.68), channel_id=1, replica_groups=mesh['y'=2,'z'=8,'c'=2,'x'=4,'w'=2] {'y','z','c'}, dimensions={0} | all-to-all | bytes 262144 | tf_op jit(solution)/shard_map/all_to_all | solution.py:363
  67.4 13.5 %all_to_all.36 = bf16[32,16,128]{2,1,0:T(8,128)(2,1)S(1)} all-to-all(bf16[32,16,128]{2,1,0:T(8,128)(2,1)S(1)} %broadcast_in_dim.10), channel_id=1, replica_groups=mesh['y'=2,'z'=8,'c'=2,'x'=4,'w'=2] {'y','z','c'}, dimensions={0} | all-to-all | bytes 262144 | tf_op jit(solution)/shard_map/all_to_all | solution.py:363
  81.2 15.5 %all_to_all.37.parts = f32[8,32,256]{2,1,0:T(8,128)S(1)} all-to-all(f32[8,32,256]{2,1,0:T(8,128)S(1)} %convolution_bitcast_fusion), channel_id=1, replica_groups=mesh['y'=2,'z'=8,'c'=2,'x'=4,'w'=2] {'x','w'}, dimensions={0} | all-to-all | bytes 524288 | tf_op jit(solution)/shard_map/all_to_all | solution.py:363
  97.6 6.0 %all-to-all-start.5 = ((bf16[32,8,128]{2,1,0:T(8,128)(2,1)}), bf16[32,8,128]{2,1,0:T(8,128)(2,1)S(1)}, u32[]{:S(2)}, u32[]{:S(2)}) async-start(bf16[32,8,128]{2,1,0:T(8,128)(2,1)} %get-tuple-element.24), calls=%async_computation.5 | async-start | bytes 131072 | tf_op jit(solution)/shard_map/all_to_all | solution.py:363
  103.6 1.3 collective-permute-start.4
  104.9 5.8 %all-to-all-done.5 = bf16[32,8,128]{2,1,0:T(8,128)(2,1)S(1)} async-done(((bf16[32,8,128]{2,1,0:T(8,128)(2,1)}), bf16[32,8,128]{2,1,0:T(8,128)(2,1)S(1)}, u32[]{:S(2)}, u32[]{:S(2)}) %all-to-all-start.5) | async-done | bytes 65568 | tf_op jit(solution)/shard_map/all_to_all | solution.py:363
  111.5 7.2 %all-to-all-start.6 = ((bf16[128,8,128]{2,1,0:T(8,128)(2,1)}), bf16[128,8,128]{2,1,0:T(8,128)(2,1)S(1)}, u32[]{:S(2)}, u32[]{:S(2)}) async-start(bf16[128,8,128]{2,1,0:T(8,128)(2,1)} %broadcast_in_dim.11), calls=%async_computation.6 | async-start | bytes 524288 | tf_op jit(solution)/shard_map/all_to_all | solution.py:363
  118.7 5.4 %shard_map.123.refs_0_ = bf16[128,1024]{1,0:T(8,128)(2,1)S(1)} custom-call(s32[3]{0:T(128)S(1)} %pad_add_fusion.pos, bf16[1024,128]{1,0:T(8,128)(2,1)S(1)} %bitcast.53, bf16[1024,128]{1,0:T(8,128)(2,1)S(1)} %bitcast.57, f32[2,1024]{1,0:T(2,128)S(1)} %get-tuple-element.16.stats, bf16[8,320,128]{2,1,0:T(8,128)(2,1)S(1)} %all-to-all-done.mine.kv, ...), custom_call_target="tpu_custom_call" | custom-call | flops 1000000000 | bytes 1000000 | tf_op jit(solution)/shard_map/pallas_call | solution.py:259
  124.1 4.7 %shard_map.125.refs_0_ = bf16[128,1024]{1,0:T(8,128)(2,1)S(1)} custom-call(s32[3]{0:T(128)S(1)} %pad_add_fusion.pos, bf16[1024,128]{1,0:T(8,128)(2,1)S(1)} %bitcast.61, bf16[1024,128]{1,0:T(8,128)(2,1)S(1)} %bitcast.65, f32[2,1024]{1,0:T(2,128)S(1)} %collective-permute-done.4.stats, bf16[8,320,128]{2,1,0:T(8,128)(2,1)S(1)} %all-to-all-done.mine.kv, ...), custom_call_target="tpu_custom_call" | custom-call | flops 1000000000 | bytes 1000000 | tf_op jit(solution)/shard_map/pallas_call | solution.py:259
  128.8 4.7 %shard_map.126 = bf16[128,1024]{1,0:T(8,128)(2,1)S(1)} custom-call(s32[3]{0:T(128)S(1)} %pad_add_fusion.pos, bf16[1024,128]{1,0:T(8,128)(2,1)S(1)} %bitcast.62, bf16[1024,128]{1,0:T(8,128)(2,1)S(1)} %bitcast.66, f32[2,1024]{1,0:T(2,128)S(1)} %collective-permute-done.4.stats, bf16[8,320,128]{2,1,0:T(8,128)(2,1)S(1)} %all-to-all-done.mine.kv, ...), custom_call_target="tpu_custom_call" | custom-call | flops 1000000000 | bytes 1000000 | tf_op jit(solution)/shard_map/pallas_call | solution.py:259
  133.5 1.3 collective-permute-start.5
  134.8 1.1 shard_map.124
  135.9 3.2 %collective-permute-start.6 = (bf16[32,256]{1,0:T(8,128)(2,1)S(1)}, bf16[32,256]{1,0:T(8,128)(2,1)S(1)}, u32[]{:S(2)}, u32[]{:S(2)}) collective-permute-start(bf16[32,256]{1,0:T(8,128)(2,1)S(1)} %get-tuple-element.21), channel_id=1, source_target_pairs={{0,1},{1,0},{2,3},{3,2},{4,5},{5,4},{6,7},{7,6},{8,9},{9,8},{10,11... | collective-permute-start | bytes 49160 | tf_op jit(solution)/shard_map/ppermute | solution.py:377
  139.1 5.0 %collective-permute-done.6 = bf16[32,256]{1,0:T(8,128)(2,1)S(1)} collective-permute-done((bf16[32,256]{1,0:T(8,128)(2,1)S(1)}, bf16[32,256]{1,0:T(8,128)(2,1)S(1)}, u32[]{:S(2)}, u32[]{:S(2)}) %collective-permute-start.6) | collective-permute-done | bytes 16416 | tf_op jit(solution)/shard_map/ppermute | solution.py:377
  144.0 3.3 %collective-permute-start.9 = (bf16[64,256]{1,0:T(8,128)(2,1)S(1)}, bf16[64,256]{1,0:T(8,128)(2,1)S(1)}, u32[]{:S(2)}, u32[]{:S(2)}) collective-permute-start(bf16[64,256]{1,0:T(8,128)(2,1)S(1)} %constant_dynamic-update-slice_fusion.refs_0_), channel_id=1, source_target_pairs={{0,6},{2,0},{4,2},{6,4},{1,7},{3,1},{5,3},{7,5},{8,14},{10,8},{12,... | collective-permute-start | bytes 98312 | tf_op jit(solution)/shard_map/ppermute | solution.py:377
  147.8 1.1 collective-permute-start.7
  149.7 1.1 shard_map.127
  150.7 2.1 %collective-permute-done.8.refs_2_ = bf16[64,256]{1,0:T(8,128)(2,1)S(1)} collective-permute-done((bf16[64,256]{1,0:T(8,128)(2,1)S(1)}, bf16[64,256]{1,0:T(8,128)(2,1)S(1)}, u32[]{:S(2)}, u32[]{:S(2)}) %collective-permute-start.8) | collective-permute-done | bytes 32800 | tf_op jit(solution)/shard_map/ppermute | solution.py:377
  153.1 1.9 %shard_map.129 = (f32[1024,256]{1,0:T(8,128)}, f32[256]{0:T(256)}) custom-call(s32[2]{0:T(128)S(1)} %pad_add_fusion.1.place, bf16[256,1024]{1,0:T(8,128)(2,1)S(1)} %copy-done.1, bf16[64,256]{1,0:T(8,128)(2,1)S(1)} %constant_dynamic-update-slice_fusion.refs_0_, bf16[64,256]{1,0:T(8,128)(2,1)S(1)} %collective-permute-done.7.refs_1_, ...), custom_call_target="tpu_custom_call" | custom-call | flops 200000000 | bytes 1000000 | tf_op jit(solution)/shard_map/pallas_call | solution.py:259
  155.0 1.6 %shard_map.130 = f32[256,1024]{1,0:T(8,128)} custom-call(s32[3]{0:T(128)S(1)} %pad_add_fusion.pos, bf16[128,8,128]{2,1,0:T(8,128)(2,1)S(1)} %all-to-all-done.6.near, bf16[128,8,128]{2,1,0:T(8,128)(2,1)S(1)} %collective-permute-done.10.far), custom_call_target="tpu_custom_call" | custom-call | flops 1000000 | bytes 1000000 | tf_op jit(solution)/shard_map/pallas_call | solution.py:259
  (42 shorter events, 6.6 us)
Async XLA Ops:
  3.6 8.3 %copy-start.3 = (bf16[128,1024]{1,0:T(8,128)(2,1)S(1)}, bf16[128,1024]{1,0:T(8,128)(2,1)}, u32[]{:S(2)}) copy-start(bf16[128,1024]{1,0:T(8,128)(2,1)} %param.12) | copy-start | bytes 786436
  3.6 9.5 %copy-start.4 = (bf16[128,1024]{1,0:T(8,128)(2,1)S(1)}, bf16[128,1024]{1,0:T(8,128)(2,1)}, u32[]{:S(2)}) copy-start(bf16[128,1024]{1,0:T(8,128)(2,1)} %param.15) | copy-start | bytes 786436
  3.6 25.2 %all-to-all-start = ((bf16[8,320,128]{2,1,0:T(8,128)(2,1)}), bf16[8,320,128]{2,1,0:T(8,128)(2,1)S(1)}, u32[]{:S(2)}, u32[]{:S(2)}) async-start(bf16[8,320,128]{2,1,0:T(8,128)(2,1)} %get-tuple-element.15), calls=%async_computation | async-start | bytes 1310720 | tf_op jit(solution)/shard_map/all_to_all | solution.py:363
  11.8 26.5 %collective-permute-start.1 = (bf16[128,1024]{1,0:T(8,128)(2,1)S(1)}, bf16[128,1024]{1,0:T(8,128)(2,1)}, u32[]{:S(2)}, u32[]{:S(2)}) collective-permute-start(bf16[128,1024]{1,0:T(8,128)(2,1)S(1)} %copy-done.3), channel_id=1, source_target_pairs={{128,0},{129,1},{130,2},{131,3},{132,4},{133,5},{134,6},{135,7},{1... | collective-permute-start | bytes 786440 | tf_op jit(solution)/shard_map/ppermute | solution.py:399
  13.1 26.2 %collective-permute-start.2 = (bf16[128,1024]{1,0:T(8,128)(2,1)S(1)}, bf16[128,1024]{1,0:T(8,128)(2,1)}, u32[]{:S(2)}, u32[]{:S(2)}) collective-permute-start(bf16[128,1024]{1,0:T(8,128)(2,1)S(1)} %copy-done.4), channel_id=1, source_target_pairs={{128,0},{129,1},{130,2},{131,3},{132,4},{133,5},{134,6},{135,7},{1... | collective-permute-start | bytes 786440 | tf_op jit(solution)/shard_map/ppermute | solution.py:400
  28.7 2.1 %collective-permute-start = (bf16[8,320,128]{2,1,0:T(8,128)(2,1)S(1)}, bf16[8,320,128]{2,1,0:T(8,128)(2,1)S(1)}, u32[]{:S(2)}, u32[]{:S(2)}) collective-permute-start(bf16[8,320,128]{2,1,0:T(8,128)(2,1)S(1)} %all-to-all-done.mine.kv), channel_id=1, source_target_pairs={{0,8},{8,0},{1,9},{9,1},{2,10},{10,2},{3,11},{11,3},{4,12},{12,4},... | collective-permute-start | bytes 1966088 | tf_op jit(solution)/shard_map/ppermute | solution.py:377
  31.6 17.8 %all-to-all-start.1 = ((bf16[16,64,128]{2,1,0:T(8,128)(2,1)}), bf16[16,64,128]{2,1,0:T(8,128)(2,1)S(1)}, u32[]{:S(2)}, u32[]{:S(2)}) async-start(bf16[16,64,128]{2,1,0:T(8,128)(2,1)} %broadcast_in_dim.9), calls=%async_computation.1 | async-start | bytes 524288 | tf_op jit(solution)/shard_map/all_to_all | solution.py:363
  45.8 3.6 %collective-permute-start.3 = (f32[3,1024]{1,0:T(4,128)S(1)}, f32[3,1024]{1,0:T(4,128)S(1)}, u32[]{:S(2)}, u32[]{:S(2)}) collective-permute-start(f32[3,1024]{1,0:T(4,128)S(1)} %shard_map.121), channel_id=1, source_target_pairs={{0,128},{1,129},{2,130},{3,131},{4,132},{5,133},{6,134},{7,135},{8... | collective-permute-start | bytes 36872 | tf_op jit(solution)/shard_map/ppermute | solution.py:409
  67.4 13.5 %copy-start.2 = (bf16[256,2,128]{2,1,0:T(2,128)(2,1)S(1)}, bf16[256,2,128]{2,1,0:T(2,128)(2,1)}, u32[]{:S(2)}) copy-start(bf16[256,2,128]{2,1,0:T(2,128)(2,1)} %w_out.1) | copy-start | bytes 393220
  81.0 15.8 %copy-start = (bf16[1024,256]{1,0:T(8,128)(2,1)S(1)}, bf16[1024,256]{1,0:T(8,128)(2,1)}, u32[]{:S(2)}) copy-start(bf16[1024,256]{1,0:T(8,128)(2,1)} %w_hidden.3) | copy-start | bytes 1572868
  97.6 13.1 %all-to-all-start.5 = ((bf16[32,8,128]{2,1,0:T(8,128)(2,1)}), bf16[32,8,128]{2,1,0:T(8,128)(2,1)S(1)}, u32[]{:S(2)}, u32[]{:S(2)}) async-start(bf16[32,8,128]{2,1,0:T(8,128)(2,1)} %get-tuple-element.24), calls=%async_computation.5 | async-start | bytes 131072 | tf_op jit(solution)/shard_map/all_to_all | solution.py:363
  103.6 20.5 %collective-permute-start.4 = (f32[2,1024]{1,0:T(2,128)S(1)}, f32[2,1024]{1,0:T(2,128)S(1)}, u32[]{:S(2)}, u32[]{:S(2)}) collective-permute-start(f32[2,1024]{1,0:T(2,128)S(1)} %get-tuple-element.16.stats), channel_id=1, source_target_pairs={{128,0},{129,1},{130,2},{131,3},{132,4},{133,5},{134,6},{135,7},{1... | collective-permute-start | bytes 24584 | tf_op jit(solution)/shard_map/ppermute | solution.py:412
  111.5 37.4 %all-to-all-start.6 = ((bf16[128,8,128]{2,1,0:T(8,128)(2,1)}), bf16[128,8,128]{2,1,0:T(8,128)(2,1)S(1)}, u32[]{:S(2)}, u32[]{:S(2)}) async-start(bf16[128,8,128]{2,1,0:T(8,128)(2,1)} %broadcast_in_dim.11), calls=%async_computation.6 | async-start | bytes 524288 | tf_op jit(solution)/shard_map/all_to_all | solution.py:363
  133.5 15.4 %collective-permute-start.5 = (bf16[128,1024]{1,0:T(8,128)(2,1)S(1)}, bf16[128,1024]{1,0:T(8,128)(2,1)S(1)}, u32[]{:S(2)}, u32[]{:S(2)}) collective-permute-start(bf16[128,1024]{1,0:T(8,128)(2,1)S(1)} %shard_map.126), channel_id=1, source_target_pairs={{0,128},{1,129},{2,130},{3,131},{4,132},{5,133},{6,134},{7,135},{8... | collective-permute-start | bytes 786440 | tf_op jit(solution)/shard_map/ppermute | solution.py:420
  135.9 8.1 %collective-permute-start.6 = (bf16[32,256]{1,0:T(8,128)(2,1)S(1)}, bf16[32,256]{1,0:T(8,128)(2,1)S(1)}, u32[]{:S(2)}, u32[]{:S(2)}) collective-permute-start(bf16[32,256]{1,0:T(8,128)(2,1)S(1)} %get-tuple-element.21), channel_id=1, source_target_pairs={{0,1},{1,0},{2,3},{3,2},{4,5},{5,4},{6,7},{7,6},{8,9},{9,8},{10,11... | collective-permute-start | bytes 49160 | tf_op jit(solution)/shard_map/ppermute | solution.py:377
  144.0 6.7 %collective-permute-start.9 = (bf16[64,256]{1,0:T(8,128)(2,1)S(1)}, bf16[64,256]{1,0:T(8,128)(2,1)S(1)}, u32[]{:S(2)}, u32[]{:S(2)}) collective-permute-start(bf16[64,256]{1,0:T(8,128)(2,1)S(1)} %constant_dynamic-update-slice_fusion.refs_0_), channel_id=1, source_target_pairs={{0,6},{2,0},{4,2},{6,4},{1,7},{3,1},{5,3},{7,5},{8,14},{10,8},{12,... | collective-permute-start | bytes 98312 | tf_op jit(solution)/shard_map/ppermute | solution.py:377
  147.4 5.4 %collective-permute-start.8 = (bf16[64,256]{1,0:T(8,128)(2,1)S(1)}, bf16[64,256]{1,0:T(8,128)(2,1)S(1)}, u32[]{:S(2)}, u32[]{:S(2)}) collective-permute-start(bf16[64,256]{1,0:T(8,128)(2,1)S(1)} %constant_dynamic-update-slice_fusion.refs_0_), channel_id=1, source_target_pairs={{0,4},{2,6},{4,0},{6,2},{1,5},{3,7},{5,1},{7,3},{8,12},{10,14},{12... | collective-permute-start | bytes 98312 | tf_op jit(solution)/shard_map/ppermute | solution.py:377
  147.8 5.4 %collective-permute-start.7 = (bf16[64,256]{1,0:T(8,128)(2,1)S(1)}, bf16[64,256]{1,0:T(8,128)(2,1)S(1)}, u32[]{:S(2)}, u32[]{:S(2)}) collective-permute-start(bf16[64,256]{1,0:T(8,128)(2,1)S(1)} %constant_dynamic-update-slice_fusion.refs_0_), channel_id=1, source_target_pairs={{0,2},{2,4},{4,6},{6,0},{1,3},{3,5},{5,7},{7,1},{8,10},{10,12},{12... | collective-permute-start | bytes 98312 | tf_op jit(solution)/shard_map/ppermute | solution.py:377
  148.9 6.2 %collective-permute-start.10 = (bf16[128,8,128]{2,1,0:T(8,128)(2,1)S(1)}, bf16[128,8,128]{2,1,0:T(8,128)(2,1)S(1)}, u32[]{:S(2)}, u32[]{:S(2)}) collective-permute-start(bf16[128,8,128]{2,1,0:T(8,128)(2,1)S(1)} %all-to-all-done.6.near), channel_id=1, source_target_pairs={{0,8},{8,0},{1,9},{9,1},{2,10},{10,2},{3,11},{11,3},{4,12},{12,4},... | collective-permute-start | bytes 786440 | tf_op jit(solution)/shard_map/ppermute | solution.py:377
  149.7 3.5 %copy-start.1 = (bf16[256,1024]{1,0:T(8,128)(2,1)S(1)}, bf16[256,1024]{1,0:T(8,128)(2,1)}, u32[]{:S(2)}) copy-start(bf16[256,1024]{1,0:T(8,128)(2,1)} %embed.3) | copy-start | bytes 1572868

commit v6 on v5

--- a/solution.py
+++ b/solution.py
@@ -196,7 +196,7 @@
 
 
 def grad_kernel(lent, piece, pos, q, g, stats, mine, other, *refs):
-    *extra, out, total, log_total, delta = refs
+    *extra, out, total, log_total, delta = refs[: len(refs) - 2 * (piece > 0)]
     rows = q.shape[0]
     pairs = mine.shape[0] // 2 // PIECES
     first = piece * pairs
@@ -226,11 +226,10 @@
         delta[...] = jnp.broadcast_to(columns[:, 1:2], (rows, HD))
 
     if piece > 0:
-        for h in range(rows // HD):
-            at = slice(h * HD, (h + 1) * HD)
-            total[at, :] = extra[0][:, at].astype(F32) * (1.0 / SCALE)
-    else:
-        total[...] = jnp.zeros((rows, HD), F32)
+        held, sem = refs[-2:]
+        copy = pltpu.make_async_copy(extra[0], held, sem)
+        copy.start()
+    total[...] = jnp.zeros((rows, HD), F32)
     if lent:
 
         @pl.when(pos[2] == 0)
@@ -249,17 +248,27 @@
         def _():
             step(half - first, True)
 
+    if piece > 0:
+        copy.wait()
     for h in range(rows // HD):
         at = slice(h * HD, (h + 1) * HD)
-        out[:, at] = (total[at, :] * SCALE).astype(out.dtype)
-
-
-def call(kernel, out_shape, flops, *values, scratch=()):
-    held = [v if v.dtype == jnp.int32 else pltpu.with_memory_space_constraint(v, pltpu.VMEM) for v in values]
+        result = total[at, :] * SCALE
+        if piece > 0:
+            result = result + held[:, at].astype(F32)
+        out[:, at] = result.astype(out.dtype)
+
+
+def call(kernel, out_shape, flops, *values, far=(), scratch=()):
+    spaces = [pltpu.SMEM if v.dtype == jnp.int32 else pltpu.VMEM for v in values]
+    spaces += [pltpu.HBM for _ in far]
+    held = [
+        v if space == pltpu.SMEM else pltpu.with_memory_space_constraint(v, space)
+        for v, space in zip((*values, *far), spaces)
+    ]
     return pl.pallas_call(
         kernel,
         out_shape=out_shape,
-        in_specs=[SMEM if v.dtype == jnp.int32 else VMEM for v in values],
+        in_specs=[pl.BlockSpec(memory_space=space) for space in spaces],
         out_specs=jax.tree.map(lambda _: VMEM, out_shape),
         scratch_shapes=list(scratch),
         compiler_params=pltpu.CompilerParams(vmem_limit_bytes=GRANT),
@@ -287,8 +296,12 @@
 def query_grad_piece(lent, piece, pos, q, g, stats, mine, other, *extra):
     out = jax.ShapeDtypeStruct(q.shape[::-1], BF16)
     scratch = [pltpu.VMEM(q.shape, F32)] * 3
+    far = ()
+    if piece > 0:
+        far, extra = extra, ()
+        scratch += [pltpu.VMEM(q.shape[::-1], BF16), pltpu.SemaphoreType.DMA]
     kernel = functools.partial(grad_kernel, lent, piece)
-    return call(kernel, out, 10**9, pos, q, g, stats, mine, other, *extra, scratch=scratch)
+    return call(kernel, out, 10**9, pos, q, g, stats, mine, other, *extra, far=far, scratch=scratch)
 
 
 def embed_kernel(parts, factor, w_hidden, pre, embed):
@@ -391,7 +404,9 @@
     place = jnp.stack([lax.axis_index("x"), lax.axis_index("w")]).astype(jnp.int32)
     pos = jnp.stack([lax.axis_index("z"), core, late]).astype(jnp.int32)
 
-    hidden, factor, payload = generated(place, prefix_embed, w_hidden, b_hidden.reshape(1, units), w_out, keys, values)
+    hidden, factor, payload = generated(
+        place, prefix_embed, w_hidden, b_hidden.reshape(1, units), w_out, keys, values
+    )
     kv_rows = 2 * keys.shape[0]
     mine = exchange(payload, "z")
     q = by_head(queries)

time: 157 us -> 159 us (1.013)
  no operation moved by 1% of the time
where the time goes in v6:
time: 159 us; the launch traced here: 158 us
  blocking collectives  44.9 us (28%)
  starting transfers between devices  42.6 us (27%)
  Pallas kernels  34.3 us (22%)
  waiting for transfers between devices  29 us (18%)
  local copies, waits for them, and re-layouts  5.02 us (3%)
    all_to_all x3, blocking collectives, exchange(): return lax.all_to_all(value, axes, 0, 0, tiled=True)  44.9 us
    pallas_call x12, Pallas kernels, call(): pl.pallas_call(kernel, out_shape=out_shape, in_specs=[pl.BlockSpec(memory...  31.5 us
    all_to_all x4, starting transfers between devices, exchange(): return lax.all_to_all(value, axes, 0, 0, tiled=True)  28.1 us
    all_to_all x4, waiting for transfers between devices, exchange(): return lax.all_to_all(value, axes, 0, 0, tiled=True)  20.1 us
    ppermute x6, waiting for transfers between devices, shift(): lax.ppermute(value, axis, [(i, (i + steps) % count) for i in range(count)])  8.82 us
    ppermute x6, starting transfers between devices, shift(): lax.ppermute(value, axis, [(i, (i + steps) % count) for i in range(count)])  8 us
  transfers between devices with their start and end apart: 15, of which 6 were waited for; matrix products, arithmetic and copies ran while one was open for 3% of the time, Pallas kernels for 17%

profile of v6, /device:TPU:64, one launch (start us, length us, event | category | flops | bytes accessed | tf_op | source)
XLA Modules:
  0.0 158.0 jit_solution(1237803242757468345)
XLA Ops:
  0.7 2.9 %generate.1 = (bf16[256,256]{1,0:T(8,128)(2,1)S(1)}, f32[32,256]{1,0:T(8,128)S(1)}, bf16[8,320,128]{2,1,0:T(8,128)(2,1)}) custom-call(s32[2]{0:T(128)S(1)} %pad_add_fusion.1.place, bf16[256,1024]{1,0:T(8,128)(2,1)} %embed.3, bf16[1024,256]{1,0:T(8,128)(2,1)} %w_hidden.3, f32[1,256]{1,0:T(1,128)} %bitcast.70, bf16[256,2,128]{2,1,0:T(2,128)(2,1)} %w_out.1, ...), custom_call_target="tpu_custom_call" | custom-call | flops 200000000 | bytes 2000000 | tf_op jit(solution)/shard_map/generate/pallas_call | solution.py:100
  3.6 8.2 %all-to-all-start = ((bf16[8,320,128]{2,1,0:T(8,128)(2,1)}), bf16[8,320,128]{2,1,0:T(8,128)(2,1)S(1)}, u32[]{:S(2)}, u32[]{:S(2)}) async-start(bf16[8,320,128]{2,1,0:T(8,128)(2,1)} %get-tuple-element.15), calls=%async_computation | async-start | bytes 1310720 | tf_op jit(solution)/shard_map/all_to_all | solution.py:376
  11.8 1.3 collective-permute-start.1
  13.1 1.3 collective-permute-start.2
  14.4 14.3 %all-to-all-done.mine.kv = bf16[8,320,128]{2,1,0:T(8,128)(2,1)S(1)} async-done(((bf16[8,320,128]{2,1,0:T(8,128)(2,1)}), bf16[8,320,128]{2,1,0:T(8,128)(2,1)S(1)}, u32[]{:S(2)}, u32[]{:S(2)}) %all-to-all-start) | async-done | bytes 655392 | tf_op jit(solution)/shard_map/all_to_all | solution.py:376
  28.9 1.9 %collective-permute-done.other.kv = bf16[8,320,128]{2,1,0:T(8,128)(2,1)S(1)} collective-permute-done((bf16[8,320,128]{2,1,0:T(8,128)(2,1)S(1)}, bf16[8,320,128]{2,1,0:T(8,128)(2,1)S(1)}, u32[]{:S(2)}, u32[]{:S(2)}) %collective-permute-start) | collective-permute-done | bytes 655392 | tf_op jit(solution)/shard_map/ppermute | solution.py:390
  31.6 6.7 %all-to-all-start.1 = ((bf16[16,64,128]{2,1,0:T(8,128)(2,1)}), bf16[16,64,128]{2,1,0:T(8,128)(2,1)S(1)}, u32[]{:S(2)}, u32[]{:S(2)}) async-start(bf16[16,64,128]{2,1,0:T(8,128)(2,1)} %broadcast_in_dim.9), calls=%async_computation.1 | async-start | bytes 524288 | tf_op jit(solution)/shard_map/all_to_all | solution.py:376
  40.4 2.7 %shard_map.120.refs_0_ = f32[3,8,1024]{2,1,0:T(8,128)S(1)} custom-call(s32[3]{0:T(128)S(1)} %pad_add_fusion.pos, bf16[1024,128]{1,0:T(8,128)(2,1)S(1)} %bitcast.59, bf16[1024,128]{1,0:T(8,128)(2,1)S(1)} %bitcast.63, bf16[8,320,128]{2,1,0:T(8,128)(2,1)S(1)} %all-to-all-done.mine.kv), custom_call_target="tpu_custom_call" | custom-call | flops 500000000 | bytes 1000000 | tf_op jit(solution)/shard_map/pallas_call | solution.py:268
  43.1 2.7 %shard_map.121 = f32[3,1024]{1,0:T(4,128)S(1)} custom-call(s32[3]{0:T(128)S(1)} %pad_add_fusion.pos, bf16[1024,128]{1,0:T(8,128)(2,1)S(1)} %bitcast.60, bf16[1024,128]{1,0:T(8,128)(2,1)S(1)} %bitcast.64, bf16[8,320,128]{2,1,0:T(8,128)(2,1)S(1)} %collective-permute-done.other.kv, f32[3,8,1024]{2,1,0:T(8,128)S(1)} %shard_map.120.refs_0_), custom_call_target="tpu_custom_call" | custom-call | flops 500000000 | bytes 1000000 | tf_op jit(solution)/shard_map/pallas_call | solution.py:268
  45.8 1.3 collective-permute-start.3
  47.1 2.3 %shard_map.119.state = f32[3,8,1024]{2,1,0:T(8,128)S(1)} custom-call(s32[3]{0:T(128)S(1)} %pad_add_fusion.pos, bf16[1024,128]{1,0:T(8,128)(2,1)S(1)} %bitcast.51, bf16[1024,128]{1,0:T(8,128)(2,1)S(1)} %bitcast.55, bf16[8,320,128]{2,1,0:T(8,128)(2,1)S(1)} %all-to-all-done.mine.kv, bf16[8,320,128]{2,1,0:T(8,128)(2,1)S(1)} %collective-permute-done.other.kv), custom_call_target="tpu_custom_call" | custom-call | flops 1000000000 | bytes 1000000 | tf_op jit(solution)/shard_map/pallas_call | solution.py:268
  49.4 2.1 %shard_map.122 = (bf16[2,256,128]{2,1,0:T(8,128)(2,1)S(1)}, f32[2,1024]{1,0:T(2,128)S(1)}, bf16[2,256,128]{2,1,0:T(8,128)(2,1)S(1)}) custom-call(s32[3]{0:T(128)S(1)} %pad_add_fusion.pos, bf16[1024,128]{1,0:T(8,128)(2,1)S(1)} %bitcast.52, bf16[1024,128]{1,0:T(8,128)(2,1)S(1)} %bitcast.56, bf16[2,2,256,128]{3,2,1,0:T(8,128)(2,1)S(1)} %bitcast.67, ...), custom_call_target="tpu_custom_call" | custom-call | flops 300000000 | bytes 1000000 | tf_op jit(solution)/shard_map/pallas_call | solution.py:268
  51.5 15.9 %all_to_all.35 = bf16[32,16,128]{2,1,0:T(8,128)(2,1)S(1)} all-to-all(bf16[32,16,128]{2,1,0:T(8,128)(2,1)S(1)} %bitcast.68), channel_id=1, replica_groups=mesh['y'=2,'z'=8,'c'=2,'x'=4,'w'=2] {'y','z','c'}, dimensions={0} | all-to-all | bytes 262144 | tf_op jit(solution)/shard_map/all_to_all | solution.py:376
  67.4 13.5 %all_to_all.36 = bf16[32,16,128]{2,1,0:T(8,128)(2,1)S(1)} all-to-all(bf16[32,16,128]{2,1,0:T(8,128)(2,1)S(1)} %broadcast_in_dim.10), channel_id=1, replica_groups=mesh['y'=2,'z'=8,'c'=2,'x'=4,'w'=2] {'y','z','c'}, dimensions={0} | all-to-all | bytes 262144 | tf_op jit(solution)/shard_map/all_to_all | solution.py:376
  81.2 15.5 %all_to_all.37.parts = f32[8,32,256]{2,1,0:T(8,128)S(1)} all-to-all(f32[8,32,256]{2,1,0:T(8,128)S(1)} %convolution_bitcast_fusion), channel_id=1, replica_groups=mesh['y'=2,'z'=8,'c'=2,'x'=4,'w'=2] {'x','w'}, dimensions={0} | all-to-all | bytes 524288 | tf_op jit(solution)/shard_map/all_to_all | solution.py:376
  97.6 6.0 %all-to-all-start.5 = ((bf16[32,8,128]{2,1,0:T(8,128)(2,1)}), bf16[32,8,128]{2,1,0:T(8,128)(2,1)S(1)}, u32[]{:S(2)}, u32[]{:S(2)}) async-start(bf16[32,8,128]{2,1,0:T(8,128)(2,1)} %get-tuple-element.24), calls=%async_computation.5 | async-start | bytes 131072 | tf_op jit(solution)/shard_map/all_to_all | solution.py:376
  103.6 1.3 collective-permute-start.4
  104.9 5.8 %all-to-all-done.5 = bf16[32,8,128]{2,1,0:T(8,128)(2,1)S(1)} async-done(((bf16[32,8,128]{2,1,0:T(8,128)(2,1)}), bf16[32,8,128]{2,1,0:T(8,128)(2,1)S(1)}, u32[]{:S(2)}, u32[]{:S(2)}) %all-to-all-start.5) | async-done | bytes 65568 | tf_op jit(solution)/shard_map/all_to_all | solution.py:376
  111.5 7.2 %all-to-all-start.6 = ((bf16[128,8,128]{2,1,0:T(8,128)(2,1)}), bf16[128,8,128]{2,1,0:T(8,128)(2,1)S(1)}, u32[]{:S(2)}, u32[]{:S(2)}) async-start(bf16[128,8,128]{2,1,0:T(8,128)(2,1)} %broadcast_in_dim.11), calls=%async_computation.6 | async-start | bytes 524288 | tf_op jit(solution)/shard_map/all_to_all | solution.py:376
  118.7 5.4 %shard_map.123.refs_0_ = bf16[128,1024]{1,0:T(8,128)(2,1)S(1)} custom-call(s32[3]{0:T(128)S(1)} %pad_add_fusion.pos, bf16[1024,128]{1,0:T(8,128)(2,1)S(1)} %bitcast.53, bf16[1024,128]{1,0:T(8,128)(2,1)S(1)} %bitcast.57, f32[2,1024]{1,0:T(2,128)S(1)} %get-tuple-element.16.stats, bf16[8,320,128]{2,1,0:T(8,128)(2,1)S(1)} %all-to-all-done.mine.kv, ...), custom_call_target="tpu_custom_call" | custom-call | flops 1000000000 | bytes 1000000 | tf_op jit(solution)/shard_map/pallas_call | solution.py:268
  124.8 4.7 %shard_map.125.refs_0_ = bf16[128,1024]{1,0:T(8,128)(2,1)S(1)} custom-call(s32[3]{0:T(128)S(1)} %pad_add_fusion.pos, bf16[1024,128]{1,0:T(8,128)(2,1)S(1)} %bitcast.61, bf16[1024,128]{1,0:T(8,128)(2,1)S(1)} %bitcast.65, f32[2,1024]{1,0:T(2,128)S(1)} %collective-permute-done.4.stats, bf16[8,320,128]{2,1,0:T(8,128)(2,1)S(1)} %all-to-all-done.mine.kv, ...), custom_call_target="tpu_custom_call" | custom-call | flops 1000000000 | bytes 1000000 | tf_op jit(solution)/shard_map/pallas_call | solution.py:268
  130.2 4.7 %shard_map.126 = bf16[128,1024]{1,0:T(8,128)(2,1)S(1)} custom-call(s32[3]{0:T(128)S(1)} %pad_add_fusion.pos, bf16[1024,128]{1,0:T(8,128)(2,1)S(1)} %bitcast.62, bf16[1024,128]{1,0:T(8,128)(2,1)S(1)} %bitcast.66, f32[2,1024]{1,0:T(2,128)S(1)} %collective-permute-done.4.stats, bf16[8,320,128]{2,1,0:T(8,128)(2,1)S(1)} %all-to-all-done.mine.kv, ...), custom_call_target="tpu_custom_call" | custom-call | flops 1000000000 | bytes 1000000 | tf_op jit(solution)/shard_map/pallas_call | solution.py:268
  134.9 1.3 collective-permute-start.5
  136.2 1.6 %shard_map.124 = bf16[128,1024]{1,0:T(8,128)(2,1)S(1)} custom-call(s32[3]{0:T(128)S(1)} %pad_add_fusion.pos, bf16[1024,128]{1,0:T(8,128)(2,1)S(1)} %bitcast.54, bf16[1024,128]{1,0:T(8,128)(2,1)S(1)} %bitcast.58, f32[2,1024]{1,0:T(2,128)S(1)} %get-tuple-element.16.stats, bf16[8,320,128]{2,1,0:T(8,128)(2,1)S(1)} %all-to-all-done.mine.kv, ...), custom_call_target="tpu_custom_call" | custom-call | flops 1000000000 | bytes 1000000 | tf_op jit(solution)/shard_map/pallas_call | solution.py:268
  137.8 3.2 %collective-permute-start.6 = (bf16[32,256]{1,0:T(8,128)(2,1)S(1)}, bf16[32,256]{1,0:T(8,128)(2,1)S(1)}, u32[]{:S(2)}, u32[]{:S(2)}) collective-permute-start(bf16[32,256]{1,0:T(8,128)(2,1)S(1)} %get-tuple-element.21), channel_id=1, source_target_pairs={{0,1},{1,0},{2,3},{3,2},{4,5},{5,4},{6,7},{7,6},{8,9},{9,8},{10,11... | collective-permute-start | bytes 49160 | tf_op jit(solution)/shard_map/ppermute | solution.py:390
  140.9 4.5 %collective-permute-done.6 = bf16[32,256]{1,0:T(8,128)(2,1)S(1)} collective-permute-done((bf16[32,256]{1,0:T(8,128)(2,1)S(1)}, bf16[32,256]{1,0:T(8,128)(2,1)S(1)}, u32[]{:S(2)}, u32[]{:S(2)}) %collective-permute-start.6) | collective-permute-done | bytes 16416 | tf_op jit(solution)/shard_map/ppermute | solution.py:390
  145.5 3.3 %collective-permute-start.9 = (bf16[64,256]{1,0:T(8,128)(2,1)S(1)}, bf16[64,256]{1,0:T(8,128)(2,1)S(1)}, u32[]{:S(2)}, u32[]{:S(2)}) collective-permute-start(bf16[64,256]{1,0:T(8,128)(2,1)S(1)} %constant_dynamic-update-slice_fusion.refs_0_), channel_id=1, source_target_pairs={{0,6},{2,0},{4,2},{6,4},{1,7},{3,1},{5,3},{7,5},{8,14},{10,8},{12,... | collective-permute-start | bytes 98312 | tf_op jit(solution)/shard_map/ppermute | solution.py:390
  149.2 1.1 collective-permute-start.7
  151.1 1.1 shard_map.127
  152.1 2.1 %collective-permute-done.8.refs_2_ = bf16[64,256]{1,0:T(8,128)(2,1)S(1)} collective-permute-done((bf16[64,256]{1,0:T(8,128)(2,1)S(1)}, bf16[64,256]{1,0:T(8,128)(2,1)S(1)}, u32[]{:S(2)}, u32[]{:S(2)}) %collective-permute-start.8) | collective-permute-done | bytes 32800 | tf_op jit(solution)/shard_map/ppermute | solution.py:390
  154.6 1.9 %shard_map.129 = (f32[1024,256]{1,0:T(8,128)}, f32[256]{0:T(256)}) custom-call(s32[2]{0:T(128)S(1)} %pad_add_fusion.1.place, bf16[256,1024]{1,0:T(8,128)(2,1)S(1)} %copy-done.1, bf16[64,256]{1,0:T(8,128)(2,1)S(1)} %constant_dynamic-update-slice_fusion.refs_0_, bf16[64,256]{1,0:T(8,128)(2,1)S(1)} %collective-permute-done.7.refs_1_, ...), custom_call_target="tpu_custom_call" | custom-call | flops 200000000 | bytes 1000000 | tf_op jit(solution)/shard_map/pallas_call | solution.py:268
  156.4 1.6 %shard_map.130 = f32[256,1024]{1,0:T(8,128)} custom-call(s32[3]{0:T(128)S(1)} %pad_add_fusion.pos, bf16[128,8,128]{2,1,0:T(8,128)(2,1)S(1)} %all-to-all-done.6.near, bf16[128,8,128]{2,1,0:T(8,128)(2,1)S(1)} %collective-permute-done.10.far), custom_call_target="tpu_custom_call" | custom-call | flops 1000000 | bytes 1000000 | tf_op jit(solution)/shard_map/pallas_call | solution.py:268
  (46 shorter events, 8.0 us)
Async XLA Ops:
  3.6 8.3 %copy-start.5 = (bf16[128,1024]{1,0:T(8,128)(2,1)S(1)}, bf16[128,1024]{1,0:T(8,128)(2,1)}, u32[]{:S(2)}) copy-start(bf16[128,1024]{1,0:T(8,128)(2,1)} %param.12) | copy-start | bytes 786436
  3.6 9.5 %copy-start.6 = (bf16[128,1024]{1,0:T(8,128)(2,1)S(1)}, bf16[128,1024]{1,0:T(8,128)(2,1)}, u32[]{:S(2)}) copy-start(bf16[128,1024]{1,0:T(8,128)(2,1)} %param.15) | copy-start | bytes 786436
  3.6 25.2 %all-to-all-start = ((bf16[8,320,128]{2,1,0:T(8,128)(2,1)}), bf16[8,320,128]{2,1,0:T(8,128)(2,1)S(1)}, u32[]{:S(2)}, u32[]{:S(2)}) async-start(bf16[8,320,128]{2,1,0:T(8,128)(2,1)} %get-tuple-element.15), calls=%async_computation | async-start | bytes 1310720 | tf_op jit(solution)/shard_map/all_to_all | solution.py:376
  11.8 26.5 %collective-permute-start.1 = (bf16[128,1024]{1,0:T(8,128)(2,1)S(1)}, bf16[128,1024]{1,0:T(8,128)(2,1)}, u32[]{:S(2)}, u32[]{:S(2)}) collective-permute-start(bf16[128,1024]{1,0:T(8,128)(2,1)S(1)} %copy-done.5), channel_id=1, source_target_pairs={{128,0},{129,1},{130,2},{131,3},{132,4},{133,5},{134,6},{135,7},{1... | collective-permute-start | bytes 786440 | tf_op jit(solution)/shard_map/ppermute | solution.py:414
  13.1 26.2 %collective-permute-start.2 = (bf16[128,1024]{1,0:T(8,128)(2,1)S(1)}, bf16[128,1024]{1,0:T(8,128)(2,1)}, u32[]{:S(2)}, u32[]{:S(2)}) collective-permute-start(bf16[128,1024]{1,0:T(8,128)(2,1)S(1)} %copy-done.6), channel_id=1, source_target_pairs={{128,0},{129,1},{130,2},{131,3},{132,4},{133,5},{134,6},{135,7},{1... | collective-permute-start | bytes 786440 | tf_op jit(solution)/shard_map/ppermute | solution.py:415
  28.7 2.1 %collective-permute-start = (bf16[8,320,128]{2,1,0:T(8,128)(2,1)S(1)}, bf16[8,320,128]{2,1,0:T(8,128)(2,1)S(1)}, u32[]{:S(2)}, u32[]{:S(2)}) collective-permute-start(bf16[8,320,128]{2,1,0:T(8,128)(2,1)S(1)} %all-to-all-done.mine.kv), channel_id=1, source_target_pairs={{0,8},{8,0},{1,9},{9,1},{2,10},{10,2},{3,11},{11,3},{4,12},{12,4},... | collective-permute-start | bytes 1966088 | tf_op jit(solution)/shard_map/ppermute | solution.py:390
  31.6 17.8 %all-to-all-start.1 = ((bf16[16,64,128]{2,1,0:T(8,128)(2,1)}), bf16[16,64,128]{2,1,0:T(8,128)(2,1)S(1)}, u32[]{:S(2)}, u32[]{:S(2)}) async-start(bf16[16,64,128]{2,1,0:T(8,128)(2,1)} %broadcast_in_dim.9), calls=%async_computation.1 | async-start | bytes 524288 | tf_op jit(solution)/shard_map/all_to_all | solution.py:376
  45.8 3.6 %collective-permute-start.3 = (f32[3,1024]{1,0:T(4,128)S(1)}, f32[3,1024]{1,0:T(4,128)S(1)}, u32[]{:S(2)}, u32[]{:S(2)}) collective-permute-start(f32[3,1024]{1,0:T(4,128)S(1)} %shard_map.121), channel_id=1, source_target_pairs={{0,128},{1,129},{2,130},{3,131},{4,132},{5,133},{6,134},{7,135},{8... | collective-permute-start | bytes 36872 | tf_op jit(solution)/shard_map/ppermute | solution.py:424
  67.4 13.5 %copy-start.4 = (bf16[256,2,128]{2,1,0:T(2,128)(2,1)S(1)}, bf16[256,2,128]{2,1,0:T(2,128)(2,1)}, u32[]{:S(2)}) copy-start(bf16[256,2,128]{2,1,0:T(2,128)(2,1)} %w_out.1) | copy-start | bytes 393220
  81.0 15.8 %copy-start = (bf16[1024,256]{1,0:T(8,128)(2,1)S(1)}, bf16[1024,256]{1,0:T(8,128)(2,1)}, u32[]{:S(2)}) copy-start(bf16[1024,256]{1,0:T(8,128)(2,1)} %w_hidden.3) | copy-start | bytes 1572868
  97.6 13.1 %all-to-all-start.5 = ((bf16[32,8,128]{2,1,0:T(8,128)(2,1)}), bf16[32,8,128]{2,1,0:T(8,128)(2,1)S(1)}, u32[]{:S(2)}, u32[]{:S(2)}) async-start(bf16[32,8,128]{2,1,0:T(8,128)(2,1)} %get-tuple-element.24), calls=%async_computation.5 | async-start | bytes 131072 | tf_op jit(solution)/shard_map/all_to_all | solution.py:376
  103.6 21.2 %collective-permute-start.4 = (f32[2,1024]{1,0:T(2,128)S(1)}, f32[2,1024]{1,0:T(2,128)S(1)}, u32[]{:S(2)}, u32[]{:S(2)}) collective-permute-start(f32[2,1024]{1,0:T(2,128)S(1)} %get-tuple-element.16.stats), channel_id=1, source_target_pairs={{128,0},{129,1},{130,2},{131,3},{132,4},{133,5},{134,6},{135,7},{1... | collective-permute-start | bytes 24584 | tf_op jit(solution)/shard_map/ppermute | solution.py:427
  111.5 38.8 %all-to-all-start.6 = ((bf16[128,8,128]{2,1,0:T(8,128)(2,1)}), bf16[128,8,128]{2,1,0:T(8,128)(2,1)S(1)}, u32[]{:S(2)}, u32[]{:S(2)}) async-start(bf16[128,8,128]{2,1,0:T(8,128)(2,1)} %broadcast_in_dim.11), calls=%async_computation.6 | async-start | bytes 524288 | tf_op jit(solution)/shard_map/all_to_all | solution.py:376
  124.1 0.7 copy-start.2
  129.5 0.7 copy-start.3
  134.9 15.4 %collective-permute-start.5 = (bf16[128,1024]{1,0:T(8,128)(2,1)S(1)}, bf16[128,1024]{1,0:T(8,128)(2,1)S(1)}, u32[]{:S(2)}, u32[]{:S(2)}) collective-permute-start(bf16[128,1024]{1,0:T(8,128)(2,1)S(1)} %shard_map.126), channel_id=1, source_target_pairs={{0,128},{1,129},{2,130},{3,131},{4,132},{5,133},{6,134},{7,135},{8... | collective-permute-start | bytes 786440 | tf_op jit(solution)/shard_map/ppermute | solution.py:435
  137.8 7.7 %collective-permute-start.6 = (bf16[32,256]{1,0:T(8,128)(2,1)S(1)}, bf16[32,256]{1,0:T(8,128)(2,1)S(1)}, u32[]{:S(2)}, u32[]{:S(2)}) collective-permute-start(bf16[32,256]{1,0:T(8,128)(2,1)S(1)} %get-tuple-element.21), channel_id=1, source_target_pairs={{0,1},{1,0},{2,3},{3,2},{4,5},{5,4},{6,7},{7,6},{8,9},{9,8},{10,11... | collective-permute-start | bytes 49160 | tf_op jit(solution)/shard_map/ppermute | solution.py:390
  145.5 6.7 %collective-permute-start.9 = (bf16[64,256]{1,0:T(8,128)(2,1)S(1)}, bf16[64,256]{1,0:T(8,128)(2,1)S(1)}, u32[]{:S(2)}, u32[]{:S(2)}) collective-permute-start(bf16[64,256]{1,0:T(8,128)(2,1)S(1)} %constant_dynamic-update-slice_fusion.refs_0_), channel_id=1, source_target_pairs={{0,6},{2,0},{4,2},{6,4},{1,7},{3,1},{5,3},{7,5},{8,14},{10,8},{12,... | collective-permute-start | bytes 98312 | tf_op jit(solution)/shard_map/ppermute | solution.py:390
  148.8 5.4 %collective-permute-start.8 = (bf16[64,256]{1,0:T(8,128)(2,1)S(1)}, bf16[64,256]{1,0:T(8,128)(2,1)S(1)}, u32[]{:S(2)}, u32[]{:S(2)}) collective-permute-start(bf16[64,256]{1,0:T(8,128)(2,1)S(1)} %constant_dynamic-update-slice_fusion.refs_0_), channel_id=1, source_target_pairs={{0,4},{2,6},{4,0},{6,2},{1,5},{3,7},{5,1},{7,3},{8,12},{10,14},{12... | collective-permute-start | bytes 98312 | tf_op jit(solution)/shard_map/ppermute | solution.py:390
  149.2 5.4 %collective-permute-start.7 = (bf16[64,256]{1,0:T(8,128)(2,1)S(1)}, bf16[64,256]{1,0:T(8,128)(2,1)S(1)}, u32[]{:S(2)}, u32[]{:S(2)}) collective-permute-start(bf16[64,256]{1,0:T(8,128)(2,1)S(1)} %constant_dynamic-update-slice_fusion.refs_0_), channel_id=1, source_target_pairs={{0,2},{2,4},{4,6},{6,0},{1,3},{3,5},{5,7},{7,1},{8,10},{10,12},{12... | collective-permute-start | bytes 98312 | tf_op jit(solution)/shard_map/ppermute | solution.py:390
  150.3 6.1 %collective-permute-start.10 = (bf16[128,8,128]{2,1,0:T(8,128)(2,1)S(1)}, bf16[128,8,128]{2,1,0:T(8,128)(2,1)S(1)}, u32[]{:S(2)}, u32[]{:S(2)}) collective-permute-start(bf16[128,8,128]{2,1,0:T(8,128)(2,1)S(1)} %all-to-all-done.6.near), channel_id=1, source_target_pairs={{0,8},{8,0},{1,9},{9,1},{2,10},{10,2},{3,11},{11,3},{4,12},{12,4},... | collective-permute-start | bytes 786440 | tf_op jit(solution)/shard_map/ppermute | solution.py:390
  151.1 3.5 %copy-start.1 = (bf16[256,1024]{1,0:T(8,128)(2,1)S(1)}, bf16[256,1024]{1,0:T(8,128)(2,1)}, u32[]{:S(2)}) copy-start(bf16[256,1024]{1,0:T(8,128)(2,1)} %embed.3) | copy-start | bytes 1572868

commit v7 on v6

--- a/solution.py
+++ b/solution.py
@@ -326,14 +326,13 @@
 def joined_kernel(heads, pos, near, far, out):
     wide = out.shape[1] // HD
     per_head = near.shape[0] // heads
-    first = pos[1] == 0
-    for t in range(near.shape[0]):
-        pair = (near[t].astype(F32), far[t].astype(F32))
-        for side in range(2):
-            tile = t // per_head * 2 * per_head + side * per_head + t % per_head
-            down, right = tile // wide * TALL, tile % wide * HD
-            value = jnp.where(first, pair[side], pair[1 - side])
-            out[down : down + TALL, right : right + HD] = value
+    deep = per_head // wide * TALL
+    for side, source in ((pos[1], near), (1 - pos[1], far)):
+        for t in range(near.shape[0]):
+            down = t // per_head * 2 * deep + t % per_head // wide * TALL
+            at = pl.multiple_of(down + side * deep, TALL)
+            right = t % wide * HD
+            out[pl.ds(at, TALL), right : right + HD] = source[t].astype(F32)
 
 
 def joined(pos, near, far, heads, npre, emb):

time: 159 us -> 159 us (level)
  no operation moved by 1% of the time
where the time goes in v7:
time: 159 us; the launch traced here: 158 us
  blocking collectives  44.9 us (28%)
  starting transfers between devices  42.6 us (27%)
  Pallas kernels  34.4 us (22%)
  waiting for transfers between devices  29 us (18%)
  local copies, waits for them, and re-layouts  5.02 us (3%)
    all_to_all x3, blocking collectives, exchange(): return lax.all_to_all(value, axes, 0, 0, tiled=True)  44.9 us
    pallas_call x12, Pallas kernels, call(): pl.pallas_call(kernel, out_shape=out_shape, in_specs=[pl.BlockSpec(memory...  31.5 us
    all_to_all x4, starting transfers between devices, exchange(): return lax.all_to_all(value, axes, 0, 0, tiled=True)  28.1 us
    all_to_all x4, waiting for transfers between devices, exchange(): return lax.all_to_all(value, axes, 0, 0, tiled=True)  20.1 us
    ppermute x6, waiting for transfers between devices, shift(): lax.ppermute(value, axis, [(i, (i + steps) % count) for i in range(count)])  8.82 us
    ppermute x6, starting transfers between devices, shift(): lax.ppermute(value, axis, [(i, (i + steps) % count) for i in range(count)])  8 us
  transfers between devices with their start and end apart: 15, of which 6 were waited for; matrix products, arithmetic and copies ran while one was open for 3% of the time, Pallas kernels for 17%

profile of v7, /device:TPU:64, one launch (start us, length us, event | category | flops | bytes accessed | tf_op | source)
XLA Modules:
  0.0 158.0 jit_solution(12197960724500883661)
XLA Ops:
  0.7 2.9 %generate.1 = (bf16[256,256]{1,0:T(8,128)(2,1)S(1)}, f32[32,256]{1,0:T(8,128)S(1)}, bf16[8,320,128]{2,1,0:T(8,128)(2,1)}) custom-call(s32[2]{0:T(128)S(1)} %pad_add_fusion.1.place, bf16[256,1024]{1,0:T(8,128)(2,1)} %embed.3, bf16[1024,256]{1,0:T(8,128)(2,1)} %w_hidden.3, f32[1,256]{1,0:T(1,128)} %bitcast.70, bf16[256,2,128]{2,1,0:T(2,128)(2,1)} %w_out.1, ...), custom_call_target="tpu_custom_call" | custom-call | flops 200000000 | bytes 2000000 | tf_op jit(solution)/shard_map/generate/pallas_call | solution.py:100
  3.6 8.2 %all-to-all-start = ((bf16[8,320,128]{2,1,0:T(8,128)(2,1)}), bf16[8,320,128]{2,1,0:T(8,128)(2,1)S(1)}, u32[]{:S(2)}, u32[]{:S(2)}) async-start(bf16[8,320,128]{2,1,0:T(8,128)(2,1)} %get-tuple-element.15), calls=%async_computation | async-start | bytes 1310720 | tf_op jit(solution)/shard_map/all_to_all | solution.py:375
  11.8 1.3 collective-permute-start.1
  13.1 1.3 collective-permute-start.2
  14.4 14.3 %all-to-all-done.mine.kv = bf16[8,320,128]{2,1,0:T(8,128)(2,1)S(1)} async-done(((bf16[8,320,128]{2,1,0:T(8,128)(2,1)}), bf16[8,320,128]{2,1,0:T(8,128)(2,1)S(1)}, u32[]{:S(2)}, u32[]{:S(2)}) %all-to-all-start) | async-done | bytes 655392 | tf_op jit(solution)/shard_map/all_to_all | solution.py:375
  28.9 1.9 %collective-permute-done.other.kv = bf16[8,320,128]{2,1,0:T(8,128)(2,1)S(1)} collective-permute-done((bf16[8,320,128]{2,1,0:T(8,128)(2,1)S(1)}, bf16[8,320,128]{2,1,0:T(8,128)(2,1)S(1)}, u32[]{:S(2)}, u32[]{:S(2)}) %collective-permute-start) | collective-permute-done | bytes 655392 | tf_op jit(solution)/shard_map/ppermute | solution.py:389
  31.6 6.7 %all-to-all-start.1 = ((bf16[16,64,128]{2,1,0:T(8,128)(2,1)}), bf16[16,64,128]{2,1,0:T(8,128)(2,1)S(1)}, u32[]{:S(2)}, u32[]{:S(2)}) async-start(bf16[16,64,128]{2,1,0:T(8,128)(2,1)} %broadcast_in_dim.9), calls=%async_computation.1 | async-start | bytes 524288 | tf_op jit(solution)/shard_map/all_to_all | solution.py:375
  40.4 2.7 %shard_map.120.refs_0_ = f32[3,8,1024]{2,1,0:T(8,128)S(1)} custom-call(s32[3]{0:T(128)S(1)} %pad_add_fusion.pos, bf16[1024,128]{1,0:T(8,128)(2,1)S(1)} %bitcast.59, bf16[1024,128]{1,0:T(8,128)(2,1)S(1)} %bitcast.63, bf16[8,320,128]{2,1,0:T(8,128)(2,1)S(1)} %all-to-all-done.mine.kv), custom_call_target="tpu_custom_call" | custom-call | flops 500000000 | bytes 1000000 | tf_op jit(solution)/shard_map/pallas_call | solution.py:268
  43.1 2.7 %shard_map.121 = f32[3,1024]{1,0:T(4,128)S(1)} custom-call(s32[3]{0:T(128)S(1)} %pad_add_fusion.pos, bf16[1024,128]{1,0:T(8,128)(2,1)S(1)} %bitcast.60, bf16[1024,128]{1,0:T(8,128)(2,1)S(1)} %bitcast.64, bf16[8,320,128]{2,1,0:T(8,128)(2,1)S(1)} %collective-permute-done.other.kv, f32[3,8,1024]{2,1,0:T(8,128)S(1)} %shard_map.120.refs_0_), custom_call_target="tpu_custom_call" | custom-call | flops 500000000 | bytes 1000000 | tf_op jit(solution)/shard_map/pallas_call | solution.py:268
  45.8 1.3 collective-permute-start.3
  47.1 2.3 %shard_map.119.state = f32[3,8,1024]{2,1,0:T(8,128)S(1)} custom-call(s32[3]{0:T(128)S(1)} %pad_add_fusion.pos, bf16[1024,128]{1,0:T(8,128)(2,1)S(1)} %bitcast.51, bf16[1024,128]{1,0:T(8,128)(2,1)S(1)} %bitcast.55, bf16[8,320,128]{2,1,0:T(8,128)(2,1)S(1)} %all-to-all-done.mine.kv, bf16[8,320,128]{2,1,0:T(8,128)(2,1)S(1)} %collective-permute-done.other.kv), custom_call_target="tpu_custom_call" | custom-call | flops 1000000000 | bytes 1000000 | tf_op jit(solution)/shard_map/pallas_call | solution.py:268
  49.4 2.1 %shard_map.122 = (bf16[2,256,128]{2,1,0:T(8,128)(2,1)S(1)}, f32[2,1024]{1,0:T(2,128)S(1)}, bf16[2,256,128]{2,1,0:T(8,128)(2,1)S(1)}) custom-call(s32[3]{0:T(128)S(1)} %pad_add_fusion.pos, bf16[1024,128]{1,0:T(8,128)(2,1)S(1)} %bitcast.52, bf16[1024,128]{1,0:T(8,128)(2,1)S(1)} %bitcast.56, bf16[2,2,256,128]{3,2,1,0:T(8,128)(2,1)S(1)} %bitcast.67, ...), custom_call_target="tpu_custom_call" | custom-call | flops 300000000 | bytes 1000000 | tf_op jit(solution)/shard_map/pallas_call | solution.py:268
  51.5 15.9 %all_to_all.35 = bf16[32,16,128]{2,1,0:T(8,128)(2,1)S(1)} all-to-all(bf16[32,16,128]{2,1,0:T(8,128)(2,1)S(1)} %bitcast.68), channel_id=1, replica_groups=mesh['y'=2,'z'=8,'c'=2,'x'=4,'w'=2] {'y','z','c'}, dimensions={0} | all-to-all | bytes 262144 | tf_op jit(solution)/shard_map/all_to_all | solution.py:375
  67.4 13.5 %all_to_all.36 = bf16[32,16,128]{2,1,0:T(8,128)(2,1)S(1)} all-to-all(bf16[32,16,128]{2,1,0:T(8,128)(2,1)S(1)} %broadcast_in_dim.10), channel_id=1, replica_groups=mesh['y'=2,'z'=8,'c'=2,'x'=4,'w'=2] {'y','z','c'}, dimensions={0} | all-to-all | bytes 262144 | tf_op jit(solution)/shard_map/all_to_all | solution.py:375
  81.2 15.5 %all_to_all.37.parts = f32[8,32,256]{2,1,0:T(8,128)S(1)} all-to-all(f32[8,32,256]{2,1,0:T(8,128)S(1)} %convolution_bitcast_fusion), channel_id=1, replica_groups=mesh['y'=2,'z'=8,'c'=2,'x'=4,'w'=2] {'x','w'}, dimensions={0} | all-to-all | bytes 524288 | tf_op jit(solution)/shard_map/all_to_all | solution.py:375
  97.6 6.0 %all-to-all-start.5 = ((bf16[32,8,128]{2,1,0:T(8,128)(2,1)}), bf16[32,8,128]{2,1,0:T(8,128)(2,1)S(1)}, u32[]{:S(2)}, u32[]{:S(2)}) async-start(bf16[32,8,128]{2,1,0:T(8,128)(2,1)} %get-tuple-element.24), calls=%async_computation.5 | async-start | bytes 131072 | tf_op jit(solution)/shard_map/all_to_all | solution.py:375
  103.6 1.3 collective-permute-start.4
  104.9 5.8 %all-to-all-done.5 = bf16[32,8,128]{2,1,0:T(8,128)(2,1)S(1)} async-done(((bf16[32,8,128]{2,1,0:T(8,128)(2,1)}), bf16[32,8,128]{2,1,0:T(8,128)(2,1)S(1)}, u32[]{:S(2)}, u32[]{:S(2)}) %all-to-all-start.5) | async-done | bytes 65568 | tf_op jit(solution)/shard_map/all_to_all | solution.py:375
  111.5 7.2 %all-to-all-start.6 = ((bf16[128,8,128]{2,1,0:T(8,128)(2,1)}), bf16[128,8,128]{2,1,0:T(8,128)(2,1)S(1)}, u32[]{:S(2)}, u32[]{:S(2)}) async-start(bf16[128,8,128]{2,1,0:T(8,128)(2,1)} %broadcast_in_dim.11), calls=%async_computation.6 | async-start | bytes 524288 | tf_op jit(solution)/shard_map/all_to_all | solution.py:375
  118.7 5.4 %shard_map.123.refs_0_ = bf16[128,1024]{1,0:T(8,128)(2,1)S(1)} custom-call(s32[3]{0:T(128)S(1)} %pad_add_fusion.pos, bf16[1024,128]{1,0:T(8,128)(2,1)S(1)} %bitcast.53, bf16[1024,128]{1,0:T(8,128)(2,1)S(1)} %bitcast.57, f32[2,1024]{1,0:T(2,128)S(1)} %get-tuple-element.16.stats, bf16[8,320,128]{2,1,0:T(8,128)(2,1)S(1)} %all-to-all-done.mine.kv, ...), custom_call_target="tpu_custom_call" | custom-call | flops 1000000000 | bytes 1000000 | tf_op jit(solution)/shard_map/pallas_call | solution.py:268
  124.8 4.7 %shard_map.125.refs_0_ = bf16[128,1024]{1,0:T(8,128)(2,1)S(1)} custom-call(s32[3]{0:T(128)S(1)} %pad_add_fusion.pos, bf16[1024,128]{1,0:T(8,128)(2,1)S(1)} %bitcast.61, bf16[1024,128]{1,0:T(8,128)(2,1)S(1)} %bitcast.65, f32[2,1024]{1,0:T(2,128)S(1)} %collective-permute-done.4.stats, bf16[8,320,128]{2,1,0:T(8,128)(2,1)S(1)} %all-to-all-done.mine.kv, ...), custom_call_target="tpu_custom_call" | custom-call | flops 1000000000 | bytes 1000000 | tf_op jit(solution)/shard_map/pallas_call | solution.py:268
  130.2 4.7 %shard_map.126 = bf16[128,1024]{1,0:T(8,128)(2,1)S(1)} custom-call(s32[3]{0:T(128)S(1)} %pad_add_fusion.pos, bf16[1024,128]{1,0:T(8,128)(2,1)S(1)} %bitcast.62, bf16[1024,128]{1,0:T(8,128)(2,1)S(1)} %bitcast.66, f32[2,1024]{1,0:T(2,128)S(1)} %collective-permute-done.4.stats, bf16[8,320,128]{2,1,0:T(8,128)(2,1)S(1)} %all-to-all-done.mine.kv, ...), custom_call_target="tpu_custom_call" | custom-call | flops 1000000000 | bytes 1000000 | tf_op jit(solution)/shard_map/pallas_call | solution.py:268
  134.9 1.3 collective-permute-start.5
  136.2 1.6 %shard_map.124 = bf16[128,1024]{1,0:T(8,128)(2,1)S(1)} custom-call(s32[3]{0:T(128)S(1)} %pad_add_fusion.pos, bf16[1024,128]{1,0:T(8,128)(2,1)S(1)} %bitcast.54, bf16[1024,128]{1,0:T(8,128)(2,1)S(1)} %bitcast.58, f32[2,1024]{1,0:T(2,128)S(1)} %get-tuple-element.16.stats, bf16[8,320,128]{2,1,0:T(8,128)(2,1)S(1)} %all-to-all-done.mine.kv, ...), custom_call_target="tpu_custom_call" | custom-call | flops 1000000000 | bytes 1000000 | tf_op jit(solution)/shard_map/pallas_call | solution.py:268
  137.8 3.2 %collective-permute-start.6 = (bf16[32,256]{1,0:T(8,128)(2,1)S(1)}, bf16[32,256]{1,0:T(8,128)(2,1)S(1)}, u32[]{:S(2)}, u32[]{:S(2)}) collective-permute-start(bf16[32,256]{1,0:T(8,128)(2,1)S(1)} %get-tuple-element.21), channel_id=1, source_target_pairs={{0,1},{1,0},{2,3},{3,2},{4,5},{5,4},{6,7},{7,6},{8,9},{9,8},{10,11... | collective-permute-start | bytes 49160 | tf_op jit(solution)/shard_map/ppermute | solution.py:389
  140.9 4.5 %collective-permute-done.6 = bf16[32,256]{1,0:T(8,128)(2,1)S(1)} collective-permute-done((bf16[32,256]{1,0:T(8,128)(2,1)S(1)}, bf16[32,256]{1,0:T(8,128)(2,1)S(1)}, u32[]{:S(2)}, u32[]{:S(2)}) %collective-permute-start.6) | collective-permute-done | bytes 16416 | tf_op jit(solution)/shard_map/ppermute | solution.py:389
  145.5 3.3 %collective-permute-start.9 = (bf16[64,256]{1,0:T(8,128)(2,1)S(1)}, bf16[64,256]{1,0:T(8,128)(2,1)S(1)}, u32[]{:S(2)}, u32[]{:S(2)}) collective-permute-start(bf16[64,256]{1,0:T(8,128)(2,1)S(1)} %constant_dynamic-update-slice_fusion.refs_0_), channel_id=1, source_target_pairs={{0,6},{2,0},{4,2},{6,4},{1,7},{3,1},{5,3},{7,5},{8,14},{10,8},{12,... | collective-permute-start | bytes 98312 | tf_op jit(solution)/shard_map/ppermute | solution.py:389
  149.2 1.1 collective-permute-start.7
  151.1 1.1 shard_map.127
  152.1 2.1 %collective-permute-done.8.refs_2_ = bf16[64,256]{1,0:T(8,128)(2,1)S(1)} collective-permute-done((bf16[64,256]{1,0:T(8,128)(2,1)S(1)}, bf16[64,256]{1,0:T(8,128)(2,1)S(1)}, u32[]{:S(2)}, u32[]{:S(2)}) %collective-permute-start.8) | collective-permute-done | bytes 32800 | tf_op jit(solution)/shard_map/ppermute | solution.py:389
  154.6 1.9 %shard_map.129 = (f32[1024,256]{1,0:T(8,128)}, f32[256]{0:T(256)}) custom-call(s32[2]{0:T(128)S(1)} %pad_add_fusion.1.place, bf16[256,1024]{1,0:T(8,128)(2,1)S(1)} %copy-done.1, bf16[64,256]{1,0:T(8,128)(2,1)S(1)} %constant_dynamic-update-slice_fusion.refs_0_, bf16[64,256]{1,0:T(8,128)(2,1)S(1)} %collective-permute-done.7.refs_1_, ...), custom_call_target="tpu_custom_call" | custom-call | flops 200000000 | bytes 1000000 | tf_op jit(solution)/shard_map/pallas_call | solution.py:268
  156.4 1.6 %shard_map.130 = f32[256,1024]{1,0:T(8,128)} custom-call(s32[3]{0:T(128)S(1)} %pad_add_fusion.pos, bf16[128,8,128]{2,1,0:T(8,128)(2,1)S(1)} %all-to-all-done.6.near, bf16[128,8,128]{2,1,0:T(8,128)(2,1)S(1)} %collective-permute-done.10.far), custom_call_target="tpu_custom_call" | custom-call | flops 1000000 | bytes 1000000 | tf_op jit(solution)/shard_map/pallas_call | solution.py:268
  (46 shorter events, 8.0 us)
Async XLA Ops:
  3.6 8.3 %copy-start.5 = (bf16[128,1024]{1,0:T(8,128)(2,1)S(1)}, bf16[128,1024]{1,0:T(8,128)(2,1)}, u32[]{:S(2)}) copy-start(bf16[128,1024]{1,0:T(8,128)(2,1)} %param.12) | copy-start | bytes 786436
  3.6 9.5 %copy-start.6 = (bf16[128,1024]{1,0:T(8,128)(2,1)S(1)}, bf16[128,1024]{1,0:T(8,128)(2,1)}, u32[]{:S(2)}) copy-start(bf16[128,1024]{1,0:T(8,128)(2,1)} %param.15) | copy-start | bytes 786436
  3.6 25.2 %all-to-all-start = ((bf16[8,320,128]{2,1,0:T(8,128)(2,1)}), bf16[8,320,128]{2,1,0:T(8,128)(2,1)S(1)}, u32[]{:S(2)}, u32[]{:S(2)}) async-start(bf16[8,320,128]{2,1,0:T(8,128)(2,1)} %get-tuple-element.15), calls=%async_computation | async-start | bytes 1310720 | tf_op jit(solution)/shard_map/all_to_all | solution.py:375
  11.8 26.5 %collective-permute-start.1 = (bf16[128,1024]{1,0:T(8,128)(2,1)S(1)}, bf16[128,1024]{1,0:T(8,128)(2,1)}, u32[]{:S(2)}, u32[]{:S(2)}) collective-permute-start(bf16[128,1024]{1,0:T(8,128)(2,1)S(1)} %copy-done.5), channel_id=1, source_target_pairs={{128,0},{129,1},{130,2},{131,3},{132,4},{133,5},{134,6},{135,7},{1... | collective-permute-start | bytes 786440 | tf_op jit(solution)/shard_map/ppermute | solution.py:413
  13.1 26.2 %collective-permute-start.2 = (bf16[128,1024]{1,0:T(8,128)(2,1)S(1)}, bf16[128,1024]{1,0:T(8,128)(2,1)}, u32[]{:S(2)}, u32[]{:S(2)}) collective-permute-start(bf16[128,1024]{1,0:T(8,128)(2,1)S(1)} %copy-done.6), channel_id=1, source_target_pairs={{128,0},{129,1},{130,2},{131,3},{132,4},{133,5},{134,6},{135,7},{1... | collective-permute-start | bytes 786440 | tf_op jit(solution)/shard_map/ppermute | solution.py:414
  28.7 2.1 %collective-permute-start = (bf16[8,320,128]{2,1,0:T(8,128)(2,1)S(1)}, bf16[8,320,128]{2,1,0:T(8,128)(2,1)S(1)}, u32[]{:S(2)}, u32[]{:S(2)}) collective-permute-start(bf16[8,320,128]{2,1,0:T(8,128)(2,1)S(1)} %all-to-all-done.mine.kv), channel_id=1, source_target_pairs={{0,8},{8,0},{1,9},{9,1},{2,10},{10,2},{3,11},{11,3},{4,12},{12,4},... | collective-permute-start | bytes 1966088 | tf_op jit(solution)/shard_map/ppermute | solution.py:389
  31.6 17.8 %all-to-all-start.1 = ((bf16[16,64,128]{2,1,0:T(8,128)(2,1)}), bf16[16,64,128]{2,1,0:T(8,128)(2,1)S(1)}, u32[]{:S(2)}, u32[]{:S(2)}) async-start(bf16[16,64,128]{2,1,0:T(8,128)(2,1)} %broadcast_in_dim.9), calls=%async_computation.1 | async-start | bytes 524288 | tf_op jit(solution)/shard_map/all_to_all | solution.py:375
  45.8 3.6 %collective-permute-start.3 = (f32[3,1024]{1,0:T(4,128)S(1)}, f32[3,1024]{1,0:T(4,128)S(1)}, u32[]{:S(2)}, u32[]{:S(2)}) collective-permute-start(f32[3,1024]{1,0:T(4,128)S(1)} %shard_map.121), channel_id=1, source_target_pairs={{0,128},{1,129},{2,130},{3,131},{4,132},{5,133},{6,134},{7,135},{8... | collective-permute-start | bytes 36872 | tf_op jit(solution)/shard_map/ppermute | solution.py:423
  67.4 13.5 %copy-start.4 = (bf16[256,2,128]{2,1,0:T(2,128)(2,1)S(1)}, bf16[256,2,128]{2,1,0:T(2,128)(2,1)}, u32[]{:S(2)}) copy-start(bf16[256,2,128]{2,1,0:T(2,128)(2,1)} %w_out.1) | copy-start | bytes 393220
  81.0 15.8 %copy-start = (bf16[1024,256]{1,0:T(8,128)(2,1)S(1)}, bf16[1024,256]{1,0:T(8,128)(2,1)}, u32[]{:S(2)}) copy-start(bf16[1024,256]{1,0:T(8,128)(2,1)} %w_hidden.3) | copy-start | bytes 1572868
  97.6 13.1 %all-to-all-start.5 = ((bf16[32,8,128]{2,1,0:T(8,128)(2,1)}), bf16[32,8,128]{2,1,0:T(8,128)(2,1)S(1)}, u32[]{:S(2)}, u32[]{:S(2)}) async-start(bf16[32,8,128]{2,1,0:T(8,128)(2,1)} %get-tuple-element.24), calls=%async_computation.5 | async-start | bytes 131072 | tf_op jit(solution)/shard_map/all_to_all | solution.py:375
  103.6 21.2 %collective-permute-start.4 = (f32[2,1024]{1,0:T(2,128)S(1)}, f32[2,1024]{1,0:T(2,128)S(1)}, u32[]{:S(2)}, u32[]{:S(2)}) collective-permute-start(f32[2,1024]{1,0:T(2,128)S(1)} %get-tuple-element.16.stats), channel_id=1, source_target_pairs={{128,0},{129,1},{130,2},{131,3},{132,4},{133,5},{134,6},{135,7},{1... | collective-permute-start | bytes 24584 | tf_op jit(solution)/shard_map/ppermute | solution.py:426
  111.5 38.8 %all-to-all-start.6 = ((bf16[128,8,128]{2,1,0:T(8,128)(2,1)}), bf16[128,8,128]{2,1,0:T(8,128)(2,1)S(1)}, u32[]{:S(2)}, u32[]{:S(2)}) async-start(bf16[128,8,128]{2,1,0:T(8,128)(2,1)} %broadcast_in_dim.11), calls=%async_computation.6 | async-start | bytes 524288 | tf_op jit(solution)/shard_map/all_to_all | solution.py:375
  124.1 0.7 copy-start.2
  129.5 0.7 copy-start.3
  134.9 15.4 %collective-permute-start.5 = (bf16[128,1024]{1,0:T(8,128)(2,1)S(1)}, bf16[128,1024]{1,0:T(8,128)(2,1)S(1)}, u32[]{:S(2)}, u32[]{:S(2)}) collective-permute-start(bf16[128,1024]{1,0:T(8,128)(2,1)S(1)} %shard_map.126), channel_id=1, source_target_pairs={{0,128},{1,129},{2,130},{3,131},{4,132},{5,133},{6,134},{7,135},{8... | collective-permute-start | bytes 786440 | tf_op jit(solution)/shard_map/ppermute | solution.py:434
  137.8 7.7 %collective-permute-start.6 = (bf16[32,256]{1,0:T(8,128)(2,1)S(1)}, bf16[32,256]{1,0:T(8,128)(2,1)S(1)}, u32[]{:S(2)}, u32[]{:S(2)}) collective-permute-start(bf16[32,256]{1,0:T(8,128)(2,1)S(1)} %get-tuple-element.21), channel_id=1, source_target_pairs={{0,1},{1,0},{2,3},{3,2},{4,5},{5,4},{6,7},{7,6},{8,9},{9,8},{10,11... | collective-permute-start | bytes 49160 | tf_op jit(solution)/shard_map/ppermute | solution.py:389
  145.5 6.7 %collective-permute-start.9 = (bf16[64,256]{1,0:T(8,128)(2,1)S(1)}, bf16[64,256]{1,0:T(8,128)(2,1)S(1)}, u32[]{:S(2)}, u32[]{:S(2)}) collective-permute-start(bf16[64,256]{1,0:T(8,128)(2,1)S(1)} %constant_dynamic-update-slice_fusion.refs_0_), channel_id=1, source_target_pairs={{0,6},{2,0},{4,2},{6,4},{1,7},{3,1},{5,3},{7,5},{8,14},{10,8},{12,... | collective-permute-start | bytes 98312 | tf_op jit(solution)/shard_map/ppermute | solution.py:389
  148.8 5.4 %collective-permute-start.8 = (bf16[64,256]{1,0:T(8,128)(2,1)S(1)}, bf16[64,256]{1,0:T(8,128)(2,1)S(1)}, u32[]{:S(2)}, u32[]{:S(2)}) collective-permute-start(bf16[64,256]{1,0:T(8,128)(2,1)S(1)} %constant_dynamic-update-slice_fusion.refs_0_), channel_id=1, source_target_pairs={{0,4},{2,6},{4,0},{6,2},{1,5},{3,7},{5,1},{7,3},{8,12},{10,14},{12... | collective-permute-start | bytes 98312 | tf_op jit(solution)/shard_map/ppermute | solution.py:389
  149.2 5.4 %collective-permute-start.7 = (bf16[64,256]{1,0:T(8,128)(2,1)S(1)}, bf16[64,256]{1,0:T(8,128)(2,1)S(1)}, u32[]{:S(2)}, u32[]{:S(2)}) collective-permute-start(bf16[64,256]{1,0:T(8,128)(2,1)S(1)} %constant_dynamic-update-slice_fusion.refs_0_), channel_id=1, source_target_pairs={{0,2},{2,4},{4,6},{6,0},{1,3},{3,5},{5,7},{7,1},{8,10},{10,12},{12... | collective-permute-start | bytes 98312 | tf_op jit(solution)/shard_map/ppermute | solution.py:389
  150.3 6.1 %collective-permute-start.10 = (bf16[128,8,128]{2,1,0:T(8,128)(2,1)S(1)}, bf16[128,8,128]{2,1,0:T(8,128)(2,1)S(1)}, u32[]{:S(2)}, u32[]{:S(2)}) collective-permute-start(bf16[128,8,128]{2,1,0:T(8,128)(2,1)S(1)} %all-to-all-done.6.near), channel_id=1, source_target_pairs={{0,8},{8,0},{1,9},{9,1},{2,10},{10,2},{3,11},{11,3},{4,12},{12,4},... | collective-permute-start | bytes 786440 | tf_op jit(solution)/shard_map/ppermute | solution.py:389
  151.1 3.5 %copy-start.1 = (bf16[256,1024]{1,0:T(8,128)(2,1)S(1)}, bf16[256,1024]{1,0:T(8,128)(2,1)}, u32[]{:S(2)}) copy-start(bf16[256,1024]{1,0:T(8,128)(2,1)} %embed.3) | copy-start | bytes 1572868
